TPU v7x, 128 devices: a whole 4x4x4 slice. The times are simulated.
128 devices in a mesh: fsdp: 128 (over z, y, x, core).
Axes of the slice: x: 4, y: 4, z: 4, core: 2. Of those that a mesh axis runs over, the one named last changes fastest.
Arguments:
- x: bfloat16 [512, 512, 512], P('fsdp')
- lengths: int32 [512], P('fsdp')
- d_y: bfloat16 [512, 512, 512], P('fsdp')
- w_attn: bfloat16 [2, 4, 512, 512], P(None, None, 'fsdp')
- b_attn: bfloat16 [2, 4, 512], P(None, None, 'fsdp')
- ln_par: bfloat16 [2, 4, 512], P(None, None, 'fsdp')
- w_up: bfloat16 [2, 512, 2048], P(None, 'fsdp')
- b_up: bfloat16 [2, 2048], P(None, 'fsdp')
- w_down: bfloat16 [2, 2048, 512], P(None, 'fsdp')
- b_down: bfloat16 [2, 512], P(None, 'fsdp')
Outputs:
- output 1: bfloat16 [512, 512, 512], P('fsdp')
- output 2: float32 [2, 4, 512, 512], P(None, None, 'fsdp')
- output 3: float32 [2, 4, 512], P(None, None, 'fsdp')
- output 4: float32 [2, 4, 512], P(None, None, 'fsdp')
- output 5: float32 [2, 512, 2048], P(None, 'fsdp')
- output 6: float32 [2, 2048], P(None, 'fsdp')
- output 7: float32 [2, 2048, 512], P(None, 'fsdp')
- output 8: float32 [2, 512], P(None, 'fsdp')
All inputs are finite; a program needn't handle non-finite values.
Results may differ from a plain program's by a relative error of at most 0.0133484.
Values are sent between devices in bfloat16 or wider.
A program may use at most 1 GiB of HBM per device.

v0:
```python
import math
import functools
import jax
import jax.numpy as jnp
from jax import lax
from jax.experimental import pallas as pl
from jax.experimental.pallas import tpu as pltpu
from jax.sharding import PartitionSpec as P

ZERO, ONE, TWO, THREE, FOUR = range(5)
EIGHT, SIXTEEN, WIDTH = 8, 16, 256

F32, BF16 = jnp.float32, jnp.bfloat16
SEQS, TOK, DIM, FFN, HEADS, HEAD, LANES = FOUR, 512, 512, 2048, EIGHT, 64, 128
HALF = HEAD // TWO
EPS = 1e-5
THETA = 10000.0
NEG_BIG = -1e30
B_ATTN, LN_PAR, B_UP, B_DOWN = ZERO, FOUR, EIGHT, 12


def nn(a, b):
    return lax.dot_general(a, b, (((ONE,), (ZERO,)), ((), ())), preferred_element_type=F32)


def nt(a, b):
    return lax.dot_general(a, b, (((ONE,), (ONE,)), ((), ())), preferred_element_type=F32)


def tn(a, b):
    return lax.dot_general(a, b, (((ZERO,), (ZERO,)), ((), ())), preferred_element_type=F32)


def lane_tiles(width=TOK, size=LANES):
    return [slice(i, i + size) for i in range(ZERO, width, size)]


def column(c_ref, lane, width=LANES):
    return jnp.broadcast_to(c_ref[:, lane:lane + ONE], (c_ref.shape[ZERO], width))


def total(value):
    return jnp.sum(value, axis=ZERO, keepdims=True)


def normed(x):
    centred = x - total(x) * (1.0 / DIM)
    rstd = lax.rsqrt(total(centred * centred) * (1.0 / DIM) + EPS)
    return centred * rstd, rstd


def norm_to(x_ref, c_ref, lane, h_ref):
    gain, shift = column(c_ref, lane), column(c_ref, lane + ONE)
    for cols in lane_tiles():
        h_ref[:, cols] = (normed(x_ref[:, cols].astype(F32))[ZERO] * gain + shift).astype(BF16)


def fold(value):
    parts = [value[:, cols] for cols in lane_tiles(value.shape[ONE])]
    return functools.reduce(jnp.add, parts)


def seq_spec(shape):
    return pl.BlockSpec((ONE, *shape), lambda s: (s,) + (ZERO,) * len(shape))


def once(shape):
    return pl.BlockSpec(shape, lambda s: (ZERO,) * len(shape), pipeline_mode=pl.Buffered(ONE))


def act_shape(rows, dtype):
    return jax.ShapeDtypeStruct((SEQS, rows, TOK), dtype)


PARAMS = pltpu.CompilerParams(vmem_limit_bytes=60 << 20, dimension_semantics=("arbitrary",))
SQUARE, TALL, WIDE, COLS = (DIM, TOK), (FFN, TOK), (DIM, FFN), (DIM, LANES)


def rotary_tables():
    inv_freq = 1.0 / (THETA ** (jnp.arange(HALF, dtype=F32) * (2.0 / HEAD)))
    angles = inv_freq[:, None] * jnp.arange(TOK, dtype=F32)[None, :]
    return jnp.cos(angles), jnp.sin(angles)


MESH = pl.DeviceIdType.MESH
AXIS = "fsdp"
ORDERS = ((TWO, ONE, ZERO), (ONE, ZERO, TWO), (ZERO, TWO, ONE))


class Place:
    def __init__(self):
        me = lax.axis_index(AXIS)
        self.me = me
        self.core = lax.rem(me, TWO)
        self.pos = (me // 32, lax.rem(me // EIGHT, FOUR), lax.rem(me // TWO, FOUR))
        self.partner = me + ONE - TWO * self.core

    def coord(self, dim, delta):
        return lax.rem(self.pos[dim] + (delta + FOUR), FOUR)

    def device(self, dim, delta):
        pos = list(self.pos)
        pos[dim] = self.coord(dim, delta)
        return pos[ZERO] * 32 + pos[ONE] * EIGHT + pos[TWO] * TWO + self.core

    def greet(self, reach=(ONE, -ONE)):
        self.greeted = THREE * len(reach) + ONE
        barrier = pltpu.get_barrier_semaphore()
        for dim in range(THREE):
            for delta in reach:
                pl.semaphore_signal(barrier, inc=ONE, device_id=(self.device(dim, delta),), device_id_type=MESH)
        pl.semaphore_signal(barrier, inc=ONE, device_id=(self.partner,), device_id_type=MESH)

    def met(self):
        pl.semaphore_wait(pltpu.get_barrier_semaphore(), self.greeted)


def remote(src, dst, send_sem, recv_sem, device):
    return pltpu.make_async_remote_copy(src_ref=src, dst_ref=dst, send_sem=send_sem, recv_sem=recv_sem,
                                        device_id=(device,), device_id_type=MESH)


class Gather:
    def __init__(self, place, buf, order, send, recv):
        self.place, self.buf, self.order, self.send, self.recv = place, buf, order, send, recv
        self.units = buf.shape[FOUR]

    def where(self, stage, at, half=None):
        dim = self.order[stage]
        index = list(self.place.pos)
        index[dim] = at
        for done in self.order[:stage]:
            index[done] = slice(ZERO, FOUR)
        unit = slice(ZERO, self.units)
        if half is not None:
            if stage > ZERO:
                index[self.order[ZERO]] = pl.ds(TWO * half, TWO)
            else:
                cut = (self.units + ONE) // TWO
                unit = slice(ZERO, cut) if half == ZERO else slice(cut, self.units)
        index = [pl.ds(i, ONE) if not isinstance(i, (slice, pl.Slice)) else i for i in index]
        return self.buf.at[index[ZERO], index[ONE], index[TWO], pl.ds(self.place.core, ONE), unit]

    def copies(self, stage, step, way):
        place, dim = self.place, self.order[stage]
        delta = ONE if way == ZERO else -ONE
        key = (stage * TWO + step) * TWO + way
        if step == ZERO:
            mine = self.where(stage, place.pos[dim])
            came = self.where(stage, place.coord(dim, -delta))
        else:
            if stage == ZERO and self.units == ONE and way == ONE:
                return None, None
            mine = self.where(stage, place.coord(dim, -delta), way)
            came = self.where(stage, place.coord(dim, -TWO * delta), way)
        def build(ref):
            return remote(ref, ref, self.send.at[key], self.recv.at[key], place.device(dim, delta))

        return lambda: build(mine), lambda: build(came)

    def step_a(self, stage):
        for way in (ZERO, ONE):
            self.copies(stage, ZERO, way)[ZERO]().start()

    def step_b(self, stage):
        for way in (ZERO, ONE):
            self.copies(stage, ZERO, way)[ONE]().wait_recv()
            out = self.copies(stage, ONE, way)[ZERO]
            if out is not None:
                out().start()

    def step_c(self, stage):
        for way in (ZERO, ONE):
            inc = self.copies(stage, ONE, way)[ONE]
            if inc is not None:
                inc().wait_recv()

    def share(self):
        half = self.buf.at[:, :, :, pl.ds(self.place.core, ONE)]
        return remote(half, half, self.send.at[12], self.recv.at[12], self.place.partner)

    def shared(self):
        half = self.buf.at[:, :, :, pl.ds(ONE - self.place.core, ONE)]
        remote(half, half, self.send.at[12], self.recv.at[12], self.place.partner).wait_recv()

    def drain(self):
        for stage in range(THREE):
            for step in range(TWO):
                for way in (ZERO, ONE):
                    out = self.copies(stage, step, way)[ZERO]
                    if out is not None:
                        out().wait_send()
        self.share().wait_send()


def gather_all(gathers):
    for stage in range(THREE):
        for g in gathers:
            g.step_a(stage)
        for g in gathers:
            g.step_b(stage)
        for g in gathers:
            g.step_c(stage)
    for g in gathers:
        g.share().start()
    for g in gathers:
        g.shared()
    for g in gathers:
        g.drain()


class Scatter:
    def __init__(self, place, grads, acc, got_a, got_b, order, send, recv):
        self.place, self.grads, self.acc, self.order = place, grads, acc, order
        self.got_a, self.got_b, self.send, self.recv = got_a, got_b, send, recv
        self.units = acc.shape[ZERO]

    def columns(self, core):
        return pl.ds(pl.multiple_of(core * WIDTH, WIDTH), WIDTH)

    def swap(self):
        place = self.place
        for u in range(self.units):
            remote(self.grads(u).at[:, :, :, :, self.columns(ONE - place.core)], self.acc.at[u],
                   self.send.at[20 + u], self.recv.at[20 + u], place.partner).start()

    def swapped(self):
        place = self.place
        for u in range(self.units):
            copy = remote(self.grads(u).at[:, :, :, :, self.columns(ONE - place.core)], self.acc.at[u],
                          self.send.at[20 + u], self.recv.at[20 + u], place.partner)
            copy.wait_recv()
            grad, acc = self.grads(u), self.acc

            @pl.loop(ZERO, SIXTEEN)
            def _(i):
                z, y = i // FOUR, lax.rem(i, FOUR)
                acc[u, z, y] = acc[u, z, y] + grad[z, y, :, :, self.columns(place.core)]

    def index(self, stage, at):
        index = [slice(ZERO, FOUR)] * THREE
        for done in self.order[:stage]:
            index[done] = pl.ds(self.place.pos[done], ONE)
        index[self.order[stage]] = pl.ds(at, ONE)
        return index

    def part(self, stage, at, half=None):
        columns = slice(ZERO, WIDTH) if half is None else slice(128 * half, 128 * half + 128)
        return self.acc.at[(slice(ZERO, self.units), *self.index(stage, at), slice(ZERO, EIGHT), columns)]

    def copy(self, stage, step, way):
        place, dim = self.place, self.order[stage]
        delta = ONE if way == ZERO else -ONE
        key = (stage * TWO + step) * TWO + way
        if step == ZERO:
            src, ref, half = self.part(stage, place.coord(dim, TWO), way), self.got_a, way
        else:
            src, ref, half = self.part(stage, place.coord(dim, delta)), self.got_b, None
        return src, ref, half, key, place.device(dim, delta)

    def start(self, stage, step, way):
        src, ref, half, key, device = self.copy(stage, step, way)
        remote(src, self.cast(ref, stage, way, half, src), self.send.at[key], self.recv.at[key], device).start()

    def wait(self, stage, step, way):
        src, ref, half, key, device = self.copy(stage, step, way)
        remote(src, self.cast(ref, stage, way, half, src), self.send.at[key], self.recv.at[key], device).wait_recv()

    def cast(self, ref, stage, way, half, src):
        columns = slice(ZERO, WIDTH) if half is None else slice(128 * half, 128 * half + 128)
        return ref[stage].at[(ZERO if half is not None else way, slice(ZERO, self.units), *([slice(None)] * THREE), slice(ZERO, EIGHT), columns)]

    def add(self, stage, at, refs, half):
        units = self.units
        shape = self.got_b[stage].shape[TWO:5]
        total = units * shape[ZERO] * shape[ONE] * shape[TWO]
        columns = slice(ZERO, WIDTH) if half is None else slice(128 * half, 128 * half + 128)
        base = [ZERO, ZERO, ZERO]
        for done in self.order[:stage]:
            base[done] = self.place.pos[done]
        base[self.order[stage]] = at
        acc = self.acc
        bunch = FOUR if total % FOUR == ZERO else ONE

        @pl.loop(ZERO, total // bunch)
        def _(k):
            for j in range(bunch):
                i = k * bunch + j
                u = i // (shape[ZERO] * shape[ONE] * shape[TWO])
                a = lax.rem(i // (shape[ONE] * shape[TWO]), shape[ZERO])
                b = lax.rem(i // shape[TWO], shape[ONE])
                c = lax.rem(i, shape[TWO])
                here = (u, base[ZERO] + a, base[ONE] + b, base[TWO] + c, slice(ZERO, EIGHT), columns)
                value = acc[here]
                for ref, way in refs:
                    value = value + ref[stage][ZERO if half is not None else way, u, a, b, c, :, columns]
                acc[here] = value

    def step_a(self, stage):
        for way in (ZERO, ONE):
            self.start(stage, ZERO, way)

    def step_b(self, stage):
        dim = self.order[stage]
        for way in (ZERO, ONE):
            delta = ONE if way == ZERO else -ONE
            self.wait(stage, ZERO, way)
            self.add(stage, self.place.coord(dim, delta), [(self.got_a, way)], way)
            self.start(stage, ONE, way)

    def step_c(self, stage):
        dim = self.order[stage]
        for way in (ZERO, ONE):
            self.wait(stage, ONE, way)
        self.add(stage, self.place.pos[dim], [(self.got_b, ZERO), (self.got_b, ONE)], None)

    def last(self, own, other):
        place = self.place
        z, y, x = place.pos
        src = self.acc.at[:, z, y, x]
        return remote(src, other, self.send.at[12], self.recv.at[12], place.partner)

    def drain(self, other):
        for stage in range(THREE):
            for step in range(TWO):
                for way in (ZERO, ONE):
                    src, ref, half, key, device = self.copy(stage, step, way)
                    remote(src, self.cast(ref, stage, way, half, src), self.send.at[key], self.recv.at[key], device).wait_send()
        for u in range(self.units):
            remote(self.grads(u).at[:, :, :, :, self.columns(ONE - self.place.core)], self.acc.at[u],
                   self.send.at[20 + u], self.recv.at[20 + u], self.place.partner).wait_send()
        self.last(None, other).wait_send()

    def result(self, unit, other):
        z, y, x = self.place.pos
        own, came = self.acc[unit, z, y, x], other[unit]
        first = self.place.core == ZERO
        return jnp.concatenate([jnp.where(first, own, came), jnp.where(first, came, own)], axis=ONE)


def landing_shapes(order, units, ways):
    shapes = []
    for stage in range(THREE):
        size = [FOUR, FOUR, FOUR]
        for done in order[:stage + ONE]:
            size[done] = ONE
        shapes.append((ways, units, *size, EIGHT, WIDTH))
    return shapes


class Small:
    def __init__(self, place, value, slots, send, recv):
        self.place, self.value, self.slots, self.send, self.recv = place, value, slots, send, recv

    def copies(self, stage):
        if stage == THREE:
            return [remote(self.value, self.slots.at[9], self.send.at[9], self.recv.at[9], self.place.partner)]
        return [remote(self.value, self.slots.at[stage * THREE + k], self.send.at[stage * THREE + k], self.recv.at[stage * THREE + k],
                       self.place.device(stage, delta)) for k, delta in enumerate((ONE, -ONE, TWO))]

    def start(self, stage):
        for copy in self.copies(stage):
            copy.start()

    def finish(self, stage):
        copies = self.copies(stage)
        for copy in copies:
            copy.wait()
        value = self.value[...]
        for k in range(len(copies)):
            value = value + self.slots[stage * THREE + k]
        self.value[...] = value

    def steps(self):
        def turn(stage):
            def step():
                self.finish(stage)
                self.start(stage + ONE)
            return step

        return [lambda: self.start(ZERO), turn(ZERO), turn(ONE), turn(TWO), lambda: self.finish(THREE)]


VMEM = pl.BlockSpec(memory_space=pltpu.VMEM)
HBM = pl.BlockSpec(memory_space=pl.ANY)
DMA = pltpu.SemaphoreType.DMA


COLOURS = ((THREE, FOUR, 5), (6, 7, EIGHT), (9, 10, 11))
SLOTS = EIGHT


def at_slot(slot, plan):
    for when, step in plan:
        pl.when(slot == when)(step)


def gather_plan(gathers, after, slots):
    def each(name, *args):
        def step():
            for g in gathers:
                getattr(g, name)(*args)
        return step

    def turn(stage):
        def step():
            each("step_c", stage)()
            each("step_a", stage + ONE)()
        return step

    def swap():
        each("step_c", TWO)()
        for g in gathers:
            g.share().start()

    def end():
        each("shared")()
        each("drain")()
        after()

    steps = [each("step_a", ZERO), each("step_b", ZERO), turn(ZERO), each("step_b", ONE), turn(ONE), each("step_b", TWO), swap, end]
    return list(zip(slots, steps))


def spread(buf, u, out_ref, column_base):
    @pl.loop(ZERO, EIGHT)
    def _(block):
        for part in range(FOUR):
            g = block * FOUR + part
            tiles = [buf[block // TWO, lax.rem(block, TWO) * TWO + part // TWO, part % TWO * TWO + k // TWO, k % TWO, u].astype(F32) for k in range(FOUR)]
            rows = pl.ds(pl.multiple_of(g * SIXTEEN, SIXTEEN), SIXTEEN)
            for j, cols in enumerate(lane_tiles()):
                value = jnp.concatenate([t[FOUR * j:FOUR * j + FOUR] for t in tiles], axis=ZERO).astype(BF16)
                out_ref[rows, column_base + cols.start:column_base + cols.stop] = value


def spread_down(buf, u, out_ref, cols):
    @pl.loop(ZERO, SIXTEEN)
    def _(i):
        for k in range(EIGHT):
            d = i * EIGHT + k
            out_ref[pl.ds(pl.multiple_of(d * SIXTEEN, SIXTEEN), SIXTEEN), cols] = buf[i // FOUR, lax.rem(i, FOUR), k // TWO, k % TWO, u]


def same(shape, test):
    row = lax.broadcasted_iota(jnp.int32, shape, ZERO)
    col = lax.broadcasted_iota(jnp.int32, shape, ONE)
    return jnp.where(test(row, col), 1.0, 0.0)


def small_columns(small_ref, c_ref):
    rows = [small_ref[z, y, x, c, ZERO] for z in range(FOUR) for y in range(FOUR) for x in range(FOUR) for c in range(TWO)]
    table = jnp.concatenate(rows, axis=ZERO).astype(BF16)
    quads = nn(same((DIM, LANES), lambda r, c: r // FOUR == c).astype(BF16), table)
    quads = (quads * same((DIM, LANES), lambda r, c: r % FOUR == c % FOUR)).astype(BF16)
    mask = same((DIM, LANES), lambda r, c: r % SIXTEEN == c % SIXTEEN)
    pick = same((DIM, 32), lambda r, c: r // SIXTEEN == c).astype(BF16)
    ups = [(nn(pick, table[32 * k:32 * k + 32]) * mask).astype(BF16) for k in range(FOUR)]
    for layer in range(TWO):
        def is_up(r):
            return (r // SIXTEEN == layer * FOUR + TWO)

        value = nn(quads, same((LANES, LANES), lambda r, c: (r // 64 == layer) & (r % 64 // FOUR == c) & ~is_up(r)).astype(BF16))
        for k in range(FOUR):
            value = value + nn(ups[k], same((LANES, LANES), lambda r, c: is_up(r) & (c == B_UP + k)).astype(BF16))
        c_ref[layer] = value


def forward_kernel(len_ref, x_ref, cos_ref, sin_ref, pack_qkv, pack_mo, small_ref,
                   xs_out, q_ref, k_ref, v_ref, p_hbm, ctx_ref, mid_ref, act_ref, slope_ref, c_ref,
                   nat_qkv, nat_wo, nat_up, nat_down,
                   xs, ctxb, wqkv, wo, up, down, n_qkv, n_wo, n_up, n_down, p_buf, h_ref, acc_ref,
                   sbuf, q0, q1, q2, r0, r1, r2, m0, m1, m2, n0, n1, n2, send, recv, local, p_sem, nat_sem):
    step = pl.program_id(ZERO)
    phase, seq, layer = step // FOUR, lax.rem(step, FOUR), step // EIGHT
    place = Place()
    z, y, x = place.pos
    bufs = ((q0, q1, q2), (m0, m1, m2), (r0, r1, r2), (n0, n1, n2))
    groups = [[Gather(place, b, ORDERS[k], send.at[i * THREE + k], recv.at[i * THREE + k]) for k, b in enumerate(group)] for i, group in enumerate(bufs)]
    little = Gather(place, sbuf, ORDERS[ZERO], send.at[12], recv.at[12])

    def own_copies():
        copies = [pltpu.make_async_copy(small_ref, sbuf.at[z, y, x, place.core], local.at[12])]
        for i, group in enumerate(bufs):
            source = (pack_qkv, pack_mo)[i % TWO]
            copies += [pltpu.make_async_copy(source.at[i // TWO, k], b.at[z, y, x, place.core], local.at[i * THREE + k]) for k, b in enumerate(group)]
        return copies

    def nat_copies(which, l):
        if which == ZERO:
            return [pltpu.make_async_copy(n_qkv, nat_qkv.at[l], nat_sem.at[ZERO])]
        return [pltpu.make_async_copy(src, dst.at[l], nat_sem.at[ONE + i]) for i, (src, dst) in enumerate(((n_wo, nat_wo), (n_up, nat_up), (n_down, nat_down)))]

    def take_qkv(l):
        if l:
            for copy in nat_copies(ZERO, ZERO):
                copy.wait()
        for m in range(THREE):
            spread(bufs[TWO * l][m], ZERO, n_qkv.at[m], ZERO)
            wqkv[m] = n_qkv[m].T
        for copy in nat_copies(ZERO, l):
            copy.start()

    def take_mo(l):
        if l:
            for copy in nat_copies(ONE, ZERO):
                copy.wait()
        for colour in range(THREE):
            for u, unit in enumerate(COLOURS[colour]):
                buf = bufs[TWO * l + ONE][colour]
                if unit == THREE:
                    spread(buf, u, n_wo, ZERO)
                    wo[...] = n_wo[...].T
                elif unit < EIGHT:
                    part = slice(DIM * (unit - FOUR), DIM * (unit - THREE))
                    spread(buf, u, n_up, part.start)
                    up[part, :] = n_up[:, part].T
                else:
                    spread_down(buf, u, n_down, lane_tiles()[unit - EIGHT])
        for k in range(FOUR):
            part = slice(DIM * k, DIM * k + DIM)
            down[:, part] = n_down[part, :].T
        for copy in nat_copies(ONE, l):
            copy.start()

    @pl.when(step == ZERO)
    def _():
        place.greet()
        for copy in own_copies():
            copy.start()
        for copy in own_copies():
            copy.wait()
        place.met()
        gather_all(groups[ZERO] + [little])
        small_columns(sbuf, c_ref)
        take_qkv(ZERO)

    attn_plan = gather_plan(groups[ONE], lambda: None, (ZERO, TWO, 5, EIGHT, 11, SIXTEEN, 24, 31)) + gather_plan(groups[THREE], lambda: None, (64, 66, 69, 72, 75, 80, 88, 95))
    mlp_plan = gather_plan(groups[TWO], lambda: None, (32, 34, 36, 40, 44, 48, 52, 60))

    @pl.when(phase % TWO == ZERO)
    def _():
        @pl.when(step < FOUR)
        def _():
            xs[seq] = x_ref[ZERO].T
            xs_out[ZERO, ZERO] = xs[seq]

        @pl.when(step == EIGHT)
        def _():
            take_qkv(ONE)

        attn_forward(len_ref[seq], layer, seq, step, xs.at[seq], wqkv, c_ref.at[layer], cos_ref, sin_ref, q_ref.at[ZERO, ZERO], k_ref.at[ZERO, ZERO],
                     v_ref.at[ZERO, ZERO], p_hbm, p_buf, p_sem, ctx_ref.at[ZERO, ZERO], ctxb.at[seq], h_ref, acc_ref, attn_plan)

    @pl.when(phase % TWO == ONE)
    def _():
        for l in range(TWO):
            pl.when(step == EIGHT * l + FOUR)(functools.partial(take_mo, l))
        mlp_forward(layer, step, ctxb.at[seq], xs.at[seq], wo, up, down, c_ref.at[layer], mid_ref.at[ZERO, ZERO], act_ref.at[ZERO, ZERO], slope_ref.at[ZERO, ZERO],
                    h_ref, mlp_plan)

        @pl.when(layer == ZERO)
        def _():
            xs_out[ZERO, ZERO] = xs[seq]

    @pl.when(step == 15)
    def _():
        for which in range(TWO):
            for copy in nat_copies(which, ONE):
                copy.wait()


def attn_forward(length, layer, seq, step, xt, w, c_ref, cos_ref, sin_ref, q_ref, k_ref, v_ref, p_hbm, p_buf, p_sem, ctx_ref, ctxb, h_ref, acc_ref, plan):
    norm_to(xt, c_ref, LN_PAR, h_ref)
    for m, out in enumerate((q_ref, k_ref, v_ref)):
        acc_ref[...] = nn(w[m], h_ref[...])
        bias = column(c_ref, B_ATTN + m)
        if m < TWO:
            scale = HEAD ** -0.5 if m == ZERO else 1.0
            for cols in lane_tiles():
                for head in range(HEADS):
                    one, two = slice(HEAD * head, HEAD * head + HALF), slice(HEAD * head + HALF, HEAD * head + HEAD)
                    a = (acc_ref[one, cols] + bias[one]) * scale
                    b = (acc_ref[two, cols] + bias[two]) * scale
                    cos, sin = cos_ref[:, cols], sin_ref[:, cols]
                    out[one, cols] = (a * cos - b * sin).astype(BF16)
                    out[two, cols] = (b * cos + a * sin).astype(BF16)
        else:
            for cols in lane_tiles():
                out[:, cols] = (acc_ref[:, cols] + bias).astype(BF16)

    key = lax.broadcasted_iota(jnp.int32, (SIXTEEN, TOK), ONE)
    row = lax.broadcasted_iota(jnp.int32, (SIXTEEN, TOK), ZERO)
    bias_rows = jnp.where((row == ZERO) & (key >= length), NEG_BIG, 0.0).astype(BF16)
    one_rows = jnp.where(row == ZERO, 1.0, 0.0).astype(BF16)

    @pl.loop(ZERO, HEADS)
    def _(head):
        at_slot(step * SLOTS + head, plan)
        rows = pl.ds(pl.multiple_of(head * HEAD, HEAD), HEAD)
        slot = lax.rem(head, TWO)
        copy = pltpu.make_async_copy(p_buf.at[slot], p_hbm.at[layer, seq, head], p_sem.at[slot])

        @pl.when((step > ZERO) | (head > ONE))
        def _():
            copy.wait()

        keys = jnp.concatenate([k_ref[rows, :], bias_rows], axis=ZERO)
        for cols in lane_tiles(TOK, WIDTH):
            queries = jnp.concatenate([q_ref[rows, cols], one_rows[:, cols]], axis=ZERO)
            scores = tn(keys, queries)
            weight = jnp.exp(scores - jnp.max(scores, axis=ZERO, keepdims=True))
            probs = (weight * (1.0 / total(weight))).astype(BF16)
            p_buf[slot, :, cols] = probs
            ctx = nn(v_ref[rows, :], probs)
            ctx_ref[rows, cols] = ctx
            ctxb[rows, cols] = ctx.astype(BF16)
        copy.start()

    @pl.when(step == 11)
    def _():
        for slot in range(TWO):
            pltpu.make_async_copy(p_buf.at[slot], p_hbm.at[layer, seq, slot], p_sem.at[slot]).wait()


def mlp_forward(layer, step, ctxb, xt, wo, up, down, c_ref, mid_ref, act_ref, slope_ref, h_ref, plan):
    attn = nn(wo[...], ctxb[...])
    for cols in lane_tiles():
        mid_ref[:, cols] = (xt[:, cols].astype(F32) + attn[:, cols] + column(c_ref, B_ATTN + THREE)).astype(BF16)
    norm_to(mid_ref, c_ref, LN_PAR + TWO, h_ref)
    for part in range(FFN // DIM):
        at_slot(step * SLOTS + TWO * part, plan)
        rows = slice(DIM * part, DIM * part + DIM)
        pre = nn(up[rows, :], h_ref[...])
        for cols in lane_tiles():
            value = pre[:, cols] + column(c_ref, B_UP + part)
            cdf = 0.5 * (1.0 + lax.erf(value * (1.0 / math.sqrt(2.0))))
            density = jnp.exp(-0.5 * value * value) * (1.0 / math.sqrt(2.0 * math.pi))
            act_ref[rows, cols] = (value * cdf).astype(BF16)
            slope_ref[rows, cols] = cdf + value * density

    @pl.when(layer == ZERO)
    def _():
        out = nn(down[...], act_ref[...])
        for cols in lane_tiles():
            xt[:, cols] = (mid_ref[:, cols].astype(F32) + out[:, cols] + column(c_ref, B_DOWN)).astype(BF16)


def forward(lengths, x, tables, pack_qkv, pack_mo, small):
    def saved(index, rows, dtype):
        return jax.ShapeDtypeStruct((TWO, SEQS, rows, TOK), dtype), pl.BlockSpec((ONE, ONE, rows, TOK), index)

    def attn_at(s):
        return s // EIGHT, jnp.where(s // FOUR % TWO == ZERO, s % FOUR, THREE), ZERO, ZERO

    def mlp_at(s):
        odd = s // FOUR % TWO == ONE
        return jnp.where(s < 12, ZERO, ONE), jnp.where(odd, s % FOUR, jnp.where(s < FOUR, ZERO, THREE)), ZERO, ZERO

    def xs_at(s):
        return jnp.where(s < FOUR, ZERO, ONE), jnp.where(s < EIGHT, s % FOUR, THREE), ZERO, ZERO

    outs = [saved(xs_at, DIM, BF16)] + [saved(attn_at, DIM, BF16)] * THREE
    outs += [(jax.ShapeDtypeStruct((TWO, SEQS, HEADS, TOK, TOK), BF16), HBM), saved(attn_at, DIM, F32)]
    outs += [saved(mlp_at, DIM, BF16), saved(mlp_at, FFN, BF16), saved(mlp_at, FFN, F32)]
    outs += [(jax.ShapeDtypeStruct((TWO, *COLS), F32), pl.BlockSpec((TWO, *COLS), lambda s: (ZERO, ZERO, ZERO), pipeline_mode=pl.Buffered(ONE)))]
    weights = ((THREE, DIM, DIM), (DIM, DIM), (DIM, FFN), (FFN, DIM))
    outs += [(jax.ShapeDtypeStruct((TWO, *w), BF16), HBM) for w in weights]
    grid = (FOUR, FOUR, FOUR, TWO)
    scratch = [(SEQS, *SQUARE), (SEQS, *SQUARE), weights[ZERO], weights[ONE], weights[THREE], weights[TWO], *weights, (TWO, TOK, TOK), SQUARE]
    scratch = [pltpu.VMEM(s, BF16) for s in scratch] + [pltpu.VMEM(SQUARE, F32), pltpu.VMEM((*grid, ONE, ONE, LANES), F32)]
    scratch += [pltpu.VMEM((*grid, n, SIXTEEN, LANES), BF16) for n in (ONE, ONE, ONE, ONE, ONE, ONE, THREE, THREE, THREE, THREE, THREE, THREE)]
    scratch += [DMA((13, 13)), DMA((13, 13)), DMA((13,)), DMA((TWO,)), DMA((FOUR,))]
    return pl.pallas_call(
        forward_kernel, grid=(SIXTEEN,),
        out_shape=[o[ZERO] for o in outs], out_specs=[o[ONE] for o in outs],
        in_specs=[pl.BlockSpec(memory_space=pltpu.SMEM), pl.BlockSpec((ONE, *SQUARE), lambda s: (jnp.minimum(s, THREE), ZERO, ZERO)),
                  once((HALF, TOK)), once((HALF, TOK)), HBM, HBM, HBM],
        scratch_shapes=scratch,
        compiler_params=pltpu.CompilerParams(collective_id=ZERO, has_side_effects=True, vmem_limit_bytes=63 << 20,
                                             dimension_semantics=("arbitrary",)),
        name="forward")(lengths, x, *tables, pack_qkv, pack_mo, small)


def norm_back(dh, x, gain):
    xhat, rstd = normed(x)
    dxhat = dh * gain
    mean_one = total(dxhat) * (1.0 / DIM)
    mean_two = total(dxhat * xhat) * (1.0 / DIM)
    return rstd * (dxhat - mean_one - xhat * mean_two), xhat


def columns_of(pairs):
    lane = lax.broadcasted_iota(jnp.int32, COLS, ONE)
    value = jnp.zeros(COLS, F32)
    for at, partial in pairs:
        value = jnp.where(lane == at, jnp.sum(partial, axis=ONE, keepdims=True), value)
    return value


def head_rows(head):
    return slice(HEAD * head, HEAD * head + HEAD), slice(HEAD * head, HEAD * head + HALF), slice(HEAD * head + HALF, HEAD * head + HEAD)


GRID = (FOUR, FOUR, FOUR)


class Reduce:
    def __init__(self, place, units, grads, accs, got_a, got_b, others, send, recv):
        self.scatters = [Scatter(place, (lambda u, k=k: grads(units[k][u])), accs[k], got_a[k], got_b[k], ORDERS[k], send.at[k], recv.at[k])
                         for k in range(THREE)]
        self.others, self.units, self.place = others, units, place

    def each(self, name, *args):
        for s in self.scatters:
            getattr(s, name)(*args)

    def first(self):
        for s in self.scatters:
            s.swapped()
            s.step_a(ZERO)

    def turn(self, stage):
        for s in self.scatters:
            s.step_c(stage)
            s.step_a(stage + ONE)

    def last(self):
        for s, other in zip(self.scatters, self.others):
            s.step_c(TWO)
            s.last(None, other).start()

    def finish(self, store):
        for k, (s, other) in enumerate(zip(self.scatters, self.others)):
            s.last(None, other).wait_recv()
            for u, unit in enumerate(self.units[k]):
                store(unit, s.result(u, other))
            s.drain(other)

    def plan(self, slots, store):
        steps = [lambda: self.each("swap"), self.first, lambda: self.each("step_b", ZERO), lambda: self.turn(ZERO), lambda: self.each("step_b", ONE),
                 lambda: self.turn(ONE), lambda: self.each("step_b", TWO), self.last, lambda: self.finish(store)]
        return list(zip(slots, steps))


def backward_kernel(dy_ref, mid_ref, ctx_ref, q_ref, k_ref, v_ref, x_ref, cos_ref, sin_ref, c_ref, p_hbm, slope_hbm, act_hbm,
                    qkv_hbm, wo_hbm, up_hbm, down_hbm,
                    dx_ref, attn_out, up_out, down_out, small_out, *refs):
    (grad, dctx, delta, big, wqkv, wo, slope, act, dpre, h_ref, s_a, s_b, d_a, d_b, sums,
     g_qkv, g_wo, g_up, g_down, rows_ref, slots_ref), refs = refs[:21], refs[21:]
    accs, others, got_a, got_b, refs = refs[:6], refs[6:12], refs[12:30], refs[30:48], refs[48:]
    send, recv, ssend, srecv, big_sem, w_sem, mlp_sem = refs
    step = pl.program_id(ZERO)
    phase, seq = step // FOUR, lax.rem(step, FOUR)
    layer = ONE - step // EIGHT
    place = Place()

    def grads(unit):
        if unit < THREE:
            return g_qkv.at[unit]
        if unit == THREE:
            return g_wo
        if unit < EIGHT:
            return g_up.at[unit - FOUR]
        return g_down.at[:, :, :, unit - EIGHT]

    def got(refs, i):
        return [refs[9 * i + THREE * k:9 * i + THREE * k + THREE] for k in range(THREE)]

    qkv_sums = Reduce(place, ((ZERO,), (ONE,), (TWO,)), grads, accs[:THREE], got(got_a, ZERO), got(got_b, ZERO), others[:THREE], send.at[ZERO], recv.at[ZERO])
    mo_sums = Reduce(place, COLOURS, grads, accs[THREE:], got(got_a, ONE), got(got_b, ONE), others[THREE:], send.at[ONE], recv.at[ONE])
    tiny = Small(place, rows_ref, slots_ref, ssend, srecv)
    first_core = place.core == ZERO

    def store(l):
        def put(unit, full):
            if unit < EIGHT:
                mine = jnp.where(first_core, full[:FOUR], full[FOUR:])
                if unit < FOUR:
                    attn_out[l, unit] = mine
                else:
                    up_out[l, :, DIM * (unit - FOUR):DIM * (unit - THREE)] = mine
            else:
                at = EIGHT * (unit % TWO)

                @pl.when(place.core == (unit - EIGHT) // TWO)
                def _():
                    down_out[l, at:at + EIGHT] = full
        return put

    def mlp_weights(l):
        copies = [pltpu.make_async_copy(wo_hbm.at[l], wo, w_sem.at[ZERO])]
        for k in range(FOUR):
            part = pl.ds(DIM * k, DIM)
            copies.append(pltpu.make_async_copy(down_hbm.at[l, part], big.at[k], big_sem.at[k]))
            copies.append(pltpu.make_async_copy(up_hbm.at[l, :, part], big.at[FOUR + k], big_sem.at[FOUR + k]))
        return copies

    def attn_weights(l):
        return [pltpu.make_async_copy(qkv_hbm.at[l], wqkv, w_sem.at[ONE])]

    def probs(l, s):
        return [pltpu.make_async_copy(p_hbm.at[l, s, k], big.at[k], big_sem.at[k]) for k in range(HEADS)]

    def saved_mlp(l, s):
        return [pltpu.make_async_copy(slope_hbm.at[l, s], slope, mlp_sem.at[ZERO]), pltpu.make_async_copy(act_hbm.at[l, s], act, mlp_sem.at[ONE])]

    def start(copies):
        for copy in copies:
            copy.start()

    def wait(copies):
        for copy in copies:
            copy.wait()

    @pl.when(step == ZERO)
    def _():
        place.greet((ONE, -ONE, TWO))
        start(mlp_weights(ONE) + saved_mlp(ONE, ZERO) + attn_weights(ONE))

    pl.when(step == ONE)(place.met)
    live = step < SIXTEEN
    attn_plan = [((when, when + 32), run) for when, run in mo_sums.plan((SIXTEEN, 20, 22, 25, 26, 28, 29, 30, 31), store(layer))]
    late = range(64, 73)
    mlp_plan = list(zip(zip((32, 34, 36, 38, 40, 42, 44, 46, 47), late), [run for _, run in qkv_sums.plan(late, store(jnp.where(live, ONE, ZERO)))]))
    mlp_plan += [((when,), run) for when, run in zip((64, 66, 68, 70, 71), tiny.steps())]

    def hook(at, plan):
        for slots, run in plan:
            for when in slots:
                if when % FOUR == at:
                    others = [w for w in slots if w % FOUR == at]
                    if when == others[ZERO]:
                        pl.when(functools.reduce(jnp.logical_or, [step * FOUR + at == w for w in others]))(run)

    @pl.when(phase % TWO == ZERO)
    def _():
        @pl.when((seq == ZERO) & live)
        def _():
            for ref in (g_wo, g_up, g_down, sums):
                ref[...] = jnp.zeros_like(ref)

        @pl.when(step < FOUR)
        def _():
            grad[seq] = dy_ref[ZERO].T

        @pl.when((seq == ZERO) & live)
        def _():
            wait(mlp_weights(layer))

        hook(ZERO, mlp_plan)
        pl.when(live)(lambda: wait(saved_mlp(layer, seq)))
        mlp_backward(grad.at[seq], slope, act, mid_ref, ctx_ref, wo, big, c_ref, dctx.at[seq], delta.at[seq], g_wo, g_up, g_down,
                     dpre, h_ref, s_a, s_b, sums, pl.when(live), lambda at: hook(at, mlp_plan),
                     lambda: pl.when(seq < THREE)(lambda: start(saved_mlp(layer, seq + ONE))))

        @pl.when((seq == THREE) & live)
        def _():
            value = columns_of([(B_UP + i, sums[i]) for i in range(FOUR)] + [
                (LN_PAR + TWO, sums[FOUR]), (LN_PAR + THREE, sums[5]), (B_DOWN, sums[6]), (B_ATTN + THREE, sums[7])])
            rows_ref[pl.ds(pl.multiple_of(layer * SIXTEEN, SIXTEEN), SIXTEEN), :] = value.T[:SIXTEEN]

        hook(THREE, mlp_plan)

    @pl.when(phase % TWO == ONE)
    def _():
        @pl.when(seq == ZERO)
        def _():
            start(probs(layer, ZERO))
            wait(attn_weights(layer))
            for ref in (g_qkv, sums):
                ref[...] = jnp.zeros_like(ref)

        @pl.when(step == FOUR)
        def _():
            start(saved_mlp(ZERO, ZERO))
        hook(ZERO, attn_plan)
        wait(probs(layer, seq))
        attn_backward(dctx.at[seq], delta.at[seq], big, q_ref, k_ref, v_ref, x_ref, grad.at[seq], wqkv, c_ref, cos_ref, sin_ref,
                      g_qkv, dpre, h_ref, s_a, s_b, d_a, d_b, sums, lambda at: hook(at, attn_plan),
                      lambda: pl.when(seq < THREE)(lambda: start(probs(layer, seq + ONE))))

        @pl.when(seq == THREE)
        def _():
            value = columns_of([(B_ATTN + i, sums[i]) for i in range(THREE)] + [(LN_PAR, sums[THREE]), (LN_PAR + ONE, sums[FOUR])])
            rows = pl.ds(pl.multiple_of(layer * SIXTEEN, SIXTEEN), SIXTEEN)
            rows_ref[rows, :] = rows_ref[rows, :] + value.T[:SIXTEEN]

        @pl.when(step == 7)
        def _():
            start(mlp_weights(ZERO) + attn_weights(ZERO))

        @pl.when(step > 11)
        def _():
            dx_ref[ZERO] = grad[seq].T
        hook(THREE, attn_plan)

    @pl.when(step == 18)
    def _():
        small_out[...] = rows_ref[...]


def add_to(ref, value):
    ref[...] = ref[...] + value.reshape(ref.shape)


def mlp_backward(grad, slope, act, mid_ref, ctx_ref, wo, big, c_ref, dctx, delta, g_wo, g_up, g_down, dpre, h_ref, s_a, s_b, sums, when, hook, prefetch):
    parts = [slice(DIM * k, DIM * k + DIM) for k in range(FOUR)]
    pre = (s_a, s_b)

    def dact(k):
        pre[k % TWO][...] = nn(big[k], grad[...])

    @when
    def _():
        norm_to(mid_ref.at[ZERO], c_ref, LN_PAR + TWO, h_ref)
        dact(ZERO)
        for k, rows in enumerate(parts):
            if k < THREE:
                dact(k + ONE)
            if k:
                add_to(g_down.at[k - ONE], nt(act[parts[k - ONE], :], grad[...]))
            for cols in lane_tiles():
                value = pre[k % TWO][:, cols] * slope[rows, cols]
                sums[k] += value
                dpre[rows, cols] = value.astype(BF16)
        add_to(g_down.at[THREE], nt(act[parts[THREE], :], grad[...]))
        prefetch()
    hook(ONE)

    @when
    def _():
        s_a[...] = functools.reduce(jnp.add, [nn(big[FOUR + k], dpre[rows, :]) for k, rows in enumerate(parts)])
    hook(TWO)

    @when
    def _():
        for k, rows in enumerate(parts):
            add_to(g_up.at[k], nt(h_ref[...], dpre[rows, :]))
        gain = column(c_ref, LN_PAR + TWO)
        for cols in lane_tiles():
            dh, dy = s_a[:, cols], grad[:, cols].astype(F32)
            dx, xhat = norm_back(dh, mid_ref[ZERO, :, cols].astype(F32), gain)
            dmid = (dy + dx).astype(BF16)
            grad[:, cols] = dmid
            sums[FOUR] += dh * xhat
            sums[5] += dh
            sums[6] += dy
            sums[7] += dmid.astype(F32)
        add_to(g_wo, nt(ctx_ref[ZERO].astype(BF16), grad[...]))
        s_b[...] = nn(wo[...], grad[...])
        for head in range(HEADS):
            rows = head_rows(head)[ZERO]
            value = s_b[rows, :].astype(BF16)
            dctx[rows, :] = value
            delta[head:head + ONE, :] = total(value.astype(F32) * ctx_ref[ZERO, rows, :])


def attn_backward(dctx, delta, probs, q_ref, k_ref, v_ref, x_ref, grad, wqkv, c_ref, cos_ref, sin_ref, g_qkv, dproj, h_ref, s_a, s_b, d_a, d_b,
                  sums, hook, prefetch):
    scores, dscores = (s_a, s_b), (d_a, d_b)
    q, k, v = q_ref.at[ZERO], k_ref.at[ZERO], v_ref.at[ZERO]

    def open_head(head):
        rows = head_rows(head)[ZERO]
        scores[head % TWO][...] = tn(v[rows, :], dctx[rows, :])

    def weigh(head):
        dscores[head % TWO][...] = (probs[head].astype(F32) * (scores[head % TWO][...] - delta[head:head + ONE, :])).astype(BF16)

    def values(head):
        rows = head_rows(head)[ZERO]
        dv = nt(dctx[rows, :], probs[head])
        sums[TWO, rows, :] += fold(dv)
        dproj[TWO * DIM + rows.start:TWO * DIM + rows.stop, :] = dv.astype(BF16)

    def close_head(head):
        rows, one, two = head_rows(head)
        ds = dscores[head % TWO][...]
        for m, value in enumerate((nn(k[rows, :], ds) * HEAD ** -0.5, nt(q[rows, :], ds))):
            cos, sin = cos_ref[...], sin_ref[...]
            a, b = value[:HALF], value[HALF:]
            for at, out in ((one, a * cos + b * sin), (two, b * cos - a * sin)):
                dproj[m * DIM + at.start:m * DIM + at.stop, :] = out.astype(BF16)
                sums[m, at, :] += fold(out)

    open_head(ZERO)
    for head in range(HEADS):
        if head + ONE < HEADS:
            open_head(head + ONE)
        if head:
            close_head(head - ONE)
        values(head)
        weigh(head)
        if head == THREE:
            hook(ONE)
    close_head(HEADS - ONE)
    prefetch()
    hook(TWO)
    norm_to(x_ref.at[ZERO], c_ref, LN_PAR, h_ref)
    parts = [slice(DIM * m, DIM * m + DIM) for m in range(THREE)]
    s_a[...] = functools.reduce(jnp.add, [nn(wqkv[m], dproj[rows, :]) for m, rows in enumerate(parts)])
    for m, rows in enumerate(parts):
        add_to(g_qkv.at[m], nt(h_ref[...], dproj[rows, :]))
    gain = column(c_ref, LN_PAR)
    for cols in lane_tiles():
        dh = s_a[:, cols]
        dx, xhat = norm_back(dh, x_ref[ZERO, :, cols].astype(F32), gain)
        grad[:, cols] = (grad[:, cols].astype(F32) + dx).astype(BF16)
        sums[THREE] += dh * xhat
        sums[FOUR] += dh


def backward(dy, xs, q, k, v, probs, ctx, mid, act, slope, c, tables, w_qkv, w_o, w_up, w_down):
    def mlp_at(s):
        s = jnp.minimum(s, 15)
        odd = s // FOUR % TWO == ONE
        return ONE - s // EIGHT, jnp.where(odd, THREE, s % FOUR), ZERO, ZERO

    def attn_at(s):
        s = jnp.minimum(s, 15)
        odd = s // FOUR % TWO == ONE
        return jnp.where(s < EIGHT, ONE, ZERO) + jnp.where((s > 7) & (s < 12), ONE, ZERO), jnp.where(odd, s % FOUR, jnp.where(s < FOUR, ZERO, THREE)), ZERO, ZERO

    per_mlp = pl.BlockSpec((None, ONE, *SQUARE), mlp_at)
    per_attn = pl.BlockSpec((None, ONE, *SQUARE), attn_at)
    acc = [(*GRID, EIGHT, WIDTH)]
    scratch = [pltpu.VMEM((SEQS, *SQUARE), BF16), pltpu.VMEM((SEQS, *SQUARE), BF16), pltpu.VMEM((SEQS, HEADS, TOK), F32),
               pltpu.VMEM((HEADS, TOK, TOK), BF16), pltpu.VMEM((THREE, DIM, DIM), BF16), pltpu.VMEM((DIM, DIM), BF16),
               pltpu.VMEM(TALL, F32), pltpu.VMEM(TALL, BF16), pltpu.VMEM(TALL, BF16), pltpu.VMEM(SQUARE, BF16),
               pltpu.VMEM(SQUARE, F32), pltpu.VMEM(SQUARE, F32), pltpu.VMEM((TOK, TOK), BF16), pltpu.VMEM((TOK, TOK), BF16),
               pltpu.VMEM((EIGHT, *COLS), F32), pltpu.VMEM((THREE, *GRID, EIGHT, DIM), F32), pltpu.VMEM((*GRID, EIGHT, DIM), F32),
               pltpu.VMEM((FOUR, *GRID, EIGHT, DIM), F32), pltpu.VMEM((*GRID, FOUR, EIGHT, DIM), F32), pltpu.VMEM((32, DIM), F32), pltpu.VMEM((10, 32, DIM), F32)]
    counts = (ONE, THREE)
    scratch += [pltpu.VMEM((n, *GRID, EIGHT, WIDTH), F32) for n in counts for _ in range(THREE)]
    scratch += [pltpu.VMEM((n, EIGHT, WIDTH), F32) for n in counts for _ in range(THREE)]
    for ways in (ONE, TWO):
        for n in counts:
            for order in ORDERS:
                scratch += [pltpu.VMEM(s, F32) for s in landing_shapes(order, n, ways)]
    scratch += [DMA((TWO, THREE, 28)), DMA((TWO, THREE, 28)), DMA((10,)), DMA((10,)), DMA((EIGHT,)), DMA((TWO,)), DMA((TWO,))]
    outs = ((TWO, FOUR, FOUR, DIM), (TWO, FOUR, FFN), (TWO, SIXTEEN, DIM), (32, DIM))
    whole = [pl.BlockSpec(s, lambda i, n=len(s): (ZERO,) * n, pipeline_mode=pl.Buffered(ONE)) for s in outs]
    dx_at = lambda s: (jnp.clip(s - 12, ZERO, THREE), ZERO, ZERO)
    return pl.pallas_call(
        backward_kernel, grid=(19,),
        out_shape=[jax.ShapeDtypeStruct((SEQS, TOK, DIM), BF16)] + [jax.ShapeDtypeStruct(s, F32) for s in outs],
        out_specs=[pl.BlockSpec((ONE, TOK, DIM), dx_at)] + whole,
        in_specs=[pl.BlockSpec((ONE, TOK, DIM), lambda s: (jnp.minimum(s, THREE), ZERO, ZERO)), per_mlp, per_mlp, per_attn, per_attn, per_attn, per_attn,
                  once((HALF, TOK)), once((HALF, TOK)), pl.BlockSpec((None, *COLS), lambda s: (ONE - jnp.minimum(s, 15) // EIGHT, ZERO, ZERO))] + [HBM] * 7,
        scratch_shapes=scratch,
        compiler_params=pltpu.CompilerParams(collective_id=ONE, has_side_effects=True, vmem_limit_bytes=67043328,
                                             dimension_semantics=("arbitrary",)),
        name="backward")(dy, mid, ctx, q, k, v, xs, *tables, c, probs, slope, act, w_qkv, w_o, w_up, w_down)


def pack_shards(w_attn, w_up, w_down):
    attn = w_attn.reshape(TWO, FOUR, FOUR, FOUR, LANES).transpose(ZERO, ONE, THREE, TWO, FOUR).reshape(TWO, FOUR, SIXTEEN, LANES)
    up = w_up.reshape(TWO, FOUR, FOUR, FOUR, LANES).transpose(ZERO, TWO, THREE, ONE, FOUR).reshape(TWO, FOUR, SIXTEEN, LANES)
    down = w_down.reshape(TWO, SIXTEEN, FOUR, LANES).transpose(ZERO, TWO, ONE, THREE)
    return attn[:, :THREE, None], jnp.concatenate([attn[:, THREE:], up, down], axis=ONE).reshape(TWO, THREE, THREE, SIXTEEN, LANES)


def pack_small(b_attn, ln_par, b_up, b_down):
    row = jnp.concatenate([b_attn.reshape(TWO, SIXTEEN), ln_par.reshape(TWO, SIXTEEN), b_up, b_down, jnp.zeros((TWO, 12), b_up.dtype)], axis=ONE)
    return row.reshape(ONE, ONE, LANES).astype(F32)


def solution(mesh):
    batch_spec = P(AXIS)
    weight_specs = (P(None, None, AXIS, None), P(None, None, AXIS), P(None, None, AXIS),
                    P(None, AXIS, None), P(None, AXIS), P(None, AXIS, None), P(None, AXIS))

    def device_step(x, lengths, d_y, w_attn, b_attn, ln_par, w_up, b_up, w_down, b_down):
        tables = rotary_tables()
        pack_qkv, pack_mo = pack_shards(w_attn, w_up, w_down)
        xs, q, k, v, probs, ctx, mid, act, slope, c, w_qkv, w_o, w_up, w_down = forward(
            lengths, x, tables, pack_qkv, pack_mo, pack_small(b_attn, ln_par, b_up, b_down))
        grad, attn, up, down, small = backward(d_y, xs, q, k, v, probs, ctx, mid, act, slope, c, tables, w_qkv, w_o, w_up, w_down)
        me = lax.axis_index(AXIS)
        small = small.reshape(TWO, SIXTEEN, DIM)
        mine = lax.dynamic_slice(small, (ZERO, ZERO, FOUR * me), (TWO, SIXTEEN, FOUR))
        b_up_grad = lax.dynamic_slice(small[:, B_UP:B_DOWN].reshape(TWO, FFN), (ZERO, SIXTEEN * me), (TWO, SIXTEEN))
        return grad, attn, mine[:, :FOUR], mine[:, FOUR:EIGHT], up, b_up_grad, down, mine[:, 12]

    return jax.shard_map(device_step, mesh=mesh,
                         in_specs=(batch_spec, batch_spec, batch_spec) + weight_specs,
                         out_specs=(batch_spec,) + weight_specs,
                         check_vma=False)
```

profile of v0, /device:TPU:1, one launch (start us, length us, event | category | flops | bytes accessed | tf_op | source)
XLA Modules:
  0.0 420.1 jit_solution(14059098501685115699)
XLA Ops:
  0.6 1.0 fusion
  1.6 0.7 slice.25
  2.3 0.8 reshape.69
  3.1 0.8 bitcast_bitcast_fusion
  3.9 0.6 pad_maximum_fusion
  4.5 1.3 slice_bitcast_fusion.pack_qkv
  5.9 0.8 reshape.73
  6.6 0.8 reshape.74
  7.4 0.8 concatenate.7
  8.2 0.6 reshape.77.small_ref
  8.8 197.6 %forward.1 = (bf16[2,4,512,512]{3,2,1,0:T(8,128)(2,1)}, bf16[2,4,512,512]{3,2,1,0:T(8,128)(2,1)}, bf16[2,4,512,512]{3,2,1,0:T(8,128)(2,1)}, bf16[2,4,512,512]{3,...) custom-call(s32[4]{0:T(128)} %len_ref.1, ...), custom_call_target="tpu_custom_call" | custom-call | tf_op jit(solution)/shard_map/forward/pallas_call | solution.py:674
  206.4 204.5 %backward.1 = (bf16[4,512,512]{2,1,0:T(8,128)(2,1)}, f32[2,4,4,512]{3,2,1,0:T(4,128)}, f32[2,4,2048]{2,1,0:T(4,128)}, f32[2,16,512]{2,1,0:T(8,128)}, f32[32,512]{1,0:T(8,128)}) custom-call(bf16[4,512,512]{2,1,0:T(8,128)(2,1)} %dy_ref.1, bf16[2,4,512,512]{3,2,1,0:T(8,128)(2,1)} %get-tuple-element.27.mid_ref, f32[2,4,512,512]{3,2,1,0:T(8,128)} %get-tuple-element.28.ctx_ref, ...), custom_call_target="tpu_custom_call" | custom-call | tf_op jit(solution)/shard_map/backward/pallas_call | solution.py:1045
  410.9 0.0 copy-start.2
  410.9 0.0 copy-start.1
  411.0 0.0 copy-start
  411.0 0.8 slice_bitcast_fusion.1
  411.8 0.6 constant_dynamic-slice_fusion.2
  412.4 1.4 constant_dynamic-slice_fusion
  413.9 1.3 constant_dynamic-slice_fusion.3
  415.2 3.0 copy.28
  418.2 0.0 copy-done.2
  418.2 0.6 copy.29
  418.9 0.0 copy-done.1
  418.9 0.6 copy.30
  419.5 0.0 copy-done
  419.5 0.6 copy.31
  (4 shorter events, 0.0 us)
Async XLA Ops:
  410.9 7.3 %copy-start.2 = (f32[2,4,4,512]{3,2,1,0:T(4,128)S(1)}, f32[2,4,4,512]{3,2,1,0:T(4,128)}, u32[]{:S(2)}) copy-start(f32[2,4,4,512]{3,2,1,0:T(4,128)} %get-tuple-element.59) | copy-start | bytes 196612
  410.9 7.9 %copy-start.1 = (f32[2,4,2048]{2,1,0:T(4,128)S(1)}, f32[2,4,2048]{2,1,0:T(4,128)}, u32[]{:S(2)}) copy-start(f32[2,4,2048]{2,1,0:T(4,128)} %get-tuple-element.62) | copy-start | bytes 196612
  411.0 8.6 %copy-start = (f32[2,16,512]{2,1,0:T(8,128)S(1)}, f32[2,16,512]{2,1,0:T(8,128)}, u32[]{:S(2)}) copy-start(f32[2,16,512]{2,1,0:T(8,128)} %get-tuple-element.64) | copy-start | bytes 196612
where the time goes:
time: 421 us; the launch traced here: 420 us
  Pallas kernels  402 us (95%)
  local copies, waits for them, and re-layouts  15.7 us (4%)
    pallas_call x1, Pallas kernels, backward(): pl.pallas_call(backward_kernel, grid=(19,), out_shape=[jax.ShapeDtypeStru...  205 us
    pallas_call x1, Pallas kernels, forward(): pl.pallas_call(forward_kernel, grid=(SIXTEEN,), out_shape=[o[ZERO] for o...  198 us

commit v1 on v0

v1 whole, which is shorter than its diff:
```python
import math
import functools
import jax
import jax.numpy as jnp
from jax import lax
from jax.experimental import pallas as pl
from jax.experimental.pallas import tpu as pltpu
from jax.sharding import PartitionSpec as P

ZERO, ONE, TWO, THREE, FOUR = range(5)
EIGHT, SIXTEEN, WIDTH = 8, 16, 256

F32, BF16 = jnp.float32, jnp.bfloat16
SEQS, TOK, DIM, FFN, HEADS, HEAD, LANES = FOUR, 512, 512, 2048, EIGHT, 64, 128
HALF = HEAD // TWO
EPS = 1e-5
THETA = 10000.0
NEG_BIG = -1e30
B_ATTN, LN_PAR, B_UP, B_DOWN = ZERO, FOUR, EIGHT, 12


def nn(a, b):
    return lax.dot_general(a, b, (((ONE,), (ZERO,)), ((), ())), preferred_element_type=F32)


def nt(a, b):
    return lax.dot_general(a, b, (((ONE,), (ONE,)), ((), ())), preferred_element_type=F32)


def tn(a, b):
    return lax.dot_general(a, b, (((ZERO,), (ZERO,)), ((), ())), preferred_element_type=F32)


def lane_tiles(width=TOK, size=LANES):
    return [slice(i, i + size) for i in range(ZERO, width, size)]


def column(c_ref, lane, width=LANES):
    return jnp.broadcast_to(c_ref[:, lane:lane + ONE], (c_ref.shape[ZERO], width))


def total(value):
    return jnp.sum(value, axis=ZERO, keepdims=True)


def normed(x):
    centred = x - total(x) * (1.0 / DIM)
    rstd = lax.rsqrt(total(centred * centred) * (1.0 / DIM) + EPS)
    return centred * rstd, rstd


def norm_to(x_ref, c_ref, lane, h_ref):
    gain, shift = column(c_ref, lane), column(c_ref, lane + ONE)
    for cols in lane_tiles():
        h_ref[:, cols] = (normed(x_ref[:, cols].astype(F32))[ZERO] * gain + shift).astype(BF16)


def fold(value):
    parts = [value[:, cols] for cols in lane_tiles(value.shape[ONE])]
    return functools.reduce(jnp.add, parts)


def seq_spec(shape):
    return pl.BlockSpec((ONE, *shape), lambda s: (s,) + (ZERO,) * len(shape))


def once(shape):
    return pl.BlockSpec(shape, lambda s: (ZERO,) * len(shape), pipeline_mode=pl.Buffered(ONE))


def act_shape(rows, dtype):
    return jax.ShapeDtypeStruct((SEQS, rows, TOK), dtype)


PARAMS = pltpu.CompilerParams(vmem_limit_bytes=60 << 20, dimension_semantics=("arbitrary",))
SQUARE, TALL, WIDE, COLS = (DIM, TOK), (FFN, TOK), (DIM, FFN), (DIM, LANES)


def rotary_tables():
    inv_freq = 1.0 / (THETA ** (jnp.arange(HALF, dtype=F32) * (2.0 / HEAD)))
    angles = inv_freq[:, None] * jnp.arange(TOK, dtype=F32)[None, :]
    return jnp.cos(angles), jnp.sin(angles)


MESH = pl.DeviceIdType.MESH
AXIS = "fsdp"
ORDERS = ((TWO, ONE, ZERO), (ONE, ZERO, TWO), (ZERO, TWO, ONE))


class Place:
    def __init__(self):
        me = lax.axis_index(AXIS)
        self.core = lax.rem(me, TWO)
        self.pos = (me // 32, lax.rem(me // EIGHT, FOUR), lax.rem(me // TWO, FOUR))
        self.partner = me + ONE - TWO * self.core

    def coord(self, dim, delta):
        return lax.rem(self.pos[dim] + (delta + FOUR), FOUR)

    def device(self, offsets):
        pos = [self.coord(dim, offsets.get(dim, ZERO)) for dim in range(THREE)]
        return pos[ZERO] * 32 + pos[ONE] * EIGHT + pos[TWO] * TWO + self.core

    def greet(self):
        barrier = pltpu.get_barrier_semaphore()

        @pl.loop(ONE, 64)
        def _(i):
            offsets = {ZERO: i // SIXTEEN, ONE: lax.rem(i // FOUR, FOUR), TWO: lax.rem(i, FOUR)}

            @pl.when(offsets[ZERO] * offsets[ONE] * offsets[TWO] == ZERO)
            def _():
                pl.semaphore_signal(barrier, inc=ONE, device_id=(self.device(offsets),), device_id_type=MESH)
        pl.semaphore_signal(barrier, inc=ONE, device_id=(self.partner,), device_id_type=MESH)

    def met(self):
        pl.semaphore_wait(pltpu.get_barrier_semaphore(), 37)


def remote(src, dst, send_sem, recv_sem, device):
    return pltpu.make_async_remote_copy(src_ref=src, dst_ref=dst, send_sem=send_sem, recv_sem=recv_sem,
                                        device_id=(device,), device_id_type=MESH)


LINE = (ONE, -ONE, TWO)


def plane_offsets(order, k, sign=ONE):
    return {order[ONE]: sign * (k // FOUR), order[TWO]: sign * lax.rem(k, FOUR)}


class Gather:
    def __init__(self, place, buf, order, send, recv):
        self.place, self.buf, self.order, self.send, self.recv = place, buf, order, send, recv

    def block(self, offsets, whole=()):
        index = [slice(ZERO, FOUR) if dim in whole else pl.ds(self.place.coord(dim, offsets.get(dim, ZERO)), ONE) for dim in range(THREE)]
        return self.buf.at[index[ZERO], index[ONE], index[TWO], pl.ds(self.place.core, ONE)]

    def copy(self, ref, key, device):
        return remote(ref, ref, self.send.at[key], self.recv.at[key], device)

    def plane_start(self):
        @pl.loop(ONE, SIXTEEN)
        def _(k):
            self.copy(self.block({}), k, self.place.device(plane_offsets(self.order, k))).start()

    def plane_wait(self):
        @pl.loop(ONE, SIXTEEN)
        def _(k):
            self.copy(self.block(plane_offsets(self.order, k, -ONE)), k, self.place.partner).wait_recv()

    def line(self, i, sign):
        offsets = {self.order[ZERO]: sign * LINE[i]}
        return self.block(offsets, self.order[ONE:])

    def line_start(self):
        for i, delta in enumerate(LINE):
            self.copy(self.line(i, ZERO), SIXTEEN + i, self.place.device({self.order[ZERO]: delta})).start()

    def line_wait(self):
        for i in range(THREE):
            self.copy(self.line(i, -ONE), SIXTEEN + i, self.place.partner).wait_recv()

    def share(self, core):
        return self.copy(self.buf.at[:, :, :, pl.ds(core, ONE)], 19, self.place.partner)

    def share_start(self):
        self.share(self.place.core).start()

    def end(self):
        self.share(ONE - self.place.core).wait_recv()

        @pl.loop(ONE, SIXTEEN)
        def _(k):
            self.copy(self.block({}), k, self.place.partner).wait_send()
        for i in range(THREE):
            self.copy(self.line(i, ZERO), SIXTEEN + i, self.place.partner).wait_send()
        self.share(self.place.core).wait_send()


def gather_steps(gathers):
    def each(*names):
        def step():
            for name in names:
                for g in gathers:
                    getattr(g, name)()
        return step

    return [each("plane_start"), each("plane_wait", "line_start"), each("line_wait", "share_start"), each("end")]


class Scatter:
    def __init__(self, place, grads, acc, got_a, got_b, got_p, other, order, send, recv):
        self.place, self.grads, self.acc, self.order = place, grads, acc, order
        self.got_a, self.got_b, self.got_p, self.other, self.send, self.recv = got_a, got_b, got_p, other, send, recv
        self.units = acc.shape[ZERO]

    def columns(self, core):
        return pl.ds(pl.multiple_of(core * WIDTH, WIDTH), WIDTH)

    def swap_copy(self, u):
        place = self.place
        return remote(self.grads(u).at[:, :, :, :, self.columns(ONE - place.core)], self.acc.at[u], self.send.at[20 + u], self.recv.at[20 + u], place.partner)

    def swap(self):
        for u in range(self.units):
            self.swap_copy(u).start()

    def swapped(self):
        for u in range(self.units):
            self.swap_copy(u).wait()
            grad, acc = self.grads(u), self.acc

            @pl.loop(ZERO, FOUR)
            def _(z):
                acc[u, z] = acc[u, z] + grad[z, :, :, :, self.columns(self.place.core)]

    def part(self, delta, half=None):
        index = [slice(ZERO, FOUR)] * THREE
        index[self.order[ZERO]] = pl.ds(self.place.coord(self.order[ZERO], delta), ONE)
        return self.acc.at[:, index[ZERO], index[ONE], index[TWO], :, slice(ZERO, WIDTH) if half is None else lane_tiles()[half]]

    def ring(self, step, way):
        delta = (ONE, -ONE)[way]
        device = self.place.device({self.order[ZERO]: delta})
        if step == ZERO:
            src, dst = self.part(TWO, way), self.got_a.at[:, :, :, :, :, lane_tiles()[way]]
        else:
            src, dst = self.part(delta), self.got_b.at[way]
        key = SIXTEEN + TWO * step + way
        return remote(src, dst, self.send.at[key], self.recv.at[key], device)

    def ring_start(self):
        for way in range(TWO):
            self.ring(ZERO, way).start()

    def ring_turn(self):
        for way in range(TWO):
            self.ring(ZERO, way).wait_recv()
            self.add((ONE, -ONE)[way], way, self.got_a)
            self.ring(ONE, way).start()

    def add(self, delta, half, *refs):
        dim, acc = self.order[ZERO], self.acc
        at = self.place.coord(dim, delta)
        columns = slice(ZERO, WIDTH) if half is None else lane_tiles()[half]

        @pl.loop(ZERO, FOUR)
        def _(i):
            index = [i if d == self.order[ONE] else slice(ZERO, FOUR) for d in range(THREE)]
            there = [slice(None), *index, slice(None), columns]
            here = list(there)
            here[ONE + dim] = pl.ds(at, ONE)
            there[ONE + dim] = slice(ZERO, ONE)
            value = acc[tuple(here)]
            for ref in refs:
                value = value + ref[tuple(there)]
            acc[tuple(here)] = value

    def plane_copy(self, k):
        offsets = plane_offsets(self.order, k)
        index = [pl.ds(self.place.coord(dim, offsets.get(dim, ZERO)), ONE) for dim in range(THREE)]
        src = self.acc.at[:, index[ZERO], index[ONE], index[TWO]]
        return remote(src, self.got_p.at[k], self.send.at[k], self.recv.at[k], self.place.device(offsets))

    def plane_start(self):
        for way in range(TWO):
            self.ring(ONE, way).wait_recv()
        self.add(ZERO, None, self.got_b.at[ZERO], self.got_b.at[ONE])

        @pl.loop(ONE, SIXTEEN)
        def _(k):
            self.plane_copy(k).start()

    def own(self):
        z, y, x = [pl.ds(p, ONE) for p in self.place.pos]
        return self.acc.at[:, z, y, x]

    def last_copy(self):
        return remote(self.own(), self.other, self.send.at[23], self.recv.at[23], self.place.partner)

    def last(self):
        @pl.loop(ONE, SIXTEEN)
        def _(k):
            self.plane_copy(k).wait_recv()
        own = self.own()
        own[...] = functools.reduce(jnp.add, [self.got_p[k] for k in range(ONE, SIXTEEN)], own[...])
        self.last_copy().start()

    def finish(self, store):
        self.last_copy().wait_recv()
        first = self.place.core == ZERO
        for u in range(self.units):
            own, came = self.own()[u, ZERO, ZERO, ZERO], self.other[u, ZERO, ZERO, ZERO]
            store(u, jnp.concatenate([jnp.where(first, own, came), jnp.where(first, came, own)], axis=ONE))
        for step in range(TWO):
            for way in range(TWO):
                self.ring(step, way).wait_send()

        @pl.loop(ONE, SIXTEEN)
        def _(k):
            self.plane_copy(k).wait_send()
        self.last_copy().wait_send()


def landing_shapes(order, units):
    size = [FOUR, FOUR, FOUR]
    size[order[ZERO]] = ONE
    return (units, *size, EIGHT, WIDTH), (TWO, units, *size, EIGHT, WIDTH), (SIXTEEN, units, ONE, ONE, ONE, EIGHT, WIDTH), (units, ONE, ONE, ONE, EIGHT, WIDTH)


class Small:
    def __init__(self, place, value, slots, send, recv):
        self.place, self.value, self.slots, self.send, self.recv = place, value, slots, send, recv

    def copies(self, stage):
        if stage == THREE:
            return [remote(self.value, self.slots.at[9], self.send.at[9], self.recv.at[9], self.place.partner)]
        return [remote(self.value, self.slots.at[stage * THREE + k], self.send.at[stage * THREE + k], self.recv.at[stage * THREE + k],
                       self.place.device({stage: delta})) for k, delta in enumerate((ONE, -ONE, TWO))]

    def start(self, stage):
        for copy in self.copies(stage):
            copy.start()

    def finish(self, stage):
        copies = self.copies(stage)
        for copy in copies:
            copy.wait()
        value = self.value[...]
        for k in range(len(copies)):
            value = value + self.slots[stage * THREE + k]
        self.value[...] = value

    def steps(self):
        def turn(stage):
            def step():
                self.finish(stage)
                self.start(stage + ONE)
            return step

        return [lambda: self.start(ZERO), turn(ZERO), turn(ONE), turn(TWO), lambda: self.finish(THREE)]


VMEM = pl.BlockSpec(memory_space=pltpu.VMEM)
HBM = pl.BlockSpec(memory_space=pl.ANY)
DMA = pltpu.SemaphoreType.DMA


COLOURS = ((THREE, FOUR, 5), (6, 7, EIGHT), (9, 10, 11))
GRID = (FOUR, FOUR, FOUR)


def spread(buf, u, out_ref, column_base):
    @pl.loop(ZERO, EIGHT)
    def _(block):
        for part in range(FOUR):
            g = block * FOUR + part
            tiles = [buf[block // TWO, lax.rem(block, TWO) * TWO + part // TWO, part % TWO * TWO + k // TWO, k % TWO, u].astype(F32) for k in range(FOUR)]
            rows = pl.ds(pl.multiple_of(g * SIXTEEN, SIXTEEN), SIXTEEN)
            for j, cols in enumerate(lane_tiles()):
                value = jnp.concatenate([t[FOUR * j:FOUR * j + FOUR] for t in tiles], axis=ZERO).astype(BF16)
                out_ref[rows, column_base + cols.start:column_base + cols.stop] = value


def spread_down(buf, u, out_ref, cols):
    @pl.loop(ZERO, SIXTEEN)
    def _(i):
        for k in range(EIGHT):
            d = i * EIGHT + k
            out_ref[pl.ds(pl.multiple_of(d * SIXTEEN, SIXTEEN), SIXTEEN), cols] = buf[i // FOUR, lax.rem(i, FOUR), k // TWO, k % TWO, u]


def same(shape, test):
    row = lax.broadcasted_iota(jnp.int32, shape, ZERO)
    col = lax.broadcasted_iota(jnp.int32, shape, ONE)
    return jnp.where(test(row, col), 1.0, 0.0)


def small_columns(small_ref, c_ref):
    rows = [small_ref[z, y, x, c, ZERO] for z in range(FOUR) for y in range(FOUR) for x in range(FOUR) for c in range(TWO)]
    table = jnp.concatenate(rows, axis=ZERO).astype(BF16)
    quads = nn(same((DIM, LANES), lambda r, c: r // FOUR == c).astype(BF16), table)
    quads = (quads * same((DIM, LANES), lambda r, c: r % FOUR == c % FOUR)).astype(BF16)
    mask = same((DIM, LANES), lambda r, c: r % SIXTEEN == c % SIXTEEN)
    pick = same((DIM, 32), lambda r, c: r // SIXTEEN == c).astype(BF16)
    ups = [(nn(pick, table[32 * k:32 * k + 32]) * mask).astype(BF16) for k in range(FOUR)]
    for layer in range(TWO):
        def is_up(r):
            return r // SIXTEEN == layer * FOUR + TWO

        value = nn(quads, same((LANES, LANES), lambda r, c: (r // 64 == layer) & (r % 64 // FOUR == c) & ~is_up(r)).astype(BF16))
        for k in range(FOUR):
            value = value + nn(ups[k], same((LANES, LANES), lambda r, c: is_up(r) & (c == B_UP + k)).astype(BF16))
        c_ref[layer] = value


def tile_of(rows):
    rows = rows.astype(F32)
    return jnp.concatenate([rows[:, cols] for cols in lane_tiles()], axis=ZERO).astype(BF16)


def small_row(b_attn, ln_par, b_up, b_down):
    lane = lax.broadcasted_iota(jnp.int32, (ONE, LANES), ONE)
    row = jnp.zeros((ONE, LANES), F32)
    pieces = []
    for l in range(TWO):
        for m in range(FOUR):
            pieces += [(b_attn[l, m:m + ONE, :], 64 * l + FOUR * m), (ln_par[l, m:m + ONE, :], 64 * l + FOUR * m + SIXTEEN)]
        pieces += [(b_up[l:l + ONE, :], 64 * l + 32), (b_down[l:l + ONE, :], 64 * l + 48)]
    for piece, at in pieces:
        n = piece.shape[ONE]
        wide = jnp.concatenate([piece.astype(F32), jnp.zeros((ONE, LANES - n), F32)], axis=ONE)
        wide = pltpu.roll(wide, at, ONE) if at else wide
        row = jnp.where((lane >= at) & (lane < at + n), wide, row)
    return row


def hooks(slot, plan):
    def hook(at):
        for slots, run in plan:
            mine = [when for when in slots if when % FOUR == at]
            if mine:
                pl.when(functools.reduce(jnp.logical_or, [slot + at == when for when in mine]))(run)
    return hook


def forward_kernel(len_ref, x_ref, cos_ref, sin_ref, w_attn, b_attn, ln_par, w_up, b_up, w_down, b_down,
                   xs_out, q_ref, k_ref, v_ref, p_hbm, ctx_ref, mid_ref, act_ref, slope_ref, c_ref,
                   nat_qkv, nat_wo, nat_up, nat_down,
                   xs, ctxb, wqkv, wo, up, down, n_qkv, n_wo, n_up, n_down, p_buf, h_ref, s_a, s_b, s_c,
                   sbuf, q0, q1, q2, m0, m1, m2, send, recv, p_sem, nat_sem):
    step = pl.program_id(ZERO)
    phase, seq, layer = step // FOUR, lax.rem(step, FOUR), step // EIGHT
    place = Place()
    z, y, x = place.pos
    qkv_bufs, mo_bufs = (q0, q1, q2), (m0, m1, m2)

    def group(bufs, base, l):
        return [Gather(place, b.at[l], ORDERS[k], send.at[base + k, l], recv.at[base + k, l]) for k, b in enumerate(bufs)]

    little = Gather(place, sbuf, ORDERS[ZERO], send.at[6, ZERO], recv.at[6, ZERO])

    def nat_copies(which, l):
        if which == ZERO:
            return [pltpu.make_async_copy(n_qkv, nat_qkv.at[l], nat_sem.at[ZERO])]
        return [pltpu.make_async_copy(src, dst.at[l], nat_sem.at[ONE + i]) for i, (src, dst) in enumerate(((n_wo, nat_wo), (n_up, nat_up), (n_down, nat_down)))]

    def wait(copies):
        for copy in copies:
            copy.wait()

    def start(copies):
        for copy in copies:
            copy.start()

    def take_qkv():
        pl.when(step > ZERO)(lambda: wait(nat_copies(ZERO, layer)))
        for m in range(THREE):
            spread(qkv_bufs[m].at[layer], ZERO, n_qkv.at[m], ZERO)
            wqkv[m] = n_qkv[m].T
        start(nat_copies(ZERO, layer))

    def take_mo():
        pl.when(step > EIGHT)(lambda: wait(nat_copies(ONE, layer)))
        for colour in range(THREE):
            for u, unit in enumerate(COLOURS[colour]):
                buf = mo_bufs[colour].at[layer]
                if unit == THREE:
                    spread(buf, u, n_wo, ZERO)
                    wo[...] = n_wo[...].T
                elif unit < EIGHT:
                    part = slice(DIM * (unit - FOUR), DIM * (unit - THREE))
                    spread(buf, u, n_up, part.start)
                    up[part, :] = n_up[:, part].T
                else:
                    spread_down(buf, u, n_down, lane_tiles()[unit - EIGHT])
        for k in range(FOUR):
            part = slice(DIM * k, DIM * k + DIM)
            down[:, part] = n_down[part, :].T
        start(nat_copies(ONE, layer))

    @pl.when(step == ZERO)
    def _():
        place.greet()
        for l in range(TWO):
            for unit in range(12):
                if unit < FOUR:
                    tile = tile_of(w_attn[l, unit])
                elif unit < EIGHT:
                    tile = tile_of(w_up[l, :, DIM * (unit - FOUR):DIM * (unit - THREE)])
                else:
                    tile = w_down[l, :, lane_tiles()[unit - EIGHT]]
                if unit < THREE:
                    qkv_bufs[unit][l, z, y, x, place.core, ZERO] = tile
                else:
                    mo_bufs[(unit - THREE) // THREE][l, z, y, x, place.core, (unit - THREE) % THREE] = tile
        sbuf[z, y, x, place.core, ZERO] = small_row(b_attn, ln_par, b_up, b_down)
        place.met()
        for run in gather_steps(group(qkv_bufs, ZERO, ZERO) + [little]):
            run()
        small_columns(sbuf, c_ref)

    attn_hook = hooks(step * FOUR, [((when, when + 32), run) for when, run in zip(MO_SLOTS, gather_steps(group(mo_bufs, THREE, layer)))])
    mlp_hook = hooks(step * FOUR, [((when,), run) for when, run in zip(QKV_SLOTS, gather_steps(group(qkv_bufs, ZERO, ONE)))])

    @pl.when(phase % TWO == ZERO)
    def _():
        pl.when(seq == ZERO)(take_qkv)

        @pl.when(step < FOUR)
        def _():
            xs[seq] = x_ref[ZERO].T
            xs_out[ZERO, ZERO] = xs[seq]

        attn_hook(ZERO)
        copies = [pltpu.make_async_copy(p_buf.at[head], p_hbm.at[layer, seq, head], p_sem.at[head]) for head in range(HEADS)]
        attn_forward(len_ref[seq], xs.at[seq], wqkv, c_ref.at[layer], cos_ref, sin_ref, q_ref.at[ZERO, ZERO], k_ref.at[ZERO, ZERO],
                     v_ref.at[ZERO, ZERO], p_buf, ctx_ref.at[ZERO, ZERO], ctxb.at[seq], h_ref, s_a, s_b, s_c, attn_hook,
                     lambda: pl.when(step > ZERO)(lambda: wait(copies)))
        start(copies)
        pl.when(step == 11)(lambda: wait(copies))
        attn_hook(THREE)

    @pl.when(phase % TWO == ONE)
    def _():
        pl.when(seq == ZERO)(take_mo)
        mlp_hook(ZERO)
        mlp_forward(layer, ctxb.at[seq], xs.at[seq], wo, up, down, c_ref.at[layer], mid_ref.at[ZERO, ZERO], act_ref.at[ZERO, ZERO], slope_ref.at[ZERO, ZERO],
                    h_ref, s_a, s_b, mlp_hook)

        @pl.when(layer == ZERO)
        def _():
            xs_out[ZERO, ZERO] = xs[seq]
        mlp_hook(THREE)

    @pl.when(step == 15)
    def _():
        for which in range(TWO):
            wait(nat_copies(which, ONE))


def attn_forward(length, xt, w, c_ref, cos_ref, sin_ref, q_ref, k_ref, v_ref, p_buf, ctx_ref, ctxb, h_ref, s_a, s_b, s_c, hook, free):
    norm_to(xt, c_ref, LN_PAR, h_ref)
    for m, acc in enumerate((s_a, s_b, s_c)):
        acc[...] = nn(w[m], h_ref[...])
    for m, (acc, out) in enumerate(((s_a, q_ref), (s_b, k_ref), (s_c, v_ref))):
        bias = column(c_ref, B_ATTN + m)
        for cols in lane_tiles():
            if m == TWO:
                out[:, cols] = (acc[:, cols] + bias).astype(BF16)
                continue
            cos, sin = cos_ref[:, cols], sin_ref[:, cols]
            for head in range(HEADS):
                _, one, two = head_rows(head)
                a, b = acc[one, cols] + bias[one], acc[two, cols] + bias[two]
                if m == ZERO:
                    a, b = a * HEAD ** -0.5, b * HEAD ** -0.5
                out[one, cols] = (a * cos - b * sin).astype(BF16)
                out[two, cols] = (b * cos + a * sin).astype(BF16)
    hook(ONE)
    free()
    key = lax.broadcasted_iota(jnp.int32, (SIXTEEN, TOK), ONE)
    row = lax.broadcasted_iota(jnp.int32, (SIXTEEN, TOK), ZERO)
    bias_rows = jnp.where((row == ZERO) & (key >= length), NEG_BIG, 0.0).astype(BF16)
    one_rows = jnp.where(row == ZERO, 1.0, 0.0).astype(BF16)
    scores = (s_a, s_b)

    def open_head(head):
        rows = head_rows(head)[ZERO]
        keys = jnp.concatenate([k_ref[rows, :], bias_rows], axis=ZERO)
        queries = jnp.concatenate([q_ref[rows, :], one_rows], axis=ZERO)
        scores[head % TWO][...] = tn(keys, queries)

    def weigh(head):
        value = scores[head % TWO][...]
        weight = jnp.exp(value - jnp.max(value, axis=ZERO, keepdims=True))
        p_buf[head] = (weight * (1.0 / total(weight))).astype(BF16)

    def close_head(head):
        rows = head_rows(head)[ZERO]
        ctx = nn(v_ref[rows, :], p_buf[head])
        ctx_ref[rows, :] = ctx
        ctxb[rows, :] = ctx.astype(BF16)

    open_head(ZERO)
    for head in range(HEADS):
        if head + ONE < HEADS:
            open_head(head + ONE)
        if head:
            close_head(head - ONE)
        weigh(head)
        if head == THREE:
            hook(TWO)
    close_head(HEADS - ONE)


def mlp_forward(layer, ctxb, xt, wo, up, down, c_ref, mid_ref, act_ref, slope_ref, h_ref, s_a, s_b, hook):
    s_a[...] = nn(wo[...], ctxb[...])
    for cols in lane_tiles():
        mid_ref[:, cols] = (xt[:, cols].astype(F32) + s_a[:, cols] + column(c_ref, B_ATTN + THREE)).astype(BF16)
    norm_to(mid_ref, c_ref, LN_PAR + TWO, h_ref)
    hook(ONE)
    pre = (s_a, s_b)
    parts = [slice(DIM * k, DIM * k + DIM) for k in range(FOUR)]

    def open_part(k):
        pre[k % TWO][...] = nn(up[parts[k], :], h_ref[...])

    open_part(ZERO)
    for k, rows in enumerate(parts):
        if k < THREE:
            open_part(k + ONE)
        for cols in lane_tiles():
            value = pre[k % TWO][:, cols] + column(c_ref, B_UP + k)
            scaled = value * math.sqrt(0.5)
            cdf = 0.5 + 0.5 * lax.erf(scaled)
            density = jnp.exp2(scaled * scaled * -math.log2(math.e) - 0.5 * math.log2(2.0 * math.pi))
            act_ref[rows, cols] = (value * cdf).astype(BF16)
            slope_ref[rows, cols] = cdf + value * density
        if k == ONE:
            hook(TWO)

    @pl.when(layer == ZERO)
    def _():
        out = nn(down[...], act_ref[...])
        for cols in lane_tiles():
            xt[:, cols] = (mid_ref[:, cols].astype(F32) + out[:, cols] + column(c_ref, B_DOWN)).astype(BF16)


MO_SLOTS = (ZERO, 5, 13, 15)
QKV_SLOTS = (SIXTEEN, 22, 26, 28)


def forward(lengths, x, tables, params):
    def saved(index, rows, dtype):
        return jax.ShapeDtypeStruct((TWO, SEQS, rows, TOK), dtype), pl.BlockSpec((ONE, ONE, rows, TOK), index)

    def attn_at(s):
        return s // EIGHT, jnp.where(s // FOUR % TWO == ZERO, s % FOUR, THREE), ZERO, ZERO

    def mlp_at(s):
        odd = s // FOUR % TWO == ONE
        return jnp.where(s < 12, ZERO, ONE), jnp.where(odd, s % FOUR, jnp.where(s < FOUR, ZERO, THREE)), ZERO, ZERO

    def xs_at(s):
        return jnp.where(s < FOUR, ZERO, ONE), jnp.where(s < EIGHT, s % FOUR, THREE), ZERO, ZERO

    outs = [saved(xs_at, DIM, BF16)] + [saved(attn_at, DIM, BF16)] * THREE
    outs += [(jax.ShapeDtypeStruct((TWO, SEQS, HEADS, TOK, TOK), BF16), HBM), saved(attn_at, DIM, F32)]
    outs += [saved(mlp_at, DIM, BF16), saved(mlp_at, FFN, BF16), saved(mlp_at, FFN, F32)]
    outs += [(jax.ShapeDtypeStruct((TWO, *COLS), F32), once((TWO, *COLS)))]
    weights = ((THREE, DIM, DIM), (DIM, DIM), (DIM, FFN), (FFN, DIM))
    outs += [(jax.ShapeDtypeStruct((TWO, *w), BF16), HBM) for w in weights]
    scratch = [(SEQS, *SQUARE), (SEQS, *SQUARE), weights[ZERO], weights[ONE], weights[THREE], weights[TWO], *weights, (HEADS, TOK, TOK), SQUARE]
    scratch = [pltpu.VMEM(s, BF16) for s in scratch] + [pltpu.VMEM(SQUARE, F32)] * THREE + [pltpu.VMEM((*GRID, TWO, ONE, ONE, LANES), F32)]
    scratch += [pltpu.VMEM((TWO, *GRID, TWO, n, SIXTEEN, LANES), BF16) for n in (ONE, THREE) for _ in range(THREE)]
    scratch += [DMA((7, TWO, 20)), DMA((7, TWO, 20)), DMA((HEADS,)), DMA((FOUR,))]
    return pl.pallas_call(
        forward_kernel, grid=(SIXTEEN,),
        out_shape=[o[ZERO] for o in outs], out_specs=[o[ONE] for o in outs],
        in_specs=[pl.BlockSpec(memory_space=pltpu.SMEM), pl.BlockSpec((ONE, *SQUARE), lambda s: (jnp.minimum(s, THREE), ZERO, ZERO)),
                  once((HALF, TOK)), once((HALF, TOK))] + [once(p.shape) for p in params],
        scratch_shapes=scratch,
        compiler_params=pltpu.CompilerParams(collective_id=ZERO, has_side_effects=True, vmem_limit_bytes=67043328,
                                             dimension_semantics=("arbitrary",)),
        name="forward")(lengths, x, *tables, *params)


def norm_back(dh, x, gain):
    xhat, rstd = normed(x)
    dxhat = dh * gain
    mean_one = total(dxhat) * (1.0 / DIM)
    mean_two = total(dxhat * xhat) * (1.0 / DIM)
    return rstd * (dxhat - mean_one - xhat * mean_two), xhat


def columns_of(pairs):
    lane = lax.broadcasted_iota(jnp.int32, COLS, ONE)
    value = jnp.zeros(COLS, F32)
    for at, partial in pairs:
        value = jnp.where(lane == at, jnp.sum(partial, axis=ONE, keepdims=True), value)
    return value


def head_rows(head):
    return slice(HEAD * head, HEAD * head + HEAD), slice(HEAD * head, HEAD * head + HALF), slice(HEAD * head + HALF, HEAD * head + HEAD)


class Reduce:
    def __init__(self, place, units, grads, buffers, send, recv):
        self.units = units
        self.scatters = [Scatter(place, (lambda u, k=k: grads(units[k][u])), *buffers[k], ORDERS[k], send.at[k], recv.at[k]) for k in range(THREE)]

    def steps(self, store):
        def each(*names):
            def step():
                for name in names:
                    for s in self.scatters:
                        getattr(s, name)()
            return step

        def finish():
            for units, s in zip(self.units, self.scatters):
                s.finish(lambda u, full, units=units: store(units[u], full))

        return [each("swap"), each("swapped", "ring_start"), each("ring_turn"), each("plane_start"), each("last"), finish]


def backward_kernel(dy_ref, mid_ref, ctx_ref, q_ref, k_ref, v_ref, x_ref, cos_ref, sin_ref, c_ref, p_hbm, slope_hbm, act_hbm,
                    qkv_hbm, wo_hbm, up_hbm, down_hbm,
                    dx_ref, attn_out, up_out, down_out, small_out, *refs):
    (grad, dctx, delta, big, wqkv, wo, slope, act, dpre, h_ref, s_a, s_b, d_a, d_b, sums,
     g_qkv, g_wo, g_up, g_down, rows_ref, slots_ref), refs = refs[:21], refs[21:]
    qkv_bufs, mo_bufs, refs = [refs[5 * k:5 * k + 5] for k in range(THREE)], [refs[5 * k + 15:5 * k + 20] for k in range(THREE)], refs[30:]
    send, recv, ssend, srecv, big_sem, w_sem, mlp_sem = refs
    step = pl.program_id(ZERO)
    phase, seq = step // FOUR, lax.rem(step, FOUR)
    layer = ONE - step // EIGHT
    place = Place()

    def grads(unit):
        if unit < THREE:
            return g_qkv.at[unit]
        if unit == THREE:
            return g_wo
        if unit < EIGHT:
            return g_up.at[unit - FOUR]
        return g_down.at[:, :, :, unit - EIGHT]

    live = step < SIXTEEN
    turn = jnp.where(live, ZERO, ONE)
    qkv_sums = Reduce(place, ((ZERO,), (ONE,), (TWO,)), grads, [(a, ra, rb, rp.at[turn], o) for a, ra, rb, rp, o in qkv_bufs], send.at[turn], recv.at[turn])
    mo_sums = Reduce(place, COLOURS, grads, mo_bufs, send.at[TWO], recv.at[TWO])
    tiny = Small(place, rows_ref, slots_ref, ssend, srecv)
    first_core = place.core == ZERO

    def store(l):
        def put(unit, full):
            if unit < EIGHT:
                mine = jnp.where(first_core, full[:FOUR], full[FOUR:])
                if unit < FOUR:
                    attn_out[l, unit] = mine
                else:
                    up_out[l, :, DIM * (unit - FOUR):DIM * (unit - THREE)] = mine
            else:
                at = EIGHT * (unit % TWO)

                @pl.when(place.core == (unit - EIGHT) // TWO)
                def _():
                    down_out[l, at:at + EIGHT] = full
        return put

    def mlp_weights(l):
        copies = [pltpu.make_async_copy(wo_hbm.at[l], wo, w_sem.at[ZERO])]
        for k in range(FOUR):
            part = pl.ds(DIM * k, DIM)
            copies.append(pltpu.make_async_copy(down_hbm.at[l, part], big.at[k], big_sem.at[k]))
            copies.append(pltpu.make_async_copy(up_hbm.at[l, :, part], big.at[FOUR + k], big_sem.at[FOUR + k]))
        return copies

    def attn_weights(l):
        return [pltpu.make_async_copy(qkv_hbm.at[l], wqkv, w_sem.at[ONE])]

    def probs(l, s):
        return [pltpu.make_async_copy(p_hbm.at[l, s, k], big.at[k], big_sem.at[k]) for k in range(HEADS)]

    def saved_mlp(l, s):
        return [pltpu.make_async_copy(slope_hbm.at[l, s], slope, mlp_sem.at[ZERO]), pltpu.make_async_copy(act_hbm.at[l, s], act, mlp_sem.at[ONE])]

    def start(copies):
        for copy in copies:
            copy.start()

    def wait(copies):
        for copy in copies:
            copy.wait()

    @pl.when(step == ZERO)
    def _():
        place.greet()
        start(mlp_weights(ONE) + saved_mlp(ONE, ZERO) + attn_weights(ONE))

    pl.when(step == ONE)(place.met)
    mo_steps, qkv_steps = mo_sums.steps(store(layer)), qkv_sums.steps(store(ONE - turn))
    late_steps = mo_sums.steps(store(ONE - turn))[FOUR:]
    attn_hook = hooks(step * FOUR, [((when, when + 32), run) for when, run in zip((SIXTEEN, 20, 24, 30), mo_steps)])
    mlp_plan = list(zip(((37, 69), (38, 70)), late_steps))
    mlp_plan += list(zip(((32, 64), (33, 65), (38, 66), (43, 67), (47, 71), (47, 71)), qkv_steps))
    mlp_plan += [((when,), run) for when, run in zip((64, 65, 66, 67, 71), tiny.steps())]
    mlp_hook = hooks(step * FOUR, mlp_plan)

    @pl.when(phase % TWO == ZERO)
    def _():
        @pl.when((seq == ZERO) & live)
        def _():
            for ref in (g_wo, g_up, g_down, sums):
                ref[...] = jnp.zeros_like(ref)

        @pl.when(step < FOUR)
        def _():
            grad[seq] = dy_ref[ZERO].T

        @pl.when((seq == ZERO) & live)
        def _():
            wait(mlp_weights(layer))

        mlp_hook(ZERO)
        pl.when(live)(lambda: wait(saved_mlp(layer, seq)))
        mlp_backward(grad.at[seq], slope, act, mid_ref, ctx_ref, wo, big, c_ref, dctx.at[seq], delta.at[seq], g_wo, g_up, g_down,
                     dpre, h_ref, s_a, s_b, sums, pl.when(live), mlp_hook,
                     lambda: pl.when(seq < THREE)(lambda: start(saved_mlp(layer, seq + ONE))))

        @pl.when((seq == THREE) & live)
        def _():
            value = columns_of([(B_UP + i, sums[i]) for i in range(FOUR)] + [
                (LN_PAR + TWO, sums[FOUR]), (LN_PAR + THREE, sums[5]), (B_DOWN, sums[6]), (B_ATTN + THREE, sums[7])])
            rows_ref[pl.ds(pl.multiple_of(layer * SIXTEEN, SIXTEEN), SIXTEEN), :] = value.T[:SIXTEEN]

        mlp_hook(THREE)

    @pl.when(phase % TWO == ONE)
    def _():
        @pl.when(seq == ZERO)
        def _():
            start(probs(layer, ZERO))
            wait(attn_weights(layer))
            for ref in (g_qkv, sums):
                ref[...] = jnp.zeros_like(ref)

        @pl.when(step == FOUR)
        def _():
            start(saved_mlp(ZERO, ZERO))
        attn_hook(ZERO)
        wait(probs(layer, seq))
        attn_backward(dctx.at[seq], delta.at[seq], big, q_ref, k_ref, v_ref, x_ref, grad.at[seq], wqkv, c_ref, cos_ref, sin_ref,
                      g_qkv, dpre, h_ref, s_a, s_b, d_a, d_b, sums, attn_hook,
                      lambda: pl.when(seq < THREE)(lambda: start(probs(layer, seq + ONE))))

        @pl.when(seq == THREE)
        def _():
            value = columns_of([(B_ATTN + i, sums[i]) for i in range(THREE)] + [(LN_PAR, sums[THREE]), (LN_PAR + ONE, sums[FOUR])])
            rows = pl.ds(pl.multiple_of(layer * SIXTEEN, SIXTEEN), SIXTEEN)
            rows_ref[rows, :] = rows_ref[rows, :] + value.T[:SIXTEEN]

        @pl.when(step == 7)
        def _():
            start(mlp_weights(ZERO) + attn_weights(ZERO))

        @pl.when(step > 11)
        def _():
            dx_ref[ZERO] = grad[seq].T
        attn_hook(THREE)

    @pl.when(step == 17)
    def _():
        small_out[...] = rows_ref[...]


def add_to(ref, value):
    ref[...] = ref[...] + value.reshape(ref.shape)


def mlp_backward(grad, slope, act, mid_ref, ctx_ref, wo, big, c_ref, dctx, delta, g_wo, g_up, g_down, dpre, h_ref, s_a, s_b, sums, when, hook, prefetch):
    parts = [slice(DIM * k, DIM * k + DIM) for k in range(FOUR)]
    pre = (s_a, s_b)

    def dact(k):
        pre[k % TWO][...] = nn(big[k], grad[...])

    @when
    def _():
        norm_to(mid_ref.at[ZERO], c_ref, LN_PAR + TWO, h_ref)
        dact(ZERO)
        for k, rows in enumerate(parts):
            if k < THREE:
                dact(k + ONE)
            if k:
                add_to(g_down.at[k - ONE], nt(act[parts[k - ONE], :], grad[...]))
            for cols in lane_tiles():
                value = pre[k % TWO][:, cols] * slope[rows, cols]
                sums[k] += value
                dpre[rows, cols] = value.astype(BF16)
        add_to(g_down.at[THREE], nt(act[parts[THREE], :], grad[...]))
        prefetch()
    hook(ONE)

    @when
    def _():
        s_a[...] = functools.reduce(jnp.add, [nn(big[FOUR + k], dpre[rows, :]) for k, rows in enumerate(parts)])
    hook(TWO)

    @when
    def _():
        for k, rows in enumerate(parts):
            add_to(g_up.at[k], nt(h_ref[...], dpre[rows, :]))
        gain = column(c_ref, LN_PAR + TWO)
        for cols in lane_tiles():
            dh, dy = s_a[:, cols], grad[:, cols].astype(F32)
            dx, xhat = norm_back(dh, mid_ref[ZERO, :, cols].astype(F32), gain)
            dmid = (dy + dx).astype(BF16)
            grad[:, cols] = dmid
            sums[FOUR] += dh * xhat
            sums[5] += dh
            sums[6] += dy
            sums[7] += dmid.astype(F32)
        add_to(g_wo, nt(ctx_ref[ZERO].astype(BF16), grad[...]))
        s_b[...] = nn(wo[...], grad[...])
        for head in range(HEADS):
            rows = head_rows(head)[ZERO]
            value = s_b[rows, :].astype(BF16)
            dctx[rows, :] = value
            delta[head:head + ONE, :] = total(value.astype(F32) * ctx_ref[ZERO, rows, :])


def attn_backward(dctx, delta, probs, q_ref, k_ref, v_ref, x_ref, grad, wqkv, c_ref, cos_ref, sin_ref, g_qkv, dproj, h_ref, s_a, s_b, d_a, d_b,
                  sums, hook, prefetch):
    scores, dscores = (s_a, s_b), (d_a, d_b)
    q, k, v = q_ref.at[ZERO], k_ref.at[ZERO], v_ref.at[ZERO]

    def open_head(head):
        rows = head_rows(head)[ZERO]
        scores[head % TWO][...] = tn(v[rows, :], dctx[rows, :])

    def weigh(head):
        dscores[head % TWO][...] = (probs[head].astype(F32) * (scores[head % TWO][...] - delta[head:head + ONE, :])).astype(BF16)

    def values(head):
        rows = head_rows(head)[ZERO]
        dv = nt(dctx[rows, :], probs[head])
        sums[TWO, rows, :] += fold(dv)
        dproj[TWO * DIM + rows.start:TWO * DIM + rows.stop, :] = dv.astype(BF16)

    def close_head(head):
        rows, one, two = head_rows(head)
        ds = dscores[head % TWO][...]
        for m, value in enumerate((nn(k[rows, :], ds) * HEAD ** -0.5, nt(q[rows, :], ds))):
            cos, sin = cos_ref[...], sin_ref[...]
            a, b = value[:HALF], value[HALF:]
            for at, out in ((one, a * cos + b * sin), (two, b * cos - a * sin)):
                dproj[m * DIM + at.start:m * DIM + at.stop, :] = out.astype(BF16)
                sums[m, at, :] += fold(out)

    open_head(ZERO)
    for head in range(HEADS):
        if head + ONE < HEADS:
            open_head(head + ONE)
        if head:
            close_head(head - ONE)
        values(head)
        weigh(head)
        if head == THREE:
            hook(ONE)
    close_head(HEADS - ONE)
    prefetch()
    hook(TWO)
    norm_to(x_ref.at[ZERO], c_ref, LN_PAR, h_ref)
    parts = [slice(DIM * m, DIM * m + DIM) for m in range(THREE)]
    s_a[...] = functools.reduce(jnp.add, [nn(wqkv[m], dproj[rows, :]) for m, rows in enumerate(parts)])
    for m, rows in enumerate(parts):
        add_to(g_qkv.at[m], nt(h_ref[...], dproj[rows, :]))
    gain = column(c_ref, LN_PAR)
    for cols in lane_tiles():
        dh = s_a[:, cols]
        dx, xhat = norm_back(dh, x_ref[ZERO, :, cols].astype(F32), gain)
        grad[:, cols] = (grad[:, cols].astype(F32) + dx).astype(BF16)
        sums[THREE] += dh * xhat
        sums[FOUR] += dh


def backward(dy, xs, q, k, v, probs, ctx, mid, act, slope, c, tables, w_qkv, w_o, w_up, w_down):
    def mlp_at(s):
        s = jnp.minimum(s, 15)
        odd = s // FOUR % TWO == ONE
        return ONE - s // EIGHT, jnp.where(odd, THREE, s % FOUR), ZERO, ZERO

    def attn_at(s):
        s = jnp.minimum(s, 15)
        odd = s // FOUR % TWO == ONE
        return jnp.where(s < EIGHT, ONE, ZERO) + jnp.where((s > 7) & (s < 12), ONE, ZERO), jnp.where(odd, s % FOUR, jnp.where(s < FOUR, ZERO, THREE)), ZERO, ZERO

    per_mlp = pl.BlockSpec((None, ONE, *SQUARE), mlp_at)
    per_attn = pl.BlockSpec((None, ONE, *SQUARE), attn_at)
    acc = [(*GRID, EIGHT, WIDTH)]
    scratch = [pltpu.VMEM((SEQS, *SQUARE), BF16), pltpu.VMEM((SEQS, *SQUARE), BF16), pltpu.VMEM((SEQS, HEADS, TOK), F32),
               pltpu.VMEM((HEADS, TOK, TOK), BF16), pltpu.VMEM((THREE, DIM, DIM), BF16), pltpu.VMEM((DIM, DIM), BF16),
               pltpu.VMEM(TALL, F32), pltpu.VMEM(TALL, BF16), pltpu.VMEM(TALL, BF16), pltpu.VMEM(SQUARE, BF16),
               pltpu.VMEM(SQUARE, F32), pltpu.VMEM(SQUARE, F32), pltpu.VMEM((TOK, TOK), BF16), pltpu.VMEM((TOK, TOK), BF16),
               pltpu.VMEM((EIGHT, *COLS), F32), pltpu.VMEM((THREE, *GRID, EIGHT, DIM), F32), pltpu.VMEM((*GRID, EIGHT, DIM), F32),
               pltpu.VMEM((FOUR, *GRID, EIGHT, DIM), F32), pltpu.VMEM((*GRID, FOUR, EIGHT, DIM), F32), pltpu.VMEM((32, DIM), F32), pltpu.VMEM((10, 32, DIM), F32)]
    for n in (ONE, THREE):
        for order in ORDERS:
            ring_a, ring_b, plane, other = landing_shapes(order, n)
            plane = (TWO, *plane) if n == ONE else plane
            scratch += [pltpu.VMEM(s, F32) for s in ((n, *GRID, EIGHT, WIDTH), ring_a, ring_b, plane, other)]
    scratch += [DMA((THREE, THREE, 24)), DMA((THREE, THREE, 24)), DMA((10,)), DMA((10,)), DMA((EIGHT,)), DMA((TWO,)), DMA((TWO,))]
    outs = ((TWO, FOUR, FOUR, DIM), (TWO, FOUR, FFN), (TWO, SIXTEEN, DIM), (32, DIM))
    whole = [pl.BlockSpec(s, lambda i, n=len(s): (ZERO,) * n, pipeline_mode=pl.Buffered(ONE)) for s in outs]
    dx_at = lambda s: (jnp.clip(s - 12, ZERO, THREE), ZERO, ZERO)
    return pl.pallas_call(
        backward_kernel, grid=(18,),
        out_shape=[jax.ShapeDtypeStruct((SEQS, TOK, DIM), BF16)] + [jax.ShapeDtypeStruct(s, F32) for s in outs],
        out_specs=[pl.BlockSpec((ONE, TOK, DIM), dx_at)] + whole,
        in_specs=[pl.BlockSpec((ONE, TOK, DIM), lambda s: (jnp.minimum(s, THREE), ZERO, ZERO)), per_mlp, per_mlp, per_attn, per_attn, per_attn, per_attn,
                  once((HALF, TOK)), once((HALF, TOK)), pl.BlockSpec((None, *COLS), lambda s: (ONE - jnp.minimum(s, 15) // EIGHT, ZERO, ZERO))] + [HBM] * 7,
        scratch_shapes=scratch,
        compiler_params=pltpu.CompilerParams(collective_id=ONE, has_side_effects=True, vmem_limit_bytes=67043328,
                                             dimension_semantics=("arbitrary",)),
        name="backward")(dy, mid, ctx, q, k, v, xs, *tables, c, probs, slope, act, w_qkv, w_o, w_up, w_down)


def solution(mesh):
    batch_spec = P(AXIS)
    weight_specs = (P(None, None, AXIS, None), P(None, None, AXIS), P(None, None, AXIS),
                    P(None, AXIS, None), P(None, AXIS), P(None, AXIS, None), P(None, AXIS))

    def device_step(x, lengths, d_y, w_attn, b_attn, ln_par, w_up, b_up, w_down, b_down):
        tables = rotary_tables()
        xs, q, k, v, probs, ctx, mid, act, slope, c, w_qkv, w_o, w_up, w_down = forward(
            lengths, x, tables, (w_attn, b_attn, ln_par, w_up, b_up, w_down, b_down))
        grad, attn, up, down, small = backward(d_y, xs, q, k, v, probs, ctx, mid, act, slope, c, tables, w_qkv, w_o, w_up, w_down)
        me = lax.axis_index(AXIS)
        small = small.reshape(TWO, SIXTEEN, DIM)
        mine = lax.dynamic_slice(small, (ZERO, ZERO, FOUR * me), (TWO, SIXTEEN, FOUR))
        b_up_grad = lax.dynamic_slice(small[:, B_UP:B_DOWN].reshape(TWO, FFN), (ZERO, SIXTEEN * me), (TWO, SIXTEEN))
        return grad, attn, mine[:, :FOUR], mine[:, FOUR:EIGHT], up, b_up_grad, down, mine[:, 12]

    return jax.shard_map(device_step, mesh=mesh,
                         in_specs=(batch_spec, batch_spec, batch_spec) + weight_specs,
                         out_specs=(batch_spec,) + weight_specs,
                         check_vma=False)
```

time: 421 us -> 320 us (0.76)
  Pallas kernels: 402 us -> 309 us
  local copies, waits for them, and re-layouts: 15.7 us -> 9.17 us
    pallas_call x1, Pallas kernels: 198 us -> 133 us  [forward(): pl.pallas_call(forward_kernel, grid=(SIXTEEN,), out_shape=[o[ZERO] for o...]
    pallas_call x1, Pallas kernels: 205 us -> 176 us  [backward(): pl.pallas_call(backward_kernel, grid=(18,), out_shape=[jax.ShapeDtypeStru...]
where the time goes in v1:
time: 320 us
  Pallas kernels  309 us (97%)
  local copies, waits for them, and re-layouts  9.17 us (3%)
    pallas_call x1, Pallas kernels, backward(): pl.pallas_call(backward_kernel, grid=(18,), out_shape=[jax.ShapeDtypeStru...  176 us
    pallas_call x1, Pallas kernels, forward(): pl.pallas_call(forward_kernel, grid=(SIXTEEN,), out_shape=[o[ZERO] for o...  133 us

profile of v1, /device:TPU:1, one launch (start us, length us, event | category | flops | bytes accessed | tf_op | source)
XLA Modules:
  0.0 320.0 jit_solution(6709990948748990103)
XLA Ops:
  0.6 1.0 fusion
  1.6 132.7 %forward.1 = (bf16[2,4,512,512]{3,2,1,0:T(8,128)(2,1)}, bf16[2,4,512,512]{3,2,1,0:T(8,128)(2,1)}, bf16[2,4,512,512]{3,2,1,0:T(8,128)(2,1)}, bf16[2,4,512,512]{3,...) custom-call(s32[4]{0:T(128)} %len_ref.1, ...), custom_call_target="tpu_custom_call" | custom-call | tf_op jit(solution)/shard_map/forward/pallas_call | solution.py:660
  134.3 176.5 %backward.1 = (bf16[4,512,512]{2,1,0:T(8,128)(2,1)}, f32[2,4,4,512]{3,2,1,0:T(4,128)}, f32[2,4,2048]{2,1,0:T(4,128)}, f32[2,16,512]{2,1,0:T(8,128)}, f32[32,512]{1,0:T(8,128)}) custom-call(bf16[4,512,512]{2,1,0:T(8,128)(2,1)} %dy_ref.1, bf16[2,4,512,512]{3,2,1,0:T(8,128)(2,1)} %get-tuple-element.27.mid_ref, f32[2,4,512,512]{3,2,1,0:T(8,128)} %get-tuple-element.28.ctx_ref, ...), custom_call_target="tpu_custom_call" | custom-call | tf_op jit(solution)/shard_map/backward/pallas_call | solution.py:1001
  310.8 0.0 copy-start.2
  310.8 0.0 copy-start.1
  310.8 0.0 copy-start
  310.8 0.8 slice_bitcast_fusion
  311.7 0.6 constant_dynamic-slice_fusion.2
  312.3 1.4 constant_dynamic-slice_fusion
  313.7 1.3 constant_dynamic-slice_fusion.3
  315.1 3.0 copy.23
  318.1 0.0 copy-done.2
  318.1 0.6 copy.24
  318.8 0.0 copy-done.1
  318.8 0.6 copy.25
  319.4 0.0 copy-done
  319.4 0.6 copy.26
  (2 shorter events, 0.0 us)
Async XLA Ops:
  310.8 7.3 %copy-start.2 = (f32[2,4,4,512]{3,2,1,0:T(4,128)S(1)}, f32[2,4,4,512]{3,2,1,0:T(4,128)}, u32[]{:S(2)}) copy-start(f32[2,4,4,512]{3,2,1,0:T(4,128)} %get-tuple-element.59) | copy-start | bytes 196612
  310.8 7.9 %copy-start.1 = (f32[2,4,2048]{2,1,0:T(4,128)S(1)}, f32[2,4,2048]{2,1,0:T(4,128)}, u32[]{:S(2)}) copy-start(f32[2,4,2048]{2,1,0:T(4,128)} %get-tuple-element.62) | copy-start | bytes 196612
  310.8 8.6 %copy-start = (f32[2,16,512]{2,1,0:T(8,128)S(1)}, f32[2,16,512]{2,1,0:T(8,128)}, u32[]{:S(2)}) copy-start(f32[2,16,512]{2,1,0:T(8,128)} %get-tuple-element.64) | copy-start | bytes 196612

commit v2 on v1

--- a/solution.py
+++ b/solution.py
@@ -35,24 +35,51 @@
     return [slice(i, i + size) for i in range(ZERO, width, size)]
 
 
-def column(c_ref, lane, width=LANES):
-    return jnp.broadcast_to(c_ref[:, lane:lane + ONE], (c_ref.shape[ZERO], width))
+def row_chunks(rows=DIM, size=64):
+    return [slice(i, i + size) for i in range(ZERO, rows, size)]
+
+
+def column(c_ref, rows, lane):
+    return jnp.broadcast_to(c_ref[rows, lane:lane + ONE], (rows.stop - rows.start, TOK))
 
 
 def total(value):
     return jnp.sum(value, axis=ZERO, keepdims=True)
 
 
-def normed(x):
-    centred = x - total(x) * (1.0 / DIM)
-    rstd = lax.rsqrt(total(centred * centred) * (1.0 / DIM) + EPS)
-    return centred * rstd, rstd
-
-
-def norm_to(x_ref, c_ref, lane, h_ref):
-    gain, shift = column(c_ref, lane), column(c_ref, lane + ONE)
-    for cols in lane_tiles():
-        h_ref[:, cols] = (normed(x_ref[:, cols].astype(F32))[ZERO] * gain + shift).astype(BF16)
+def norm_stats(x_ref):
+    mean = functools.reduce(jnp.add, [total(x_ref[rows, :].astype(F32)) for rows in row_chunks()]) * (1.0 / DIM)
+    squares = []
+    for rows in row_chunks():
+        centred = x_ref[rows, :].astype(F32) - mean
+        squares.append(total(centred * centred))
+    return mean, lax.rsqrt(functools.reduce(jnp.add, squares) * (1.0 / DIM) + EPS)
+
+
+def norm_to(x_ref, stats, c_ref, lane, h_ref):
+    mean, rstd = stats
+    for rows in row_chunks():
+        xhat = (x_ref[rows, :].astype(F32) - mean) * rstd
+        h_ref[rows, :] = (xhat * column(c_ref, rows, lane) + column(c_ref, rows, lane + ONE)).astype(BF16)
+
+
+def put_stats(ref, stats):
+    ref[ZERO:ONE, :], ref[ONE:TWO, :] = stats
+
+
+def get_stats(ref):
+    return ref[ZERO:ONE, :], ref[ONE:TWO, :]
+
+
+def woven(products, rest):
+    done = ZERO
+    for n, step in enumerate(rest):
+        while done < len(products) and done * len(rest) <= n * len(products):
+            products[done]()
+            done += ONE
+        step()
+    for product in products[done:]:
+        product()
 
 
 def fold(value):
@@ -427,7 +454,7 @@
 
 
 def forward_kernel(len_ref, x_ref, cos_ref, sin_ref, w_attn, b_attn, ln_par, w_up, b_up, w_down, b_down,
-                   xs_out, q_ref, k_ref, v_ref, p_hbm, ctx_ref, mid_ref, act_ref, slope_ref, c_ref,
+                   xs_out, q_ref, k_ref, v_ref, p_hbm, ctx_ref, mid_ref, act_ref, slope_ref, st1_ref, st2_ref, c_ref,
                    nat_qkv, nat_wo, nat_up, nat_down,
                    xs, ctxb, wqkv, wo, up, down, n_qkv, n_wo, n_up, n_down, p_buf, h_ref, s_a, s_b, s_c,
                    sbuf, q0, q1, q2, m0, m1, m2, send, recv, p_sem, nat_sem):
@@ -517,9 +544,8 @@
         attn_hook(ZERO)
         copies = [pltpu.make_async_copy(p_buf.at[head], p_hbm.at[layer, seq, head], p_sem.at[head]) for head in range(HEADS)]
         attn_forward(len_ref[seq], xs.at[seq], wqkv, c_ref.at[layer], cos_ref, sin_ref, q_ref.at[ZERO, ZERO], k_ref.at[ZERO, ZERO],
-                     v_ref.at[ZERO, ZERO], p_buf, ctx_ref.at[ZERO, ZERO], ctxb.at[seq], h_ref, s_a, s_b, s_c, attn_hook,
-                     lambda: pl.when(step > ZERO)(lambda: wait(copies)))
-        start(copies)
+                     v_ref.at[ZERO, ZERO], p_buf, ctx_ref.at[ZERO, ZERO], ctxb.at[seq], st1_ref.at[ZERO, ZERO], h_ref, s_a, s_b, s_c, attn_hook,
+                     lambda heads: pl.when(step > ZERO)(lambda: wait(copies[heads])), lambda heads: start(copies[heads]))
         pl.when(step == 11)(lambda: wait(copies))
         attn_hook(THREE)
 
@@ -528,7 +554,7 @@
         pl.when(seq == ZERO)(take_mo)
         mlp_hook(ZERO)
         mlp_forward(layer, ctxb.at[seq], xs.at[seq], wo, up, down, c_ref.at[layer], mid_ref.at[ZERO, ZERO], act_ref.at[ZERO, ZERO], slope_ref.at[ZERO, ZERO],
-                    h_ref, s_a, s_b, mlp_hook)
+                    st2_ref.at[ZERO, ZERO], h_ref, s_a, s_b, mlp_hook)
 
         @pl.when(layer == ZERO)
         def _():
@@ -541,26 +567,27 @@
             wait(nat_copies(which, ONE))
 
 
-def attn_forward(length, xt, w, c_ref, cos_ref, sin_ref, q_ref, k_ref, v_ref, p_buf, ctx_ref, ctxb, h_ref, s_a, s_b, s_c, hook, free):
-    norm_to(xt, c_ref, LN_PAR, h_ref)
+def attn_forward(length, xt, w, c_ref, cos_ref, sin_ref, q_ref, k_ref, v_ref, p_buf, ctx_ref, ctxb, stat_ref, h_ref, s_a, s_b, s_c, hook, free, ship):
+    stats = norm_stats(xt)
+    put_stats(stat_ref, stats)
+    norm_to(xt, stats, c_ref, LN_PAR, h_ref)
     for m, acc in enumerate((s_a, s_b, s_c)):
         acc[...] = nn(w[m], h_ref[...])
+    cos, sin = cos_ref[...], sin_ref[...]
     for m, (acc, out) in enumerate(((s_a, q_ref), (s_b, k_ref), (s_c, v_ref))):
-        bias = column(c_ref, B_ATTN + m)
-        for cols in lane_tiles():
+        for head in range(HEADS):
+            rows, one, two = head_rows(head)
             if m == TWO:
-                out[:, cols] = (acc[:, cols] + bias).astype(BF16)
+                out[rows, :] = (acc[rows, :] + column(c_ref, rows, B_ATTN + m)).astype(BF16)
                 continue
-            cos, sin = cos_ref[:, cols], sin_ref[:, cols]
-            for head in range(HEADS):
-                _, one, two = head_rows(head)
-                a, b = acc[one, cols] + bias[one], acc[two, cols] + bias[two]
-                if m == ZERO:
-                    a, b = a * HEAD ** -0.5, b * HEAD ** -0.5
-                out[one, cols] = (a * cos - b * sin).astype(BF16)
-                out[two, cols] = (b * cos + a * sin).astype(BF16)
+            a, b = [acc[half, :] + column(c_ref, half, B_ATTN + m) for half in (one, two)]
+            if m == ZERO:
+                a, b = a * HEAD ** -0.5, b * HEAD ** -0.5
+            out[one, :] = (a * cos - b * sin).astype(BF16)
+            out[two, :] = (b * cos + a * sin).astype(BF16)
     hook(ONE)
-    free()
+    halves = slice(ZERO, FOUR), slice(FOUR, EIGHT)
+    free(halves[ZERO])
     key = lax.broadcasted_iota(jnp.int32, (SIXTEEN, TOK), ONE)
     row = lax.broadcasted_iota(jnp.int32, (SIXTEEN, TOK), ZERO)
     bias_rows = jnp.where((row == ZERO) & (key >= length), NEG_BIG, 0.0).astype(BF16)
@@ -574,9 +601,24 @@
         scores[head % TWO][...] = tn(keys, queries)
 
     def weigh(head):
-        value = scores[head % TWO][...]
-        weight = jnp.exp(value - jnp.max(value, axis=ZERO, keepdims=True))
-        p_buf[head] = (weight * (1.0 / total(weight))).astype(BF16)
+        value, tops, sums = scores[head % TWO], [], []
+
+        def top(rows):
+            tops.append(jnp.max(value[rows, :], axis=ZERO, keepdims=True))
+            if rows.stop == TOK:
+                tops[:] = [functools.reduce(jnp.maximum, tops)]
+
+        def power(rows):
+            weight = jnp.exp(value[rows, :] - tops[ZERO])
+            value[rows, :] = weight
+            sums.append(total(weight))
+            if rows.stop == TOK:
+                sums[:] = [1.0 / functools.reduce(jnp.add, sums)]
+
+        def share(rows):
+            p_buf[head, rows, :] = (value[rows, :] * sums[ZERO]).astype(BF16)
+
+        return [functools.partial(run, rows) for run in (top, power, share) for rows in row_chunks()]
 
     def close_head(head):
         rows = head_rows(head)[ZERO]
@@ -586,21 +628,25 @@
 
     open_head(ZERO)
     for head in range(HEADS):
-        if head + ONE < HEADS:
-            open_head(head + ONE)
+        products = [functools.partial(open_head, head + ONE)] if head + ONE < HEADS else []
         if head:
-            close_head(head - ONE)
-        weigh(head)
+            products.append(functools.partial(close_head, head - ONE))
+        woven(products, weigh(head))
         if head == THREE:
+            ship(halves[ZERO])
             hook(TWO)
+            free(halves[ONE])
+    ship(halves[ONE])
     close_head(HEADS - ONE)
 
 
-def mlp_forward(layer, ctxb, xt, wo, up, down, c_ref, mid_ref, act_ref, slope_ref, h_ref, s_a, s_b, hook):
+def mlp_forward(layer, ctxb, xt, wo, up, down, c_ref, mid_ref, act_ref, slope_ref, stat_ref, h_ref, s_a, s_b, hook):
     s_a[...] = nn(wo[...], ctxb[...])
-    for cols in lane_tiles():
-        mid_ref[:, cols] = (xt[:, cols].astype(F32) + s_a[:, cols] + column(c_ref, B_ATTN + THREE)).astype(BF16)
-    norm_to(mid_ref, c_ref, LN_PAR + TWO, h_ref)
+    for rows in row_chunks():
+        mid_ref[rows, :] = (xt[rows, :].astype(F32) + s_a[rows, :] + column(c_ref, rows, B_ATTN + THREE)).astype(BF16)
+    stats = norm_stats(mid_ref)
+    put_stats(stat_ref, stats)
+    norm_to(mid_ref, stats, c_ref, LN_PAR + TWO, h_ref)
     hook(ONE)
     pre = (s_a, s_b)
     parts = [slice(DIM * k, DIM * k + DIM) for k in range(FOUR)]
@@ -609,24 +655,25 @@
         pre[k % TWO][...] = nn(up[parts[k], :], h_ref[...])
 
     open_part(ZERO)
-    for k, rows in enumerate(parts):
+    for k, part in enumerate(parts):
         if k < THREE:
             open_part(k + ONE)
-        for cols in lane_tiles():
-            value = pre[k % TWO][:, cols] + column(c_ref, B_UP + k)
+        for rows in row_chunks():
+            value = pre[k % TWO][rows, :] + column(c_ref, rows, B_UP + k)
             scaled = value * math.sqrt(0.5)
             cdf = 0.5 + 0.5 * lax.erf(scaled)
             density = jnp.exp2(scaled * scaled * -math.log2(math.e) - 0.5 * math.log2(2.0 * math.pi))
-            act_ref[rows, cols] = (value * cdf).astype(BF16)
-            slope_ref[rows, cols] = cdf + value * density
+            there = slice(part.start + rows.start, part.start + rows.stop)
+            act_ref[there, :] = (value * cdf).astype(BF16)
+            slope_ref[there, :] = cdf + value * density
         if k == ONE:
             hook(TWO)
 
     @pl.when(layer == ZERO)
     def _():
-        out = nn(down[...], act_ref[...])
-        for cols in lane_tiles():
-            xt[:, cols] = (mid_ref[:, cols].astype(F32) + out[:, cols] + column(c_ref, B_DOWN)).astype(BF16)
+        s_a[...] = nn(down[...], act_ref[...])
+        for rows in row_chunks():
+            xt[rows, :] = (mid_ref[rows, :].astype(F32) + s_a[rows, :] + column(c_ref, rows, B_DOWN)).astype(BF16)
 
 
 MO_SLOTS = (ZERO, 5, 13, 15)
@@ -649,7 +696,7 @@
 
     outs = [saved(xs_at, DIM, BF16)] + [saved(attn_at, DIM, BF16)] * THREE
     outs += [(jax.ShapeDtypeStruct((TWO, SEQS, HEADS, TOK, TOK), BF16), HBM), saved(attn_at, DIM, F32)]
-    outs += [saved(mlp_at, DIM, BF16), saved(mlp_at, FFN, BF16), saved(mlp_at, FFN, F32)]
+    outs += [saved(mlp_at, DIM, BF16), saved(mlp_at, FFN, BF16), saved(mlp_at, FFN, F32), saved(attn_at, EIGHT, F32), saved(mlp_at, EIGHT, F32)]
     outs += [(jax.ShapeDtypeStruct((TWO, *COLS), F32), once((TWO, *COLS)))]
     weights = ((THREE, DIM, DIM), (DIM, DIM), (DIM, FFN), (FFN, DIM))
     outs += [(jax.ShapeDtypeStruct((TWO, *w), BF16), HBM) for w in weights]
@@ -668,12 +715,25 @@
         name="forward")(lengths, x, *tables, *params)
 
 
-def norm_back(dh, x, gain):
-    xhat, rstd = normed(x)
-    dxhat = dh * gain
-    mean_one = total(dxhat) * (1.0 / DIM)
-    mean_two = total(dxhat * xhat) * (1.0 / DIM)
-    return rstd * (dxhat - mean_one - xhat * mean_two), xhat
+def norm_back(dh_ref, x_ref, stats, c_ref, lane, sums, at, write, beside):
+    mean, rstd = stats
+    means = [0.0, 0.0]
+
+    def both(rows):
+        dh = dh_ref[rows, :]
+        return dh, dh * column(c_ref, rows, lane), (x_ref[rows, :].astype(F32) - mean) * rstd
+
+    def first(rows):
+        dh, dxhat, xhat = both(rows)
+        means[ZERO], means[ONE] = means[ZERO] + total(dxhat), means[ONE] + total(dxhat * xhat)
+        sums[at, rows, :] += fold(dh * xhat)
+        sums[at + ONE, rows, :] += fold(dh)
+
+    def second(rows):
+        dh, dxhat, xhat = both(rows)
+        write(rows, rstd * (dxhat - means[ZERO] * (1.0 / DIM) - xhat * (means[ONE] * (1.0 / DIM))))
+
+    woven(beside, [functools.partial(run, rows) for run in (first, second) for rows in row_chunks()])
 
 
 def columns_of(pairs):
@@ -708,7 +768,7 @@
         return [each("swap"), each("swapped", "ring_start"), each("ring_turn"), each("plane_start"), each("last"), finish]
 
 
-def backward_kernel(dy_ref, mid_ref, ctx_ref, q_ref, k_ref, v_ref, x_ref, cos_ref, sin_ref, c_ref, p_hbm, slope_hbm, act_hbm,
+def backward_kernel(dy_ref, mid_ref, ctx_ref, st2_ref, q_ref, k_ref, v_ref, x_ref, st1_ref, cos_ref, sin_ref, c_ref, p_hbm, slope_hbm, act_hbm,
                     qkv_hbm, wo_hbm, up_hbm, down_hbm,
                     dx_ref, attn_out, up_out, down_out, small_out, *refs):
     (grad, dctx, delta, big, wqkv, wo, slope, act, dpre, h_ref, s_a, s_b, d_a, d_b, sums,
@@ -753,12 +813,10 @@
         return put
 
     def mlp_weights(l):
-        copies = [pltpu.make_async_copy(wo_hbm.at[l], wo, w_sem.at[ZERO])]
-        for k in range(FOUR):
-            part = pl.ds(DIM * k, DIM)
-            copies.append(pltpu.make_async_copy(down_hbm.at[l, part], big.at[k], big_sem.at[k]))
-            copies.append(pltpu.make_async_copy(up_hbm.at[l, :, part], big.at[FOUR + k], big_sem.at[FOUR + k]))
-        return copies
+        parts = [pl.ds(DIM * k, DIM) for k in range(FOUR)]
+        return ([pltpu.make_async_copy(down_hbm.at[l, part], big.at[k], big_sem.at[k]) for k, part in enumerate(parts)],
+                [pltpu.make_async_copy(up_hbm.at[l, :, part], big.at[FOUR + k], big_sem.at[FOUR + k]) for k, part in enumerate(parts)] +
+                [pltpu.make_async_copy(wo_hbm.at[l], wo, w_sem.at[ZERO])])
 
     def attn_weights(l):
         return [pltpu.make_async_copy(qkv_hbm.at[l], wqkv, w_sem.at[ONE])]
@@ -780,7 +838,7 @@
     @pl.when(step == ZERO)
     def _():
         place.greet()
-        start(mlp_weights(ONE) + saved_mlp(ONE, ZERO) + attn_weights(ONE))
+        start(mlp_weights(ONE)[ZERO] + saved_mlp(ONE, ZERO) + mlp_weights(ONE)[ONE] + attn_weights(ONE))
 
     pl.when(step == ONE)(place.met)
     mo_steps, qkv_steps = mo_sums.steps(store(layer)), qkv_sums.steps(store(ONE - turn))
@@ -804,13 +862,24 @@
 
         @pl.when((seq == ZERO) & live)
         def _():
-            wait(mlp_weights(layer))
+            wait(mlp_weights(layer)[ZERO])
 
         mlp_hook(ZERO)
+
+        def after_first():
+            pl.when(seq < THREE)(lambda: start(saved_mlp(layer, seq + ONE)))
+            pl.when(seq == THREE)(lambda: start(probs(layer, ZERO)[:FOUR]))
+
+        def before_second():
+            pl.when(seq == ZERO)(lambda: wait(mlp_weights(layer)[ONE]))
+
+        def after_second():
+            pl.when(seq == THREE)(lambda: start(probs(layer, ZERO)[FOUR:]))
+
         pl.when(live)(lambda: wait(saved_mlp(layer, seq)))
-        mlp_backward(grad.at[seq], slope, act, mid_ref, ctx_ref, wo, big, c_ref, dctx.at[seq], delta.at[seq], g_wo, g_up, g_down,
+        mlp_backward(grad.at[seq], slope, act, mid_ref, ctx_ref, st2_ref.at[ZERO], wo, big, c_ref, dctx.at[seq], delta.at[seq], g_wo, g_up, g_down,
                      dpre, h_ref, s_a, s_b, sums, pl.when(live), mlp_hook,
-                     lambda: pl.when(seq < THREE)(lambda: start(saved_mlp(layer, seq + ONE))))
+                     after_first, after_second, before_second)
 
         @pl.when((seq == THREE) & live)
         def _():
@@ -824,7 +893,6 @@
     def _():
         @pl.when(seq == ZERO)
         def _():
-            start(probs(layer, ZERO))
             wait(attn_weights(layer))
             for ref in (g_qkv, sums):
                 ref[...] = jnp.zeros_like(ref)
@@ -833,10 +901,15 @@
         def _():
             start(saved_mlp(ZERO, ZERO))
         attn_hook(ZERO)
+
+        def after_heads():
+            pl.when(seq < THREE)(lambda: start(probs(layer, seq + ONE)))
+            pl.when(step == 7)(lambda: start(mlp_weights(ZERO)[ZERO] + mlp_weights(ZERO)[ONE]))
+
         wait(probs(layer, seq))
-        attn_backward(dctx.at[seq], delta.at[seq], big, q_ref, k_ref, v_ref, x_ref, grad.at[seq], wqkv, c_ref, cos_ref, sin_ref,
+        attn_backward(dctx.at[seq], delta.at[seq], big, q_ref, k_ref, v_ref, x_ref, st1_ref.at[ZERO], grad.at[seq], wqkv, c_ref, cos_ref, sin_ref,
                       g_qkv, dpre, h_ref, s_a, s_b, d_a, d_b, sums, attn_hook,
-                      lambda: pl.when(seq < THREE)(lambda: start(probs(layer, seq + ONE))))
+                      after_heads)
 
         @pl.when(seq == THREE)
         def _():
@@ -846,7 +919,7 @@
 
         @pl.when(step == 7)
         def _():
-            start(mlp_weights(ZERO) + attn_weights(ZERO))
+            start(attn_weights(ZERO))
 
         @pl.when(step > 11)
         def _():
@@ -862,7 +935,7 @@
     ref[...] = ref[...] + value.reshape(ref.shape)
 
 
-def mlp_backward(grad, slope, act, mid_ref, ctx_ref, wo, big, c_ref, dctx, delta, g_wo, g_up, g_down, dpre, h_ref, s_a, s_b, sums, when, hook, prefetch):
+def mlp_backward(grad, slope, act, mid_ref, ctx_ref, stat_ref, wo, big, c_ref, dctx, delta, g_wo, g_up, g_down, dpre, h_ref, s_a, s_b, sums, when, hook, after_first, after_second, before_second):
     parts = [slice(DIM * k, DIM * k + DIM) for k in range(FOUR)]
     pre = (s_a, s_b)
 
@@ -871,40 +944,43 @@
 
     @when
     def _():
-        norm_to(mid_ref.at[ZERO], c_ref, LN_PAR + TWO, h_ref)
+        def scale(k, chunk):
+            there = slice(parts[k].start + chunk.start, parts[k].start + chunk.stop)
+            value = pre[k % TWO][chunk, :] * slope[there, :]
+            sums[k, chunk, :] += fold(value)
+            dpre[there, :] = value.astype(BF16)
+
+        def down_product(k):
+            add_to(g_down.at[k], nt(act[parts[k], :], grad[...]))
+
         dact(ZERO)
-        for k, rows in enumerate(parts):
+        norm_to(mid_ref.at[ZERO], get_stats(stat_ref), c_ref, LN_PAR + TWO, h_ref)
+        for k in range(FOUR):
+            products = [functools.partial(down_product, k)]
             if k < THREE:
-                dact(k + ONE)
-            if k:
-                add_to(g_down.at[k - ONE], nt(act[parts[k - ONE], :], grad[...]))
-            for cols in lane_tiles():
-                value = pre[k % TWO][:, cols] * slope[rows, cols]
-                sums[k] += value
-                dpre[rows, cols] = value.astype(BF16)
-        add_to(g_down.at[THREE], nt(act[parts[THREE], :], grad[...]))
-        prefetch()
+                products = [functools.partial(dact, k + ONE)] + products
+            woven(products, [functools.partial(scale, k, chunk) for chunk in row_chunks()])
+        after_first()
     hook(ONE)
 
     @when
     def _():
+        before_second()
         s_a[...] = functools.reduce(jnp.add, [nn(big[FOUR + k], dpre[rows, :]) for k, rows in enumerate(parts)])
+        after_second()
     hook(TWO)
 
     @when
     def _():
-        for k, rows in enumerate(parts):
-            add_to(g_up.at[k], nt(h_ref[...], dpre[rows, :]))
-        gain = column(c_ref, LN_PAR + TWO)
-        for cols in lane_tiles():
-            dh, dy = s_a[:, cols], grad[:, cols].astype(F32)
-            dx, xhat = norm_back(dh, mid_ref[ZERO, :, cols].astype(F32), gain)
+        def write(rows, dx):
+            dy = grad[rows, :].astype(F32)
             dmid = (dy + dx).astype(BF16)
-            grad[:, cols] = dmid
-            sums[FOUR] += dh * xhat
-            sums[5] += dh
-            sums[6] += dy
-            sums[7] += dmid.astype(F32)
+            grad[rows, :] = dmid
+            sums[6, rows, :] += fold(dy)
+            sums[7, rows, :] += fold(dmid.astype(F32))
+
+        norm_back(s_a, mid_ref.at[ZERO], get_stats(stat_ref), c_ref, LN_PAR + TWO, sums, FOUR, write,
+                  [lambda k=k, rows=rows: add_to(g_up.at[k], nt(h_ref[...], dpre[rows, :])) for k, rows in enumerate(parts)])
         add_to(g_wo, nt(ctx_ref[ZERO].astype(BF16), grad[...]))
         s_b[...] = nn(wo[...], grad[...])
         for head in range(HEADS):
@@ -914,7 +990,7 @@
             delta[head:head + ONE, :] = total(value.astype(F32) * ctx_ref[ZERO, rows, :])
 
 
-def attn_backward(dctx, delta, probs, q_ref, k_ref, v_ref, x_ref, grad, wqkv, c_ref, cos_ref, sin_ref, g_qkv, dproj, h_ref, s_a, s_b, d_a, d_b,
+def attn_backward(dctx, delta, probs, q_ref, k_ref, v_ref, x_ref, stat_ref, grad, wqkv, c_ref, cos_ref, sin_ref, g_qkv, dproj, h_ref, s_a, s_b, d_a, d_b,
                   sums, hook, prefetch):
     scores, dscores = (s_a, s_b), (d_a, d_b)
     q, k, v = q_ref.at[ZERO], k_ref.at[ZERO], v_ref.at[ZERO]
@@ -923,8 +999,8 @@
         rows = head_rows(head)[ZERO]
         scores[head % TWO][...] = tn(v[rows, :], dctx[rows, :])
 
-    def weigh(head):
-        dscores[head % TWO][...] = (probs[head].astype(F32) * (scores[head % TWO][...] - delta[head:head + ONE, :])).astype(BF16)
+    def weigh(head, rows):
+        dscores[head % TWO][rows, :] = (probs[head, rows, :].astype(F32) * (scores[head % TWO][rows, :] - delta[head:head + ONE, :])).astype(BF16)
 
     def values(head):
         rows = head_rows(head)[ZERO]
@@ -932,44 +1008,42 @@
         sums[TWO, rows, :] += fold(dv)
         dproj[TWO * DIM + rows.start:TWO * DIM + rows.stop, :] = dv.astype(BF16)
 
-    def close_head(head):
+    def close_head(head, m):
         rows, one, two = head_rows(head)
         ds = dscores[head % TWO][...]
-        for m, value in enumerate((nn(k[rows, :], ds) * HEAD ** -0.5, nt(q[rows, :], ds))):
-            cos, sin = cos_ref[...], sin_ref[...]
-            a, b = value[:HALF], value[HALF:]
-            for at, out in ((one, a * cos + b * sin), (two, b * cos - a * sin)):
-                dproj[m * DIM + at.start:m * DIM + at.stop, :] = out.astype(BF16)
-                sums[m, at, :] += fold(out)
+        value = nn(k[rows, :], ds) * HEAD ** -0.5 if m == ZERO else nt(q[rows, :], ds)
+        cos, sin = cos_ref[...], sin_ref[...]
+        a, b = value[:HALF], value[HALF:]
+        for at, out in ((one, a * cos + b * sin), (two, b * cos - a * sin)):
+            dproj[m * DIM + at.start:m * DIM + at.stop, :] = out.astype(BF16)
+            sums[m, at, :] += fold(out)
 
     open_head(ZERO)
     for head in range(HEADS):
+        products = [functools.partial(values, head)]
+        if head:
+            products = [functools.partial(close_head, head - ONE, m) for m in range(TWO)] + products
         if head + ONE < HEADS:
-            open_head(head + ONE)
-        if head:
-            close_head(head - ONE)
-        values(head)
-        weigh(head)
+            products = [functools.partial(open_head, head + ONE)] + products
+        woven(products, [functools.partial(weigh, head, rows) for rows in row_chunks()])
         if head == THREE:
             hook(ONE)
-    close_head(HEADS - ONE)
+    for m in range(TWO):
+        close_head(HEADS - ONE, m)
     prefetch()
     hook(TWO)
-    norm_to(x_ref.at[ZERO], c_ref, LN_PAR, h_ref)
+    norm_to(x_ref.at[ZERO], get_stats(stat_ref), c_ref, LN_PAR, h_ref)
     parts = [slice(DIM * m, DIM * m + DIM) for m in range(THREE)]
     s_a[...] = functools.reduce(jnp.add, [nn(wqkv[m], dproj[rows, :]) for m, rows in enumerate(parts)])
-    for m, rows in enumerate(parts):
-        add_to(g_qkv.at[m], nt(h_ref[...], dproj[rows, :]))
-    gain = column(c_ref, LN_PAR)
-    for cols in lane_tiles():
-        dh = s_a[:, cols]
-        dx, xhat = norm_back(dh, x_ref[ZERO, :, cols].astype(F32), gain)
-        grad[:, cols] = (grad[:, cols].astype(F32) + dx).astype(BF16)
-        sums[THREE] += dh * xhat
-        sums[FOUR] += dh
-
-
-def backward(dy, xs, q, k, v, probs, ctx, mid, act, slope, c, tables, w_qkv, w_o, w_up, w_down):
+
+    def write(rows, dx):
+        grad[rows, :] = (grad[rows, :].astype(F32) + dx).astype(BF16)
+
+    norm_back(s_a, x_ref.at[ZERO], get_stats(stat_ref), c_ref, LN_PAR, sums, THREE, write,
+              [lambda m=m, rows=rows: add_to(g_qkv.at[m], nt(h_ref[...], dproj[rows, :])) for m, rows in enumerate(parts)])
+
+
+def backward(dy, xs, q, k, v, probs, ctx, mid, act, slope, st1, st2, c, tables, w_qkv, w_o, w_up, w_down):
     def mlp_at(s):
         s = jnp.minimum(s, 15)
         odd = s // FOUR % TWO == ONE
@@ -982,6 +1056,10 @@
 
     per_mlp = pl.BlockSpec((None, ONE, *SQUARE), mlp_at)
     per_attn = pl.BlockSpec((None, ONE, *SQUARE), attn_at)
+
+    def stat(at):
+        return pl.BlockSpec((None, ONE, EIGHT, TOK), at)
+
     acc = [(*GRID, EIGHT, WIDTH)]
     scratch = [pltpu.VMEM((SEQS, *SQUARE), BF16), pltpu.VMEM((SEQS, *SQUARE), BF16), pltpu.VMEM((SEQS, HEADS, TOK), F32),
                pltpu.VMEM((HEADS, TOK, TOK), BF16), pltpu.VMEM((THREE, DIM, DIM), BF16), pltpu.VMEM((DIM, DIM), BF16),
@@ -1002,12 +1080,12 @@
         backward_kernel, grid=(18,),
         out_shape=[jax.ShapeDtypeStruct((SEQS, TOK, DIM), BF16)] + [jax.ShapeDtypeStruct(s, F32) for s in outs],
         out_specs=[pl.BlockSpec((ONE, TOK, DIM), dx_at)] + whole,
-        in_specs=[pl.BlockSpec((ONE, TOK, DIM), lambda s: (jnp.minimum(s, THREE), ZERO, ZERO)), per_mlp, per_mlp, per_attn, per_attn, per_attn, per_attn,
+        in_specs=[pl.BlockSpec((ONE, TOK, DIM), lambda s: (jnp.minimum(s, THREE), ZERO, ZERO)), per_mlp, per_mlp, stat(mlp_at)] + [per_attn] * FOUR + [stat(attn_at),
                   once((HALF, TOK)), once((HALF, TOK)), pl.BlockSpec((None, *COLS), lambda s: (ONE - jnp.minimum(s, 15) // EIGHT, ZERO, ZERO))] + [HBM] * 7,
         scratch_shapes=scratch,
         compiler_params=pltpu.CompilerParams(collective_id=ONE, has_side_effects=True, vmem_limit_bytes=67043328,
                                              dimension_semantics=("arbitrary",)),
-        name="backward")(dy, mid, ctx, q, k, v, xs, *tables, c, probs, slope, act, w_qkv, w_o, w_up, w_down)
+        name="backward")(dy, mid, ctx, st2, q, k, v, xs, st1, *tables, c, probs, slope, act, w_qkv, w_o, w_up, w_down)
 
 
 def solution(mesh):
@@ -1017,9 +1095,9 @@
 
     def device_step(x, lengths, d_y, w_attn, b_attn, ln_par, w_up, b_up, w_down, b_down):
         tables = rotary_tables()
-        xs, q, k, v, probs, ctx, mid, act, slope, c, w_qkv, w_o, w_up, w_down = forward(
+        xs, q, k, v, probs, ctx, mid, act, slope, st1, st2, c, w_qkv, w_o, w_up, w_down = forward(
             lengths, x, tables, (w_attn, b_attn, ln_par, w_up, b_up, w_down, b_down))
-        grad, attn, up, down, small = backward(d_y, xs, q, k, v, probs, ctx, mid, act, slope, c, tables, w_qkv, w_o, w_up, w_down)
+        grad, attn, up, down, small = backward(d_y, xs, q, k, v, probs, ctx, mid, act, slope, st1, st2, c, tables, w_qkv, w_o, w_up, w_down)
         me = lax.axis_index(AXIS)
         small = small.reshape(TWO, SIXTEEN, DIM)
         mine = lax.dynamic_slice(small, (ZERO, ZERO, FOUR * me), (TWO, SIXTEEN, FOUR))

time: 320 us -> 307 us (0.959)
  Pallas kernels: 309 us -> 296 us
    pallas_call x1, Pallas kernels: 176 us -> 163 us  [backward(): pl.pallas_call(backward_kernel, grid=(18,), out_shape=[jax.ShapeDtypeStru...]
where the time goes in v2:
time: 307 us
  Pallas kernels  296 us (96%)
  local copies, waits for them, and re-layouts  9.17 us (3%)
    pallas_call x1, Pallas kernels, backward(): pl.pallas_call(backward_kernel, grid=(18,), out_shape=[jax.ShapeDtypeStru...  163 us
    pallas_call x1, Pallas kernels, forward(): pl.pallas_call(forward_kernel, grid=(SIXTEEN,), out_shape=[o[ZERO] for o...  132 us

profile of v2, /device:TPU:1, one launch (start us, length us, event | category | flops | bytes accessed | tf_op | source)
XLA Modules:
  0.0 306.5 jit_solution(292025251601179219)
XLA Ops:
  0.6 1.0 fusion
  1.6 132.3 %forward.1 = (bf16[2,4,512,512]{3,2,1,0:T(8,128)(2,1)}, bf16[2,4,512,512]{3,2,1,0:T(8,128)(2,1)}, bf16[2,4,512,512]{3,2,1,0:T(8,128)(2,1)}, bf16[2,4,512,512]{3,...) custom-call(s32[4]{0:T(128)} %len_ref.1, ...), custom_call_target="tpu_custom_call" | custom-call | tf_op jit(solution)/shard_map/forward/pallas_call | solution.py:707
  133.9 163.4 %backward.1 = (bf16[4,512,512]{2,1,0:T(8,128)(2,1)}, f32[2,4,4,512]{3,2,1,0:T(4,128)}, f32[2,4,2048]{2,1,0:T(4,128)}, f32[2,16,512]{2,1,0:T(8,128)}, f32[32,512]{1,0:T(8,128)}) custom-call(bf16[4,512,512]{2,1,0:T(8,128)(2,1)} %dy_ref.1, bf16[2,4,512,512]{3,2,1,0:T(8,128)(2,1)} %get-tuple-element.29.mid_ref, f32[2,4,512,512]{3,2,1,0:T(8,128)} %get-tuple-element.30.ctx_ref, ...), custom_call_target="tpu_custom_call" | custom-call | tf_op jit(solution)/shard_map/backward/pallas_call | solution.py:1079
  297.3 0.0 copy-start.2
  297.3 0.0 copy-start.1
  297.3 0.0 copy-start
  297.3 0.8 slice_bitcast_fusion
  298.2 0.6 constant_dynamic-slice_fusion.2
  298.8 1.4 constant_dynamic-slice_fusion
  300.2 1.3 constant_dynamic-slice_fusion.3
  301.6 3.0 copy.23
  304.6 0.0 copy-done.2
  304.6 0.6 copy.24
  305.2 0.0 copy-done.1
  305.3 0.6 copy.25
  305.9 0.0 copy-done
  305.9 0.6 copy.26
  (2 shorter events, 0.0 us)
Async XLA Ops:
  297.3 7.3 %copy-start.2 = (f32[2,4,4,512]{3,2,1,0:T(4,128)S(1)}, f32[2,4,4,512]{3,2,1,0:T(4,128)}, u32[]{:S(2)}) copy-start(f32[2,4,4,512]{3,2,1,0:T(4,128)} %get-tuple-element.63) | copy-start | bytes 196612
  297.3 7.9 %copy-start.1 = (f32[2,4,2048]{2,1,0:T(4,128)S(1)}, f32[2,4,2048]{2,1,0:T(4,128)}, u32[]{:S(2)}) copy-start(f32[2,4,2048]{2,1,0:T(4,128)} %get-tuple-element.66) | copy-start | bytes 196612
  297.3 8.6 %copy-start = (f32[2,16,512]{2,1,0:T(8,128)S(1)}, f32[2,16,512]{2,1,0:T(8,128)}, u32[]{:S(2)}) copy-start(f32[2,16,512]{2,1,0:T(8,128)} %get-tuple-element.68) | copy-start | bytes 196612

commit v3 on v2

--- a/solution.py
+++ b/solution.py
@@ -341,11 +341,14 @@
     def __init__(self, place, value, slots, send, recv):
         self.place, self.value, self.slots, self.send, self.recv = place, value, slots, send, recv
 
+    def peers(self, stage):
+        if stage == THREE:
+            return [self.place.partner]
+        return [self.place.device({stage: delta}) for delta in LINE]
+
     def copies(self, stage):
-        if stage == THREE:
-            return [remote(self.value, self.slots.at[9], self.send.at[9], self.recv.at[9], self.place.partner)]
-        return [remote(self.value, self.slots.at[stage * THREE + k], self.send.at[stage * THREE + k], self.recv.at[stage * THREE + k],
-                       self.place.device({stage: delta})) for k, delta in enumerate((ONE, -ONE, TWO))]
+        return [remote(self.value, self.slots.at[THREE * stage + k], self.send.at[THREE * stage + k], self.recv.at[THREE * stage + k], peer)
+                for k, peer in enumerate(self.peers(stage))]
 
     def start(self, stage):
         for copy in self.copies(stage):
@@ -355,19 +358,43 @@
         copies = self.copies(stage)
         for copy in copies:
             copy.wait()
-        value = self.value[...]
-        for k in range(len(copies)):
-            value = value + self.slots[stage * THREE + k]
-        self.value[...] = value
+        self.value[...] = functools.reduce(jnp.add, [self.slots[THREE * stage + k] for k in range(len(copies))], self.value[...])
+
+    def turn(self, stage):
+        def step():
+            self.finish(stage)
+            self.start(stage + ONE)
+        return step
 
     def steps(self):
-        def turn(stage):
-            def step():
-                self.finish(stage)
-                self.start(stage + ONE)
-            return step
-
-        return [lambda: self.start(ZERO), turn(ZERO), turn(ONE), turn(TWO), lambda: self.finish(THREE)]
+        return [lambda: self.start(ZERO), self.turn(ZERO), self.turn(ONE), self.turn(TWO), lambda: self.finish(THREE)]
+
+
+class Late(Small):
+    def __init__(self, place, value, slots, send, recv, planes, plane_send, plane_recv):
+        super().__init__(place, value, slots, send, recv)
+        self.planes, self.plane_send, self.plane_recv = planes, plane_send, plane_recv
+
+    def peers(self, stage):
+        return super().peers({ZERO: ORDERS[ZERO][ZERO], ONE: THREE}[stage])
+
+    def plane(self, k):
+        return remote(self.value, self.planes.at[k], self.plane_send.at[k], self.plane_recv.at[k], self.place.device(plane_offsets(ORDERS[ZERO], k)))
+
+    def steps(self):
+        def first():
+            @pl.loop(ONE, SIXTEEN)
+            def _(k):
+                self.plane(k).start()
+
+        def second():
+            @pl.loop(ONE, SIXTEEN)
+            def _(k):
+                self.plane(k).wait()
+            self.value[...] = functools.reduce(jnp.add, [self.planes[k] for k in range(ONE, SIXTEEN)], self.value[...])
+            self.start(ZERO)
+
+        return [first, second, self.turn(ZERO), lambda: self.finish(ONE)]
 
 
 VMEM = pl.BlockSpec(memory_space=pltpu.VMEM)
@@ -453,11 +480,11 @@
     return hook
 
 
-def forward_kernel(len_ref, x_ref, cos_ref, sin_ref, w_attn, b_attn, ln_par, w_up, b_up, w_down, b_down,
+def forward_kernel(len_ref, x_hbm, cos_ref, sin_ref, w_attn, b_attn, ln_par, w_up, b_up, w_down, b_down,
                    xs_out, q_ref, k_ref, v_ref, p_hbm, ctx_ref, mid_ref, act_ref, slope_ref, st1_ref, st2_ref, c_ref,
                    nat_qkv, nat_wo, nat_up, nat_down,
                    xs, ctxb, wqkv, wo, up, down, n_qkv, n_wo, n_up, n_down, p_buf, h_ref, s_a, s_b, s_c,
-                   sbuf, q0, q1, q2, m0, m1, m2, send, recv, p_sem, nat_sem):
+                   sbuf, q0, q1, q2, m0, m1, m2, stats, send, recv, p_sem, nat_sem, x_sem):
     step = pl.program_id(ZERO)
     phase, seq, layer = step // FOUR, lax.rem(step, FOUR), step // EIGHT
     place = Place()
@@ -508,9 +535,12 @@
             down[:, part] = n_down[part, :].T
         start(nat_copies(ONE, layer))
 
+    x_copies = [pltpu.make_async_copy(x_hbm.at[s], ctxb.at[s], x_sem.at[s]) for s in range(SEQS)]
+
     @pl.when(step == ZERO)
     def _():
         place.greet()
+        start(x_copies)
         for l in range(TWO):
             for unit in range(12):
                 if unit < FOUR:
@@ -524,13 +554,29 @@
                 else:
                     mo_bufs[(unit - THREE) // THREE][l, z, y, x, place.core, (unit - THREE) % THREE] = tile
         sbuf[z, y, x, place.core, ZERO] = small_row(b_attn, ln_par, b_up, b_down)
+        first, second = gather_steps(group(qkv_bufs, ZERO, ZERO) + [little]), gather_steps(group(mo_bufs, THREE, ZERO))
+
+        def ready(s):
+            x_copies[s].wait()
+            xs[s] = ctxb[s].T
+            put_stats(stats.at[s], norm_stats(xs.at[s]))
+
         place.met()
-        for run in gather_steps(group(qkv_bufs, ZERO, ZERO) + [little]):
-            run()
+        first[ZERO]()
+        second[ZERO]()
+        ready(ZERO)
+        ready(ONE)
+        first[ONE]()
+        ready(TWO)
+        ready(THREE)
+        first[TWO]()
+        second[ONE]()
+        first[THREE]()
         small_columns(sbuf, c_ref)
 
-    attn_hook = hooks(step * FOUR, [((when, when + 32), run) for when, run in zip(MO_SLOTS, gather_steps(group(mo_bufs, THREE, layer)))])
-    mlp_hook = hooks(step * FOUR, [((when,), run) for when, run in zip(QKV_SLOTS, gather_steps(group(qkv_bufs, ZERO, ONE)))])
+    attn_hook = hooks(step * FOUR, [((when, when + 32), run) for when, run in zip((9, 13), gather_steps(group(mo_bufs, THREE, layer))[TWO:])])
+    mlp_steps = gather_steps(group(qkv_bufs, ZERO, ONE)) + gather_steps(group(mo_bufs, THREE, ONE))[:TWO]
+    mlp_hook = hooks(step * FOUR, [((when,), run) for when, run in zip((SIXTEEN, 25, 30, 31, 17, 26), mlp_steps)])
 
     @pl.when(phase % TWO == ZERO)
     def _():
@@ -538,13 +584,16 @@
 
         @pl.when(step < FOUR)
         def _():
-            xs[seq] = x_ref[ZERO].T
             xs_out[ZERO, ZERO] = xs[seq]
+
+        @pl.when(step > 7)
+        def _():
+            put_stats(stats.at[seq], norm_stats(xs.at[seq]))
 
         attn_hook(ZERO)
         copies = [pltpu.make_async_copy(p_buf.at[head], p_hbm.at[layer, seq, head], p_sem.at[head]) for head in range(HEADS)]
         attn_forward(len_ref[seq], xs.at[seq], wqkv, c_ref.at[layer], cos_ref, sin_ref, q_ref.at[ZERO, ZERO], k_ref.at[ZERO, ZERO],
-                     v_ref.at[ZERO, ZERO], p_buf, ctx_ref.at[ZERO, ZERO], ctxb.at[seq], st1_ref.at[ZERO, ZERO], h_ref, s_a, s_b, s_c, attn_hook,
+                     v_ref.at[ZERO, ZERO], p_buf, ctx_ref.at[ZERO, ZERO], ctxb.at[seq], get_stats(stats.at[seq]), st1_ref.at[ZERO, ZERO], h_ref, s_a, s_b, s_c, attn_hook,
                      lambda heads: pl.when(step > ZERO)(lambda: wait(copies[heads])), lambda heads: start(copies[heads]))
         pl.when(step == 11)(lambda: wait(copies))
         attn_hook(THREE)
@@ -567,8 +616,7 @@
             wait(nat_copies(which, ONE))
 
 
-def attn_forward(length, xt, w, c_ref, cos_ref, sin_ref, q_ref, k_ref, v_ref, p_buf, ctx_ref, ctxb, stat_ref, h_ref, s_a, s_b, s_c, hook, free, ship):
-    stats = norm_stats(xt)
+def attn_forward(length, xt, w, c_ref, cos_ref, sin_ref, q_ref, k_ref, v_ref, p_buf, ctx_ref, ctxb, stats, stat_ref, h_ref, s_a, s_b, s_c, hook, free, ship):
     put_stats(stat_ref, stats)
     norm_to(xt, stats, c_ref, LN_PAR, h_ref)
     for m, acc in enumerate((s_a, s_b, s_c)):
@@ -676,10 +724,6 @@
             xt[rows, :] = (mid_ref[rows, :].astype(F32) + s_a[rows, :] + column(c_ref, rows, B_DOWN)).astype(BF16)
 
 
-MO_SLOTS = (ZERO, 5, 13, 15)
-QKV_SLOTS = (SIXTEEN, 22, 26, 28)
-
-
 def forward(lengths, x, tables, params):
     def saved(index, rows, dtype):
         return jax.ShapeDtypeStruct((TWO, SEQS, rows, TOK), dtype), pl.BlockSpec((ONE, ONE, rows, TOK), index)
@@ -703,12 +747,11 @@
     scratch = [(SEQS, *SQUARE), (SEQS, *SQUARE), weights[ZERO], weights[ONE], weights[THREE], weights[TWO], *weights, (HEADS, TOK, TOK), SQUARE]
     scratch = [pltpu.VMEM(s, BF16) for s in scratch] + [pltpu.VMEM(SQUARE, F32)] * THREE + [pltpu.VMEM((*GRID, TWO, ONE, ONE, LANES), F32)]
     scratch += [pltpu.VMEM((TWO, *GRID, TWO, n, SIXTEEN, LANES), BF16) for n in (ONE, THREE) for _ in range(THREE)]
-    scratch += [DMA((7, TWO, 20)), DMA((7, TWO, 20)), DMA((HEADS,)), DMA((FOUR,))]
+    scratch += [pltpu.VMEM((SEQS, EIGHT, TOK), F32), DMA((7, TWO, 20)), DMA((7, TWO, 20)), DMA((HEADS,)), DMA((FOUR,)), DMA((SEQS,))]
     return pl.pallas_call(
         forward_kernel, grid=(SIXTEEN,),
         out_shape=[o[ZERO] for o in outs], out_specs=[o[ONE] for o in outs],
-        in_specs=[pl.BlockSpec(memory_space=pltpu.SMEM), pl.BlockSpec((ONE, *SQUARE), lambda s: (jnp.minimum(s, THREE), ZERO, ZERO)),
-                  once((HALF, TOK)), once((HALF, TOK))] + [once(p.shape) for p in params],
+        in_specs=[pl.BlockSpec(memory_space=pltpu.SMEM), HBM, once((HALF, TOK)), once((HALF, TOK))] + [once(p.shape) for p in params],
         scratch_shapes=scratch,
         compiler_params=pltpu.CompilerParams(collective_id=ZERO, has_side_effects=True, vmem_limit_bytes=67043328,
                                              dimension_semantics=("arbitrary",)),
@@ -736,12 +779,12 @@
     woven(beside, [functools.partial(run, rows) for run in (first, second) for rows in row_chunks()])
 
 
-def columns_of(pairs):
+def columns_of(partials):
     lane = lax.broadcasted_iota(jnp.int32, COLS, ONE)
     value = jnp.zeros(COLS, F32)
-    for at, partial in pairs:
+    for at, partial in enumerate(partials):
         value = jnp.where(lane == at, jnp.sum(partial, axis=ONE, keepdims=True), value)
-    return value
+    return value.T[:EIGHT]
 
 
 def head_rows(head):
@@ -772,9 +815,9 @@
                     qkv_hbm, wo_hbm, up_hbm, down_hbm,
                     dx_ref, attn_out, up_out, down_out, small_out, *refs):
     (grad, dctx, delta, big, wqkv, wo, slope, act, dpre, h_ref, s_a, s_b, d_a, d_b, sums,
-     g_qkv, g_wo, g_up, g_down, rows_ref, slots_ref), refs = refs[:21], refs[21:]
+     g_qkv, g_wo, g_up, g_down, rows_ref, slots_ref, late_ref, late_slots, planes_ref), refs = refs[:24], refs[24:]
     qkv_bufs, mo_bufs, refs = [refs[5 * k:5 * k + 5] for k in range(THREE)], [refs[5 * k + 15:5 * k + 20] for k in range(THREE)], refs[30:]
-    send, recv, ssend, srecv, big_sem, w_sem, mlp_sem = refs
+    send, recv, small_sem, late_sem, plane_sem, big_sem, w_sem, mlp_sem = refs
     step = pl.program_id(ZERO)
     phase, seq = step // FOUR, lax.rem(step, FOUR)
     layer = ONE - step // EIGHT
@@ -793,7 +836,8 @@
     turn = jnp.where(live, ZERO, ONE)
     qkv_sums = Reduce(place, ((ZERO,), (ONE,), (TWO,)), grads, [(a, ra, rb, rp.at[turn], o) for a, ra, rb, rp, o in qkv_bufs], send.at[turn], recv.at[turn])
     mo_sums = Reduce(place, COLOURS, grads, mo_bufs, send.at[TWO], recv.at[TWO])
-    tiny = Small(place, rows_ref, slots_ref, ssend, srecv)
+    tiny = Small(place, rows_ref, slots_ref, small_sem.at[ZERO], small_sem.at[ONE])
+    late = Late(place, late_ref, late_slots, late_sem.at[ZERO], late_sem.at[ONE], planes_ref, plane_sem.at[ZERO], plane_sem.at[ONE])
     first_core = place.core == ZERO
 
     def store(l):
@@ -843,10 +887,10 @@
     pl.when(step == ONE)(place.met)
     mo_steps, qkv_steps = mo_sums.steps(store(layer)), qkv_sums.steps(store(ONE - turn))
     late_steps = mo_sums.steps(store(ONE - turn))[FOUR:]
-    attn_hook = hooks(step * FOUR, [((when, when + 32), run) for when, run in zip((SIXTEEN, 20, 24, 30), mo_steps)])
+    attn_hook = hooks(step * FOUR, [((when, when + 32), run) for when, run in zip((SIXTEEN, 20, 24, 30), mo_steps)] + [((when,), run) for when, run in zip((48, 53, 57, 61, 63), tiny.steps())])
     mlp_plan = list(zip(((37, 69), (38, 70)), late_steps))
     mlp_plan += list(zip(((32, 64), (33, 65), (38, 66), (43, 67), (47, 71), (47, 71)), qkv_steps))
-    mlp_plan += [((when,), run) for when, run in zip((64, 65, 66, 67, 71), tiny.steps())]
+    mlp_plan += [((when,), run) for when, run in zip((64, 66, 67, 70), late.steps())]
     mlp_hook = hooks(step * FOUR, mlp_plan)
 
     @pl.when(phase % TWO == ZERO)
@@ -883,9 +927,7 @@
 
         @pl.when((seq == THREE) & live)
         def _():
-            value = columns_of([(B_UP + i, sums[i]) for i in range(FOUR)] + [
-                (LN_PAR + TWO, sums[FOUR]), (LN_PAR + THREE, sums[5]), (B_DOWN, sums[6]), (B_ATTN + THREE, sums[7])])
-            rows_ref[pl.ds(pl.multiple_of(layer * SIXTEEN, SIXTEEN), SIXTEEN), :] = value.T[:SIXTEEN]
+            rows_ref[pl.ds(pl.multiple_of(SIXTEEN - SIXTEEN * layer, EIGHT), EIGHT), :] = columns_of([sums[i] for i in range(EIGHT)])
 
         mlp_hook(THREE)
 
@@ -913,9 +955,11 @@
 
         @pl.when(seq == THREE)
         def _():
-            value = columns_of([(B_ATTN + i, sums[i]) for i in range(THREE)] + [(LN_PAR, sums[THREE]), (LN_PAR + ONE, sums[FOUR])])
-            rows = pl.ds(pl.multiple_of(layer * SIXTEEN, SIXTEEN), SIXTEEN)
-            rows_ref[rows, :] = rows_ref[rows, :] + value.T[:SIXTEEN]
+            late_ref[...] = columns_of([sums[i] for i in range(5)])
+
+        @pl.when(step == 7)
+        def _():
+            rows_ref[EIGHT:SIXTEEN, :] = late_ref[...]
 
         @pl.when(step == 7)
         def _():
@@ -928,7 +972,7 @@
 
     @pl.when(step == 17)
     def _():
-        small_out[...] = rows_ref[...]
+        small_out[:24, :], small_out[24:, :] = rows_ref[...], late_ref[...]
 
 
 def add_to(ref, value):
@@ -1066,13 +1110,14 @@
                pltpu.VMEM(TALL, F32), pltpu.VMEM(TALL, BF16), pltpu.VMEM(TALL, BF16), pltpu.VMEM(SQUARE, BF16),
                pltpu.VMEM(SQUARE, F32), pltpu.VMEM(SQUARE, F32), pltpu.VMEM((TOK, TOK), BF16), pltpu.VMEM((TOK, TOK), BF16),
                pltpu.VMEM((EIGHT, *COLS), F32), pltpu.VMEM((THREE, *GRID, EIGHT, DIM), F32), pltpu.VMEM((*GRID, EIGHT, DIM), F32),
-               pltpu.VMEM((FOUR, *GRID, EIGHT, DIM), F32), pltpu.VMEM((*GRID, FOUR, EIGHT, DIM), F32), pltpu.VMEM((32, DIM), F32), pltpu.VMEM((10, 32, DIM), F32)]
+               pltpu.VMEM((FOUR, *GRID, EIGHT, DIM), F32), pltpu.VMEM((*GRID, FOUR, EIGHT, DIM), F32), pltpu.VMEM((24, DIM), F32), pltpu.VMEM((10, 24, DIM), F32),
+               pltpu.VMEM((EIGHT, DIM), F32), pltpu.VMEM((6, EIGHT, DIM), F32), pltpu.VMEM((SIXTEEN, EIGHT, DIM), F32)]
     for n in (ONE, THREE):
         for order in ORDERS:
             ring_a, ring_b, plane, other = landing_shapes(order, n)
             plane = (TWO, *plane) if n == ONE else plane
             scratch += [pltpu.VMEM(s, F32) for s in ((n, *GRID, EIGHT, WIDTH), ring_a, ring_b, plane, other)]
-    scratch += [DMA((THREE, THREE, 24)), DMA((THREE, THREE, 24)), DMA((10,)), DMA((10,)), DMA((EIGHT,)), DMA((TWO,)), DMA((TWO,))]
+    scratch += [DMA((THREE, THREE, 24)), DMA((THREE, THREE, 24)), DMA((TWO, 10)), DMA((TWO, 6)), DMA((TWO, SIXTEEN)), DMA((EIGHT,)), DMA((TWO,)), DMA((TWO,))]
     outs = ((TWO, FOUR, FOUR, DIM), (TWO, FOUR, FFN), (TWO, SIXTEEN, DIM), (32, DIM))
     whole = [pl.BlockSpec(s, lambda i, n=len(s): (ZERO,) * n, pipeline_mode=pl.Buffered(ONE)) for s in outs]
     dx_at = lambda s: (jnp.clip(s - 12, ZERO, THREE), ZERO, ZERO)
@@ -1088,6 +1133,34 @@
         name="backward")(dy, mid, ctx, st2, q, k, v, xs, st1, *tables, c, probs, slope, act, w_qkv, w_o, w_up, w_down)
 
 
+def results_kernel(dx_ref, attn_ref, up_ref, down_ref, small_ref, dx_out, attn_out, gb_attn, g_ln, up_out, gb_up, down_out, gb_down):
+    dx_out[...] = dx_ref[...]
+
+    @pl.when(pl.program_id(ZERO) == ZERO)
+    def _():
+        me = lax.axis_index(AXIS)
+        attn_out[...], up_out[...], down_out[...] = attn_ref[...], up_ref[...], down_ref[...]
+        mine = pltpu.roll(small_ref[...], lax.rem(DIM - FOUR * me + FOUR * LANES, DIM), ONE)
+        for l in range(TWO):
+            mlp = SIXTEEN - SIXTEEN * l
+            attn = mlp + EIGHT
+            gb_attn[l, :THREE], gb_attn[l, THREE:] = mine[attn:attn + THREE, :FOUR], mine[mlp + 7:mlp + EIGHT, :FOUR]
+            g_ln[l, :TWO], g_ln[l, TWO:] = mine[attn + THREE:attn + 5, :FOUR], mine[mlp + FOUR:mlp + 6, :FOUR]
+            gb_down[l:l + ONE, :] = mine[mlp + 6:mlp + 7, :FOUR]
+            ups = small_ref[pl.ds(mlp + me // 32, ONE), :]
+            gb_up[l:l + ONE, :] = pltpu.roll(ups, lax.rem(DIM - SIXTEEN * lax.rem(me, 32), DIM), ONE)[:, :SIXTEEN]
+
+
+def results(dx, attn, up, down, small):
+    shapes = [attn.shape, (TWO, FOUR, FOUR), (TWO, FOUR, FOUR), up.shape, (TWO, SIXTEEN), down.shape, (TWO, FOUR)]
+    per = pl.BlockSpec((ONE, TOK, DIM), lambda s: (s, ZERO, ZERO))
+    return pl.pallas_call(
+        results_kernel, grid=(SEQS,), name="results",
+        out_shape=[jax.ShapeDtypeStruct(dx.shape, BF16)] + [jax.ShapeDtypeStruct(s, F32) for s in shapes],
+        in_specs=[per] + [once(a.shape) for a in (attn, up, down, small)],
+        out_specs=[per] + [once(s) for s in shapes])(dx, attn, up, down, small)
+
+
 def solution(mesh):
     batch_spec = P(AXIS)
     weight_specs = (P(None, None, AXIS, None), P(None, None, AXIS), P(None, None, AXIS),
@@ -1097,12 +1170,7 @@
         tables = rotary_tables()
         xs, q, k, v, probs, ctx, mid, act, slope, st1, st2, c, w_qkv, w_o, w_up, w_down = forward(
             lengths, x, tables, (w_attn, b_attn, ln_par, w_up, b_up, w_down, b_down))
-        grad, attn, up, down, small = backward(d_y, xs, q, k, v, probs, ctx, mid, act, slope, st1, st2, c, tables, w_qkv, w_o, w_up, w_down)
-        me = lax.axis_index(AXIS)
-        small = small.reshape(TWO, SIXTEEN, DIM)
-        mine = lax.dynamic_slice(small, (ZERO, ZERO, FOUR * me), (TWO, SIXTEEN, FOUR))
-        b_up_grad = lax.dynamic_slice(small[:, B_UP:B_DOWN].reshape(TWO, FFN), (ZERO, SIXTEEN * me), (TWO, SIXTEEN))
-        return grad, attn, mine[:, :FOUR], mine[:, FOUR:EIGHT], up, b_up_grad, down, mine[:, 12]
+        return results(*backward(d_y, xs, q, k, v, probs, ctx, mid, act, slope, st1, st2, c, tables, w_qkv, w_o, w_up, w_down))
 
     return jax.shard_map(device_step, mesh=mesh,
                          in_specs=(batch_spec, batch_spec, batch_spec) + weight_specs,

time: 307 us -> 302 us (0.984)
  local copies, waits for them, and re-layouts: 9.17 us -> 0 us
  Pallas kernels: 296 us -> 300 us
    unnamed x12 -> x0, local copies, waits for them, and re-layouts: 5.76 us -> none
    pallas_call x1, Pallas kernels: 163 us -> 168 us  [backward(): pl.pallas_call(backward_kernel, grid=(18,), out_shape=[jax.ShapeDtypeStru...]
    pallas_call x0 -> x1, Pallas kernels: none -> 3.98 us  [results(): pl.pallas_call(results_kernel, grid=(SEQS,), name='results', out_shape=[j...]
    pallas_call x1, Pallas kernels: 132 us -> 128 us  [forward(): pl.pallas_call(forward_kernel, grid=(SIXTEEN,), out_shape=[o[ZERO] for o...]
where the time goes in v3:
time: 302 us
  Pallas kernels  300 us (99%)
    pallas_call x1, Pallas kernels, backward(): pl.pallas_call(backward_kernel, grid=(18,), out_shape=[jax.ShapeDtypeStru...  168 us
    pallas_call x1, Pallas kernels, forward(): pl.pallas_call(forward_kernel, grid=(SIXTEEN,), out_shape=[o[ZERO] for o...  128 us

profile of v3, /device:TPU:1, one launch (start us, length us, event | category | flops | bytes accessed | tf_op | source)
XLA Modules:
  0.0 302.3 jit_solution(18172080224467847145)
XLA Ops:
  0.6 1.0 fusion
  1.6 128.3 %forward.1 = (bf16[2,4,512,512]{3,2,1,0:T(8,128)(2,1)}, bf16[2,4,512,512]{3,2,1,0:T(8,128)(2,1)}, bf16[2,4,512,512]{3,2,1,0:T(8,128)(2,1)}, bf16[2,4,512,512]{3,...) custom-call(s32[4]{0:T(128)} %len_ref.1, ...), custom_call_target="tpu_custom_call" | custom-call | tf_op jit(solution)/shard_map/forward/pallas_call | solution.py:751
  130.0 168.1 %backward.1 = (bf16[4,512,512]{2,1,0:T(8,128)(2,1)}, f32[2,4,4,512]{3,2,1,0:T(4,128)}, f32[2,4,2048]{2,1,0:T(4,128)}, f32[2,16,512]{2,1,0:T(8,128)}, f32[32,512]{1,0:T(8,128)}) custom-call(bf16[4,512,512]{2,1,0:T(8,128)(2,1)} %dy_ref.1, bf16[2,4,512,512]{3,2,1,0:T(8,128)(2,1)} %get-tuple-element.29.mid_ref, f32[2,4,512,512]{3,2,1,0:T(8,128)} %get-tuple-element.30.ctx_ref, ...), custom_call_target="tpu_custom_call" | custom-call | tf_op jit(solution)/shard_map/backward/pallas_call | solution.py:1124
  298.1 4.0 %results.1 = (bf16[4,512,512]{2,1,0:T(8,128)(2,1)}, f32[2,4,4,512]{3,2,1,0:T(4,128)}, f32[2,4,4]{2,1,0:T(4,128)}, f32[2,4,4]{2,1,0:T(4,128)}, f32[2,4,2048]{2,1,...) custom-call(bf16[4,512,512]{2,1,0:T(8,128)(2,1)} %get-tuple-element.45.dx_ref, ...), custom_call_target="tpu_custom_call" | custom-call | tf_op jit(solution)/shard_map/results/pallas_call | solution.py:1157
  (1 shorter events, 0.0 us)

commit v4 on v3

--- a/solution.py
+++ b/solution.py
@@ -157,8 +157,8 @@
 
 
 class Gather:
-    def __init__(self, place, buf, order, send, recv):
-        self.place, self.buf, self.order, self.send, self.recv = place, buf, order, send, recv
+    def __init__(self, place, buf, fifteen, order, send, recv):
+        self.place, self.buf, self.fifteen, self.order, self.send, self.recv = place, buf, fifteen, order, send, recv
 
     def block(self, offsets, whole=()):
         index = [slice(ZERO, FOUR) if dim in whole else pl.ds(self.place.coord(dim, offsets.get(dim, ZERO)), ONE) for dim in range(THREE)]
@@ -170,12 +170,13 @@
     def plane_start(self):
         @pl.loop(ONE, SIXTEEN)
         def _(k):
-            self.copy(self.block({}), k, self.place.device(plane_offsets(self.order, k))).start()
+            self.copy(self.block({}), ZERO, self.place.device(plane_offsets(self.order, k))).start()
+
+    def plane_all(self):
+        return self.copy(self.fifteen, ZERO, self.place.partner)
 
     def plane_wait(self):
-        @pl.loop(ONE, SIXTEEN)
-        def _(k):
-            self.copy(self.block(plane_offsets(self.order, k, -ONE)), k, self.place.partner).wait_recv()
+        self.plane_all().wait_recv()
 
     def line(self, i, sign):
         offsets = {self.order[ZERO]: sign * LINE[i]}
@@ -183,26 +184,23 @@
 
     def line_start(self):
         for i, delta in enumerate(LINE):
-            self.copy(self.line(i, ZERO), SIXTEEN + i, self.place.device({self.order[ZERO]: delta})).start()
+            self.copy(self.line(i, ZERO), ONE + i, self.place.device({self.order[ZERO]: delta})).start()
 
     def line_wait(self):
         for i in range(THREE):
-            self.copy(self.line(i, -ONE), SIXTEEN + i, self.place.partner).wait_recv()
+            self.copy(self.line(i, -ONE), ONE + i, self.place.partner).wait_recv()
 
     def share(self, core):
-        return self.copy(self.buf.at[:, :, :, pl.ds(core, ONE)], 19, self.place.partner)
+        return self.copy(self.buf.at[:, :, :, pl.ds(core, ONE)], FOUR, self.place.partner)
 
     def share_start(self):
         self.share(self.place.core).start()
 
     def end(self):
         self.share(ONE - self.place.core).wait_recv()
-
-        @pl.loop(ONE, SIXTEEN)
-        def _(k):
-            self.copy(self.block({}), k, self.place.partner).wait_send()
+        self.plane_all().wait_send()
         for i in range(THREE):
-            self.copy(self.line(i, ZERO), SIXTEEN + i, self.place.partner).wait_send()
+            self.copy(self.line(i, ZERO), ONE + i, self.place.partner).wait_send()
         self.share(self.place.core).wait_send()
 
 
@@ -228,7 +226,7 @@
 
     def swap_copy(self, u):
         place = self.place
-        return remote(self.grads(u).at[:, :, :, :, self.columns(ONE - place.core)], self.acc.at[u], self.send.at[20 + u], self.recv.at[20 + u], place.partner)
+        return remote(self.grads(u).at[:, :, :, :, self.columns(ONE - place.core)], self.acc.at[u], self.send.at[6 + u], self.recv.at[6 + u], place.partner)
 
     def swap(self):
         for u in range(self.units):
@@ -255,7 +253,7 @@
             src, dst = self.part(TWO, way), self.got_a.at[:, :, :, :, :, lane_tiles()[way]]
         else:
             src, dst = self.part(delta), self.got_b.at[way]
-        key = SIXTEEN + TWO * step + way
+        key = TWO * step + way
         return remote(src, dst, self.send.at[key], self.recv.at[key], device)
 
     def ring_start(self):
@@ -289,7 +287,10 @@
         offsets = plane_offsets(self.order, k)
         index = [pl.ds(self.place.coord(dim, offsets.get(dim, ZERO)), ONE) for dim in range(THREE)]
         src = self.acc.at[:, index[ZERO], index[ONE], index[TWO]]
-        return remote(src, self.got_p.at[k], self.send.at[k], self.recv.at[k], self.place.device(offsets))
+        return remote(src, self.got_p.at[k], self.send.at[FOUR], self.recv.at[FOUR], self.place.device(offsets))
+
+    def plane_all(self):
+        return remote(self.got_p.at[ONE:], self.got_p.at[ONE:], self.send.at[FOUR], self.recv.at[FOUR], self.place.partner)
 
     def plane_start(self):
         for way in range(TWO):
@@ -305,12 +306,10 @@
         return self.acc.at[:, z, y, x]
 
     def last_copy(self):
-        return remote(self.own(), self.other, self.send.at[23], self.recv.at[23], self.place.partner)
+        return remote(self.own(), self.other, self.send.at[5], self.recv.at[5], self.place.partner)
 
     def last(self):
-        @pl.loop(ONE, SIXTEEN)
-        def _(k):
-            self.plane_copy(k).wait_recv()
+        self.plane_all().wait_recv()
         own = self.own()
         own[...] = functools.reduce(jnp.add, [self.got_p[k] for k in range(ONE, SIXTEEN)], own[...])
         self.last_copy().start()
@@ -324,10 +323,7 @@
         for step in range(TWO):
             for way in range(TWO):
                 self.ring(step, way).wait_send()
-
-        @pl.loop(ONE, SIXTEEN)
-        def _(k):
-            self.plane_copy(k).wait_send()
+        self.plane_all().wait_send()
         self.last_copy().wait_send()
 
 
@@ -379,7 +375,7 @@
         return super().peers({ZERO: ORDERS[ZERO][ZERO], ONE: THREE}[stage])
 
     def plane(self, k):
-        return remote(self.value, self.planes.at[k], self.plane_send.at[k], self.plane_recv.at[k], self.place.device(plane_offsets(ORDERS[ZERO], k)))
+        return remote(self.value, self.planes.at[k], self.plane_send, self.plane_recv, self.place.device(plane_offsets(ORDERS[ZERO], k)))
 
     def steps(self):
         def first():
@@ -388,9 +384,7 @@
                 self.plane(k).start()
 
         def second():
-            @pl.loop(ONE, SIXTEEN)
-            def _(k):
-                self.plane(k).wait()
+            remote(self.planes.at[ONE:], self.planes.at[ONE:], self.plane_send, self.plane_recv, self.place.partner).wait()
             self.value[...] = functools.reduce(jnp.add, [self.planes[k] for k in range(ONE, SIXTEEN)], self.value[...])
             self.start(ZERO)
 
@@ -484,17 +478,17 @@
                    xs_out, q_ref, k_ref, v_ref, p_hbm, ctx_ref, mid_ref, act_ref, slope_ref, st1_ref, st2_ref, c_ref,
                    nat_qkv, nat_wo, nat_up, nat_down,
                    xs, ctxb, wqkv, wo, up, down, n_qkv, n_wo, n_up, n_down, p_buf, h_ref, s_a, s_b, s_c,
-                   sbuf, q0, q1, q2, m0, m1, m2, stats, send, recv, p_sem, nat_sem, x_sem):
+                   sbuf, q0, q1, q2, m0, m1, m2, stats, f0, f1, f2, send, recv, p_sem, nat_sem, x_sem):
     step = pl.program_id(ZERO)
     phase, seq, layer = step // FOUR, lax.rem(step, FOUR), step // EIGHT
     place = Place()
     z, y, x = place.pos
-    qkv_bufs, mo_bufs = (q0, q1, q2), (m0, m1, m2)
+    qkv_bufs, mo_bufs, fifteen = (q0, q1, q2), (m0, m1, m2), (f0, f1, f2)
 
     def group(bufs, base, l):
-        return [Gather(place, b.at[l], ORDERS[k], send.at[base + k, l], recv.at[base + k, l]) for k, b in enumerate(bufs)]
-
-    little = Gather(place, sbuf, ORDERS[ZERO], send.at[6, ZERO], recv.at[6, ZERO])
+        return [Gather(place, b.at[l], fifteen[base // THREE], ORDERS[k], send.at[base + k, l], recv.at[base + k, l]) for k, b in enumerate(bufs)]
+
+    little = Gather(place, sbuf, fifteen[TWO], ORDERS[ZERO], send.at[6, ZERO], recv.at[6, ZERO])
 
     def nat_copies(which, l):
         if which == ZERO:
@@ -684,8 +678,8 @@
             ship(halves[ZERO])
             hook(TWO)
             free(halves[ONE])
+    close_head(HEADS - ONE)
     ship(halves[ONE])
-    close_head(HEADS - ONE)
 
 
 def mlp_forward(layer, ctxb, xt, wo, up, down, c_ref, mid_ref, act_ref, slope_ref, stat_ref, h_ref, s_a, s_b, hook):
@@ -747,7 +741,8 @@
     scratch = [(SEQS, *SQUARE), (SEQS, *SQUARE), weights[ZERO], weights[ONE], weights[THREE], weights[TWO], *weights, (HEADS, TOK, TOK), SQUARE]
     scratch = [pltpu.VMEM(s, BF16) for s in scratch] + [pltpu.VMEM(SQUARE, F32)] * THREE + [pltpu.VMEM((*GRID, TWO, ONE, ONE, LANES), F32)]
     scratch += [pltpu.VMEM((TWO, *GRID, TWO, n, SIXTEEN, LANES), BF16) for n in (ONE, THREE) for _ in range(THREE)]
-    scratch += [pltpu.VMEM((SEQS, EIGHT, TOK), F32), DMA((7, TWO, 20)), DMA((7, TWO, 20)), DMA((HEADS,)), DMA((FOUR,)), DMA((SEQS,))]
+    scratch += [pltpu.VMEM((SEQS, EIGHT, TOK), F32)] + [pltpu.VMEM((15, n, SIXTEEN, LANES), BF16) for n in (ONE, THREE)]
+    scratch += [pltpu.VMEM((15, ONE, ONE, LANES), F32), DMA((7, TWO, 5)), DMA((7, TWO, 5)), DMA((HEADS,)), DMA((FOUR,)), DMA((SEQS,))]
     return pl.pallas_call(
         forward_kernel, grid=(SIXTEEN,),
         out_shape=[o[ZERO] for o in outs], out_specs=[o[ONE] for o in outs],
@@ -815,9 +810,9 @@
                     qkv_hbm, wo_hbm, up_hbm, down_hbm,
                     dx_ref, attn_out, up_out, down_out, small_out, *refs):
     (grad, dctx, delta, big, wqkv, wo, slope, act, dpre, h_ref, s_a, s_b, d_a, d_b, sums,
-     g_qkv, g_wo, g_up, g_down, rows_ref, slots_ref, late_ref, late_slots, planes_ref), refs = refs[:24], refs[24:]
+     g_qkv, g_wo, g_up, g_down, *small_bufs), refs = refs[:28], refs[28:]
     qkv_bufs, mo_bufs, refs = [refs[5 * k:5 * k + 5] for k in range(THREE)], [refs[5 * k + 15:5 * k + 20] for k in range(THREE)], refs[30:]
-    send, recv, small_sem, late_sem, plane_sem, big_sem, w_sem, mlp_sem = refs
+    send, recv, late_sem, plane_sem, big_sem, w_sem, mlp_sem = refs
     step = pl.program_id(ZERO)
     phase, seq = step // FOUR, lax.rem(step, FOUR)
     layer = ONE - step // EIGHT
@@ -836,8 +831,9 @@
     turn = jnp.where(live, ZERO, ONE)
     qkv_sums = Reduce(place, ((ZERO,), (ONE,), (TWO,)), grads, [(a, ra, rb, rp.at[turn], o) for a, ra, rb, rp, o in qkv_bufs], send.at[turn], recv.at[turn])
     mo_sums = Reduce(place, COLOURS, grads, mo_bufs, send.at[TWO], recv.at[TWO])
-    tiny = Small(place, rows_ref, slots_ref, small_sem.at[ZERO], small_sem.at[ONE])
-    late = Late(place, late_ref, late_slots, late_sem.at[ZERO], late_sem.at[ONE], planes_ref, plane_sem.at[ZERO], plane_sem.at[ONE])
+    small_refs = small_bufs[::THREE]
+    early, middle, late = [Late(place, small_refs[i], small_bufs[THREE * i + ONE], late_sem.at[i, ZERO], late_sem.at[i, ONE], small_bufs[THREE * i + TWO],
+                                plane_sem.at[i, ZERO], plane_sem.at[i, ONE]).steps() for i in range(THREE)]
     first_core = place.core == ZERO
 
     def store(l):
@@ -887,10 +883,12 @@
     pl.when(step == ONE)(place.met)
     mo_steps, qkv_steps = mo_sums.steps(store(layer)), qkv_sums.steps(store(ONE - turn))
     late_steps = mo_sums.steps(store(ONE - turn))[FOUR:]
-    attn_hook = hooks(step * FOUR, [((when, when + 32), run) for when, run in zip((SIXTEEN, 20, 24, 30), mo_steps)] + [((when,), run) for when, run in zip((48, 53, 57, 61, 63), tiny.steps())])
+    attn_hook = hooks(step * FOUR, list(zip(((48,), (52,), (57,), (61,)), middle)) +
+                      [((when, when + 32), run) for when, run in zip((SIXTEEN, 20, 24, 30), mo_steps)])
     mlp_plan = list(zip(((37, 69), (38, 70)), late_steps))
     mlp_plan += list(zip(((32, 64), (33, 65), (38, 66), (43, 67), (47, 71), (47, 71)), qkv_steps))
-    mlp_plan += [((when,), run) for when, run in zip((64, 66, 67, 70), late.steps())]
+    mlp_plan += [((when,), run) for when, run in zip((64, 66, 67, 70), late)]
+    mlp_plan += [((when,), run) for when, run in zip((34, 37, 41, 45), early)]
     mlp_hook = hooks(step * FOUR, mlp_plan)
 
     @pl.when(phase % TWO == ZERO)
@@ -927,7 +925,15 @@
 
         @pl.when((seq == THREE) & live)
         def _():
-            rows_ref[pl.ds(pl.multiple_of(SIXTEEN - SIXTEEN * layer, EIGHT), EIGHT), :] = columns_of([sums[i] for i in range(EIGHT)])
+            value = columns_of([sums[i] for i in range(EIGHT)])
+
+            @pl.when(layer == ONE)
+            def _():
+                small_refs[ZERO][:EIGHT, :] = value
+
+            @pl.when(layer == ZERO)
+            def _():
+                small_refs[ONE][...] = value
 
         mlp_hook(THREE)
 
@@ -955,11 +961,15 @@
 
         @pl.when(seq == THREE)
         def _():
-            late_ref[...] = columns_of([sums[i] for i in range(5)])
-
-        @pl.when(step == 7)
-        def _():
-            rows_ref[EIGHT:SIXTEEN, :] = late_ref[...]
+            value = columns_of([sums[i] for i in range(5)])
+
+            @pl.when(layer == ONE)
+            def _():
+                small_refs[ZERO][EIGHT:, :] = value
+
+            @pl.when(layer == ZERO)
+            def _():
+                small_refs[TWO][...] = value
 
         @pl.when(step == 7)
         def _():
@@ -972,7 +982,7 @@
 
     @pl.when(step == 17)
     def _():
-        small_out[:24, :], small_out[24:, :] = rows_ref[...], late_ref[...]
+        small_out[:SIXTEEN, :], small_out[SIXTEEN:24, :], small_out[24:, :] = [ref[...] for ref in small_refs]
 
 
 def add_to(ref, value):
@@ -1110,14 +1120,13 @@
                pltpu.VMEM(TALL, F32), pltpu.VMEM(TALL, BF16), pltpu.VMEM(TALL, BF16), pltpu.VMEM(SQUARE, BF16),
                pltpu.VMEM(SQUARE, F32), pltpu.VMEM(SQUARE, F32), pltpu.VMEM((TOK, TOK), BF16), pltpu.VMEM((TOK, TOK), BF16),
                pltpu.VMEM((EIGHT, *COLS), F32), pltpu.VMEM((THREE, *GRID, EIGHT, DIM), F32), pltpu.VMEM((*GRID, EIGHT, DIM), F32),
-               pltpu.VMEM((FOUR, *GRID, EIGHT, DIM), F32), pltpu.VMEM((*GRID, FOUR, EIGHT, DIM), F32), pltpu.VMEM((24, DIM), F32), pltpu.VMEM((10, 24, DIM), F32),
-               pltpu.VMEM((EIGHT, DIM), F32), pltpu.VMEM((6, EIGHT, DIM), F32), pltpu.VMEM((SIXTEEN, EIGHT, DIM), F32)]
+               pltpu.VMEM((FOUR, *GRID, EIGHT, DIM), F32), pltpu.VMEM((*GRID, FOUR, EIGHT, DIM), F32), *[pltpu.VMEM((*lead, rows, DIM), F32) for rows in (SIXTEEN, EIGHT, EIGHT) for lead in ((), (6,), (SIXTEEN,))]]
     for n in (ONE, THREE):
         for order in ORDERS:
             ring_a, ring_b, plane, other = landing_shapes(order, n)
             plane = (TWO, *plane) if n == ONE else plane
             scratch += [pltpu.VMEM(s, F32) for s in ((n, *GRID, EIGHT, WIDTH), ring_a, ring_b, plane, other)]
-    scratch += [DMA((THREE, THREE, 24)), DMA((THREE, THREE, 24)), DMA((TWO, 10)), DMA((TWO, 6)), DMA((TWO, SIXTEEN)), DMA((EIGHT,)), DMA((TWO,)), DMA((TWO,))]
+    scratch += [DMA((THREE, THREE, 9)), DMA((THREE, THREE, 9)), DMA((THREE, TWO, 6)), DMA((THREE, TWO)), DMA((EIGHT,)), DMA((TWO,)), DMA((TWO,))]
     outs = ((TWO, FOUR, FOUR, DIM), (TWO, FOUR, FFN), (TWO, SIXTEEN, DIM), (32, DIM))
     whole = [pl.BlockSpec(s, lambda i, n=len(s): (ZERO,) * n, pipeline_mode=pl.Buffered(ONE)) for s in outs]
     dx_at = lambda s: (jnp.clip(s - 12, ZERO, THREE), ZERO, ZERO)

time: 302 us -> 298 us (0.987)
  Pallas kernels: 300 us -> 296 us
    pallas_call x1, Pallas kernels: 128 us -> 123 us  [forward(): pl.pallas_call(forward_kernel, grid=(SIXTEEN,), out_shape=[o[ZERO] for o...]
where the time goes in v4:
time: 298 us
  Pallas kernels  296 us (99%)
    pallas_call x1, Pallas kernels, backward(): pl.pallas_call(backward_kernel, grid=(18,), out_shape=[jax.ShapeDtypeStru...  169 us
    pallas_call x1, Pallas kernels, forward(): pl.pallas_call(forward_kernel, grid=(SIXTEEN,), out_shape=[o[ZERO] for o...  123 us

profile of v4, /device:TPU:1, one launch (start us, length us, event | category | flops | bytes accessed | tf_op | source)
XLA Modules:
  0.0 297.5 jit_solution(7028929917751086529)
XLA Ops:
  0.6 1.0 fusion
  1.6 123.1 %forward.1 = (bf16[2,4,512,512]{3,2,1,0:T(8,128)(2,1)}, bf16[2,4,512,512]{3,2,1,0:T(8,128)(2,1)}, bf16[2,4,512,512]{3,2,1,0:T(8,128)(2,1)}, bf16[2,4,512,512]{3,...) custom-call(s32[4]{0:T(128)} %len_ref.1, ...), custom_call_target="tpu_custom_call" | custom-call | tf_op jit(solution)/shard_map/forward/pallas_call | solution.py:746
  124.7 168.7 %backward.1 = (bf16[4,512,512]{2,1,0:T(8,128)(2,1)}, f32[2,4,4,512]{3,2,1,0:T(4,128)}, f32[2,4,2048]{2,1,0:T(4,128)}, f32[2,16,512]{2,1,0:T(8,128)}, f32[32,512]{1,0:T(8,128)}) custom-call(bf16[4,512,512]{2,1,0:T(8,128)(2,1)} %dy_ref.1, bf16[2,4,512,512]{3,2,1,0:T(8,128)(2,1)} %get-tuple-element.29.mid_ref, f32[2,4,512,512]{3,2,1,0:T(8,128)} %get-tuple-element.30.ctx_ref, ...), custom_call_target="tpu_custom_call" | custom-call | tf_op jit(solution)/shard_map/backward/pallas_call | solution.py:1133
  293.4 4.0 %results.1 = (bf16[4,512,512]{2,1,0:T(8,128)(2,1)}, f32[2,4,4,512]{3,2,1,0:T(4,128)}, f32[2,4,4]{2,1,0:T(4,128)}, f32[2,4,4]{2,1,0:T(4,128)}, f32[2,4,2048]{2,1,...) custom-call(bf16[4,512,512]{2,1,0:T(8,128)(2,1)} %get-tuple-element.45.dx_ref, ...), custom_call_target="tpu_custom_call" | custom-call | tf_op jit(solution)/shard_map/results/pallas_call | solution.py:1166
  (1 shorter events, 0.0 us)

commit v5 on v4

--- a/solution.py
+++ b/solution.py
@@ -120,9 +120,12 @@
         self.core = lax.rem(me, TWO)
         self.pos = (me // 32, lax.rem(me // EIGHT, FOUR), lax.rem(me // TWO, FOUR))
         self.partner = me + ONE - TWO * self.core
+        self.near = [[lax.rem(at + delta, FOUR) if delta else at for delta in range(FOUR)] for at in self.pos]
 
     def coord(self, dim, delta):
-        return lax.rem(self.pos[dim] + (delta + FOUR), FOUR)
+        if isinstance(delta, int):
+            return self.near[dim][delta % FOUR]
+        return lax.rem(self.pos[dim] + delta, FOUR)
 
     def device(self, offsets):
         pos = [self.coord(dim, offsets.get(dim, ZERO)) for dim in range(THREE)]
@@ -130,13 +133,9 @@
 
     def greet(self):
         barrier = pltpu.get_barrier_semaphore()
-
-        @pl.loop(ONE, 64)
-        def _(i):
-            offsets = {ZERO: i // SIXTEEN, ONE: lax.rem(i // FOUR, FOUR), TWO: lax.rem(i, FOUR)}
-
-            @pl.when(offsets[ZERO] * offsets[ONE] * offsets[TWO] == ZERO)
-            def _():
+        for i in range(ONE, 64):
+            offsets = {ZERO: i // SIXTEEN, ONE: i // FOUR % FOUR, TWO: i % FOUR}
+            if min(offsets.values()) == ZERO:
                 pl.semaphore_signal(barrier, inc=ONE, device_id=(self.device(offsets),), device_id_type=MESH)
         pl.semaphore_signal(barrier, inc=ONE, device_id=(self.partner,), device_id_type=MESH)
 
@@ -152,8 +151,15 @@
 LINE = (ONE, -ONE, TWO)
 
 
-def plane_offsets(order, k, sign=ONE):
-    return {order[ONE]: sign * (k // FOUR), order[TWO]: sign * lax.rem(k, FOUR)}
+def each_of_plane(order, run):
+    @pl.loop(ZERO, FOUR)
+    def _(high):
+        for low in range(FOUR):
+            step = functools.partial(run, FOUR * high + low, {order[ONE]: high, order[TWO]: low})
+            if low:
+                step()
+            else:
+                pl.when(high > ZERO)(step)
 
 
 class Gather:
@@ -168,9 +174,7 @@
         return remote(ref, ref, self.send.at[key], self.recv.at[key], device)
 
     def plane_start(self):
-        @pl.loop(ONE, SIXTEEN)
-        def _(k):
-            self.copy(self.block({}), ZERO, self.place.device(plane_offsets(self.order, k))).start()
+        each_of_plane(self.order, lambda k, offsets: self.copy(self.block({}), ZERO, self.place.device(offsets)).start())
 
     def plane_all(self):
         return self.copy(self.fifteen, ZERO, self.place.partner)
@@ -216,9 +220,9 @@
 
 
 class Scatter:
-    def __init__(self, place, grads, acc, got_a, got_b, got_p, other, order, send, recv):
+    def __init__(self, place, grads, acc, got_a, got_b, got_p, mine, other, order, send, recv):
         self.place, self.grads, self.acc, self.order = place, grads, acc, order
-        self.got_a, self.got_b, self.got_p, self.other, self.send, self.recv = got_a, got_b, got_p, other, send, recv
+        self.got_a, self.got_b, self.got_p, self.mine, self.other, self.send, self.recv = got_a, got_b, got_p, mine, other, send, recv
         self.units = acc.shape[ZERO]
 
     def columns(self, core):
@@ -283,8 +287,7 @@
                 value = value + ref[tuple(there)]
             acc[tuple(here)] = value
 
-    def plane_copy(self, k):
-        offsets = plane_offsets(self.order, k)
+    def plane_copy(self, k, offsets):
         index = [pl.ds(self.place.coord(dim, offsets.get(dim, ZERO)), ONE) for dim in range(THREE)]
         src = self.acc.at[:, index[ZERO], index[ONE], index[TWO]]
         return remote(src, self.got_p.at[k], self.send.at[FOUR], self.recv.at[FOUR], self.place.device(offsets))
@@ -297,40 +300,37 @@
             self.ring(ONE, way).wait_recv()
         self.add(ZERO, None, self.got_b.at[ZERO], self.got_b.at[ONE])
 
-        @pl.loop(ONE, SIXTEEN)
-        def _(k):
-            self.plane_copy(k).start()
+        each_of_plane(self.order, lambda k, offsets: self.plane_copy(k, offsets).start())
 
     def own(self):
         z, y, x = [pl.ds(p, ONE) for p in self.place.pos]
         return self.acc.at[:, z, y, x]
 
     def last_copy(self):
-        return remote(self.own(), self.other, self.send.at[5], self.recv.at[5], self.place.partner)
+        return remote(self.mine, self.other, self.send.at[5], self.recv.at[5], self.place.partner)
 
     def last(self):
         self.plane_all().wait_recv()
-        own = self.own()
-        own[...] = functools.reduce(jnp.add, [self.got_p[k] for k in range(ONE, SIXTEEN)], own[...])
+        self.mine[...] = functools.reduce(jnp.add, [self.got_p[k] for k in range(ONE, SIXTEEN)], self.own()[...])
+        for step in range(TWO):
+            for way in range(TWO):
+                self.ring(step, way).wait_send()
+        self.plane_all().wait_send()
         self.last_copy().start()
 
     def finish(self, store):
         self.last_copy().wait_recv()
         first = self.place.core == ZERO
         for u in range(self.units):
-            own, came = self.own()[u, ZERO, ZERO, ZERO], self.other[u, ZERO, ZERO, ZERO]
+            own, came = self.mine[u, ZERO, ZERO, ZERO], self.other[u, ZERO, ZERO, ZERO]
             store(u, jnp.concatenate([jnp.where(first, own, came), jnp.where(first, came, own)], axis=ONE))
-        for step in range(TWO):
-            for way in range(TWO):
-                self.ring(step, way).wait_send()
-        self.plane_all().wait_send()
         self.last_copy().wait_send()
 
 
 def landing_shapes(order, units):
     size = [FOUR, FOUR, FOUR]
     size[order[ZERO]] = ONE
-    return (units, *size, EIGHT, WIDTH), (TWO, units, *size, EIGHT, WIDTH), (SIXTEEN, units, ONE, ONE, ONE, EIGHT, WIDTH), (units, ONE, ONE, ONE, EIGHT, WIDTH)
+    return (units, *size, EIGHT, WIDTH), (TWO, units, *size, EIGHT, WIDTH), (SIXTEEN, units, ONE, ONE, ONE, EIGHT, WIDTH), (units, ONE, ONE, ONE, EIGHT, WIDTH), (units, ONE, ONE, ONE, EIGHT, WIDTH)
 
 
 class Small:
@@ -374,14 +374,12 @@
     def peers(self, stage):
         return super().peers({ZERO: ORDERS[ZERO][ZERO], ONE: THREE}[stage])
 
-    def plane(self, k):
-        return remote(self.value, self.planes.at[k], self.plane_send, self.plane_recv, self.place.device(plane_offsets(ORDERS[ZERO], k)))
+    def plane(self, k, offsets):
+        return remote(self.value, self.planes.at[k], self.plane_send, self.plane_recv, self.place.device(offsets))
 
     def steps(self):
         def first():
-            @pl.loop(ONE, SIXTEEN)
-            def _(k):
-                self.plane(k).start()
+            each_of_plane(ORDERS[ZERO], lambda k, offsets: self.plane(k, offsets).start())
 
         def second():
             remote(self.planes.at[ONE:], self.planes.at[ONE:], self.plane_send, self.plane_recv, self.place.partner).wait()
@@ -811,7 +809,7 @@
                     dx_ref, attn_out, up_out, down_out, small_out, *refs):
     (grad, dctx, delta, big, wqkv, wo, slope, act, dpre, h_ref, s_a, s_b, d_a, d_b, sums,
      g_qkv, g_wo, g_up, g_down, *small_bufs), refs = refs[:28], refs[28:]
-    qkv_bufs, mo_bufs, refs = [refs[5 * k:5 * k + 5] for k in range(THREE)], [refs[5 * k + 15:5 * k + 20] for k in range(THREE)], refs[30:]
+    qkv_bufs, mo_bufs, refs = [refs[6 * k:6 * k + 6] for k in range(THREE)], [refs[6 * k + 18:6 * k + 24] for k in range(THREE)], refs[36:]
     send, recv, late_sem, plane_sem, big_sem, w_sem, mlp_sem = refs
     step = pl.program_id(ZERO)
     phase, seq = step // FOUR, lax.rem(step, FOUR)
@@ -829,7 +827,7 @@
 
     live = step < SIXTEEN
     turn = jnp.where(live, ZERO, ONE)
-    qkv_sums = Reduce(place, ((ZERO,), (ONE,), (TWO,)), grads, [(a, ra, rb, rp.at[turn], o) for a, ra, rb, rp, o in qkv_bufs], send.at[turn], recv.at[turn])
+    qkv_sums = Reduce(place, ((ZERO,), (ONE,), (TWO,)), grads, [(a, ra, rb, rp.at[turn], *last) for a, ra, rb, rp, *last in qkv_bufs], send.at[turn], recv.at[turn])
     mo_sums = Reduce(place, COLOURS, grads, mo_bufs, send.at[TWO], recv.at[TWO])
     small_refs = small_bufs[::THREE]
     early, middle, late = [Late(place, small_refs[i], small_bufs[THREE * i + ONE], late_sem.at[i, ZERO], late_sem.at[i, ONE], small_bufs[THREE * i + TWO],
@@ -881,15 +879,17 @@
         start(mlp_weights(ONE)[ZERO] + saved_mlp(ONE, ZERO) + mlp_weights(ONE)[ONE] + attn_weights(ONE))
 
     pl.when(step == ONE)(place.met)
-    mo_steps, qkv_steps = mo_sums.steps(store(layer)), qkv_sums.steps(store(ONE - turn))
-    late_steps = mo_sums.steps(store(ONE - turn))[FOUR:]
-    attn_hook = hooks(step * FOUR, list(zip(((48,), (52,), (57,), (61,)), middle)) +
-                      [((when, when + 32), run) for when, run in zip((SIXTEEN, 20, 24, 30), mo_steps)])
-    mlp_plan = list(zip(((37, 69), (38, 70)), late_steps))
-    mlp_plan += list(zip(((32, 64), (33, 65), (38, 66), (43, 67), (47, 71), (47, 71)), qkv_steps))
-    mlp_plan += [((when,), run) for when, run in zip((64, 66, 67, 70), late)]
-    mlp_plan += [((when,), run) for when, run in zip((34, 37, 41, 45), early)]
-    mlp_hook = hooks(step * FOUR, mlp_plan)
+    mo_steps, qkv_steps = mo_sums.steps(store(ONE - turn)), qkv_sums.steps(store(ONE - turn))
+
+    def plan(slots, steps):
+        return [((slot,), run) for slot, run in zip(slots, steps)]
+
+    attn_hook = hooks(step * FOUR, plan((48, 57, 61, 63), middle) + plan((SIXTEEN, 24, 28), mo_steps) + plan((48, 53, 58), mo_steps) +
+                      plan((53, 53), qkv_steps[FOUR:]))
+    mlp_plan = plan((37, 45, 46), mo_steps[THREE:]) + plan((32, 36, 40, 47), qkv_steps) + plan((34, 41, 45, 47), early)
+    mlp_hook = hooks(step * FOUR, mlp_plan + plan((64, 66, 70, 72, 75), qkv_steps) + plan((64, 72, 74, 75), late) + plan((65, 73, 74), mo_steps[THREE:]) +
+                     plan((75,), qkv_steps[5:]))
+
 
     @pl.when(phase % TWO == ZERO)
     def _():
@@ -980,7 +980,7 @@
             dx_ref[ZERO] = grad[seq].T
         attn_hook(THREE)
 
-    @pl.when(step == 17)
+    @pl.when(step == 18)
     def _():
         small_out[:SIXTEEN, :], small_out[SIXTEEN:24, :], small_out[24:, :] = [ref[...] for ref in small_refs]
 
@@ -1123,15 +1123,15 @@
                pltpu.VMEM((FOUR, *GRID, EIGHT, DIM), F32), pltpu.VMEM((*GRID, FOUR, EIGHT, DIM), F32), *[pltpu.VMEM((*lead, rows, DIM), F32) for rows in (SIXTEEN, EIGHT, EIGHT) for lead in ((), (6,), (SIXTEEN,))]]
     for n in (ONE, THREE):
         for order in ORDERS:
-            ring_a, ring_b, plane, other = landing_shapes(order, n)
+            ring_a, ring_b, plane, *last = landing_shapes(order, n)
             plane = (TWO, *plane) if n == ONE else plane
-            scratch += [pltpu.VMEM(s, F32) for s in ((n, *GRID, EIGHT, WIDTH), ring_a, ring_b, plane, other)]
+            scratch += [pltpu.VMEM(s, F32) for s in ((n, *GRID, EIGHT, WIDTH), ring_a, ring_b, plane, *last)]
     scratch += [DMA((THREE, THREE, 9)), DMA((THREE, THREE, 9)), DMA((THREE, TWO, 6)), DMA((THREE, TWO)), DMA((EIGHT,)), DMA((TWO,)), DMA((TWO,))]
     outs = ((TWO, FOUR, FOUR, DIM), (TWO, FOUR, FFN), (TWO, SIXTEEN, DIM), (32, DIM))
     whole = [pl.BlockSpec(s, lambda i, n=len(s): (ZERO,) * n, pipeline_mode=pl.Buffered(ONE)) for s in outs]
     dx_at = lambda s: (jnp.clip(s - 12, ZERO, THREE), ZERO, ZERO)
     return pl.pallas_call(
-        backward_kernel, grid=(18,),
+        backward_kernel, grid=(19,),
         out_shape=[jax.ShapeDtypeStruct((SEQS, TOK, DIM), BF16)] + [jax.ShapeDtypeStruct(s, F32) for s in outs],
         out_specs=[pl.BlockSpec((ONE, TOK, DIM), dx_at)] + whole,
         in_specs=[pl.BlockSpec((ONE, TOK, DIM), lambda s: (jnp.minimum(s, THREE), ZERO, ZERO)), per_mlp, per_mlp, stat(mlp_at)] + [per_attn] * FOUR + [stat(attn_at),
@@ -1162,9 +1162,9 @@
 
 def results(dx, attn, up, down, small):
     shapes = [attn.shape, (TWO, FOUR, FOUR), (TWO, FOUR, FOUR), up.shape, (TWO, SIXTEEN), down.shape, (TWO, FOUR)]
-    per = pl.BlockSpec((ONE, TOK, DIM), lambda s: (s, ZERO, ZERO))
+    per = pl.BlockSpec((TWO, TOK, DIM), lambda s: (s, ZERO, ZERO))
     return pl.pallas_call(
-        results_kernel, grid=(SEQS,), name="results",
+        results_kernel, grid=(SEQS // TWO,), name="results",
         out_shape=[jax.ShapeDtypeStruct(dx.shape, BF16)] + [jax.ShapeDtypeStruct(s, F32) for s in shapes],
         in_specs=[per] + [once(a.shape) for a in (attn, up, down, small)],
         out_specs=[per] + [once(s) for s in shapes])(dx, attn, up, down, small)

time: 298 us -> 291 us (0.977)
  Pallas kernels: 296 us -> 289 us
    pallas_call x2, Pallas kernels: 173 us -> 169 us  [the longest x1 166 us: backward(): pl.pallas_call(backward_kernel, grid=(19,), out_shape=[jax.ShapeDtypeStru...]
where the time goes in v5:
time: 291 us
  Pallas kernels  289 us (99%)
    pallas_call x1, Pallas kernels, backward(): pl.pallas_call(backward_kernel, grid=(19,), out_shape=[jax.ShapeDtypeStru...  166 us
    pallas_call x1, Pallas kernels, forward(): pl.pallas_call(forward_kernel, grid=(SIXTEEN,), out_shape=[o[ZERO] for o...  121 us

profile of v5, /device:TPU:1, one launch (start us, length us, event | category | flops | bytes accessed | tf_op | source)
XLA Modules:
  0.0 291.0 jit_solution(16531175873807975167)
XLA Ops:
  0.6 1.0 fusion
  1.6 120.6 %forward.1 = (bf16[2,4,512,512]{3,2,1,0:T(8,128)(2,1)}, bf16[2,4,512,512]{3,2,1,0:T(8,128)(2,1)}, bf16[2,4,512,512]{3,2,1,0:T(8,128)(2,1)}, bf16[2,4,512,512]{3,...) custom-call(s32[4]{0:T(128)} %len_ref.1, ...), custom_call_target="tpu_custom_call" | custom-call | tf_op jit(solution)/shard_map/forward/pallas_call | solution.py:744
  122.2 165.9 %backward.1 = (bf16[4,512,512]{2,1,0:T(8,128)(2,1)}, f32[2,4,4,512]{3,2,1,0:T(4,128)}, f32[2,4,2048]{2,1,0:T(4,128)}, f32[2,16,512]{2,1,0:T(8,128)}, f32[32,512]{1,0:T(8,128)}) custom-call(bf16[4,512,512]{2,1,0:T(8,128)(2,1)} %dy_ref.1, bf16[2,4,512,512]{3,2,1,0:T(8,128)(2,1)} %get-tuple-element.29.mid_ref, f32[2,4,512,512]{3,2,1,0:T(8,128)} %get-tuple-element.30.ctx_ref, ...), custom_call_target="tpu_custom_call" | custom-call | tf_op jit(solution)/shard_map/backward/pallas_call | solution.py:1133
  288.1 2.8 results.1
  (1 shorter events, 0.0 us)

commit v6 on v5

--- a/solution.py
+++ b/solution.py
@@ -473,10 +473,10 @@
 
 
 def forward_kernel(len_ref, x_hbm, cos_ref, sin_ref, w_attn, b_attn, ln_par, w_up, b_up, w_down, b_down,
-                   xs_out, q_ref, k_ref, v_ref, p_hbm, ctx_ref, mid_ref, act_ref, slope_ref, st1_ref, st2_ref, c_ref,
+                   xs_out, q_ref, k_ref, v_ref, p_ref, ctx_ref, mid_ref, act_ref, slope_ref, st1_ref, st2_ref, c_ref,
                    nat_qkv, nat_wo, nat_up, nat_down,
-                   xs, ctxb, wqkv, wo, up, down, n_qkv, n_wo, n_up, n_down, p_buf, h_ref, s_a, s_b, s_c,
-                   sbuf, q0, q1, q2, m0, m1, m2, stats, f0, f1, f2, send, recv, p_sem, nat_sem, x_sem):
+                   xs, ctxb, n_qkv, n_wo, n_up, n_down, h_ref, s_a, s_b, s_c,
+                   sbuf, q0, q1, q2, m0, m1, m2, stats, f0, f1, f2, send, recv, nat_sem, x_sem):
     step = pl.program_id(ZERO)
     phase, seq, layer = step // FOUR, lax.rem(step, FOUR), step // EIGHT
     place = Place()
@@ -505,7 +505,6 @@
         pl.when(step > ZERO)(lambda: wait(nat_copies(ZERO, layer)))
         for m in range(THREE):
             spread(qkv_bufs[m].at[layer], ZERO, n_qkv.at[m], ZERO)
-            wqkv[m] = n_qkv[m].T
         start(nat_copies(ZERO, layer))
 
     def take_mo():
@@ -515,16 +514,10 @@
                 buf = mo_bufs[colour].at[layer]
                 if unit == THREE:
                     spread(buf, u, n_wo, ZERO)
-                    wo[...] = n_wo[...].T
                 elif unit < EIGHT:
-                    part = slice(DIM * (unit - FOUR), DIM * (unit - THREE))
-                    spread(buf, u, n_up, part.start)
-                    up[part, :] = n_up[:, part].T
+                    spread(buf, u, n_up, DIM * (unit - FOUR))
                 else:
                     spread_down(buf, u, n_down, lane_tiles()[unit - EIGHT])
-        for k in range(FOUR):
-            part = slice(DIM * k, DIM * k + DIM)
-            down[:, part] = n_down[part, :].T
         start(nat_copies(ONE, layer))
 
     x_copies = [pltpu.make_async_copy(x_hbm.at[s], ctxb.at[s], x_sem.at[s]) for s in range(SEQS)]
@@ -583,18 +576,15 @@
             put_stats(stats.at[seq], norm_stats(xs.at[seq]))
 
         attn_hook(ZERO)
-        copies = [pltpu.make_async_copy(p_buf.at[head], p_hbm.at[layer, seq, head], p_sem.at[head]) for head in range(HEADS)]
-        attn_forward(len_ref[seq], xs.at[seq], wqkv, c_ref.at[layer], cos_ref, sin_ref, q_ref.at[ZERO, ZERO], k_ref.at[ZERO, ZERO],
-                     v_ref.at[ZERO, ZERO], p_buf, ctx_ref.at[ZERO, ZERO], ctxb.at[seq], get_stats(stats.at[seq]), st1_ref.at[ZERO, ZERO], h_ref, s_a, s_b, s_c, attn_hook,
-                     lambda heads: pl.when(step > ZERO)(lambda: wait(copies[heads])), lambda heads: start(copies[heads]))
-        pl.when(step == 11)(lambda: wait(copies))
+        attn_forward(len_ref[seq], xs.at[seq], n_qkv, c_ref.at[layer], cos_ref, sin_ref, q_ref.at[ZERO, ZERO], k_ref.at[ZERO, ZERO],
+                     v_ref.at[ZERO, ZERO], p_ref.at[ZERO, ZERO], ctx_ref.at[ZERO, ZERO], ctxb.at[seq], get_stats(stats.at[seq]), st1_ref.at[ZERO, ZERO], h_ref, s_a, s_b, s_c, attn_hook)
         attn_hook(THREE)
 
     @pl.when(phase % TWO == ONE)
     def _():
         pl.when(seq == ZERO)(take_mo)
         mlp_hook(ZERO)
-        mlp_forward(layer, ctxb.at[seq], xs.at[seq], wo, up, down, c_ref.at[layer], mid_ref.at[ZERO, ZERO], act_ref.at[ZERO, ZERO], slope_ref.at[ZERO, ZERO],
+        mlp_forward(layer, ctxb.at[seq], xs.at[seq], n_wo, n_up, n_down, c_ref.at[layer], mid_ref.at[ZERO, ZERO], act_ref.at[ZERO, ZERO], slope_ref.at[ZERO, ZERO],
                     st2_ref.at[ZERO, ZERO], h_ref, s_a, s_b, mlp_hook)
 
         @pl.when(layer == ZERO)
@@ -608,11 +598,11 @@
             wait(nat_copies(which, ONE))
 
 
-def attn_forward(length, xt, w, c_ref, cos_ref, sin_ref, q_ref, k_ref, v_ref, p_buf, ctx_ref, ctxb, stats, stat_ref, h_ref, s_a, s_b, s_c, hook, free, ship):
+def attn_forward(length, xt, w, c_ref, cos_ref, sin_ref, q_ref, k_ref, v_ref, p_buf, ctx_ref, ctxb, stats, stat_ref, h_ref, s_a, s_b, s_c, hook):
     put_stats(stat_ref, stats)
     norm_to(xt, stats, c_ref, LN_PAR, h_ref)
     for m, acc in enumerate((s_a, s_b, s_c)):
-        acc[...] = nn(w[m], h_ref[...])
+        acc[...] = tn(w[m], h_ref[...])
     cos, sin = cos_ref[...], sin_ref[...]
     for m, (acc, out) in enumerate(((s_a, q_ref), (s_b, k_ref), (s_c, v_ref))):
         for head in range(HEADS):
@@ -626,8 +616,6 @@
             out[one, :] = (a * cos - b * sin).astype(BF16)
             out[two, :] = (b * cos + a * sin).astype(BF16)
     hook(ONE)
-    halves = slice(ZERO, FOUR), slice(FOUR, EIGHT)
-    free(halves[ZERO])
     key = lax.broadcasted_iota(jnp.int32, (SIXTEEN, TOK), ONE)
     row = lax.broadcasted_iota(jnp.int32, (SIXTEEN, TOK), ZERO)
     bias_rows = jnp.where((row == ZERO) & (key >= length), NEG_BIG, 0.0).astype(BF16)
@@ -673,15 +661,12 @@
             products.append(functools.partial(close_head, head - ONE))
         woven(products, weigh(head))
         if head == THREE:
-            ship(halves[ZERO])
             hook(TWO)
-            free(halves[ONE])
     close_head(HEADS - ONE)
-    ship(halves[ONE])
 
 
 def mlp_forward(layer, ctxb, xt, wo, up, down, c_ref, mid_ref, act_ref, slope_ref, stat_ref, h_ref, s_a, s_b, hook):
-    s_a[...] = nn(wo[...], ctxb[...])
+    s_a[...] = tn(wo[...], ctxb[...])
     for rows in row_chunks():
         mid_ref[rows, :] = (xt[rows, :].astype(F32) + s_a[rows, :] + column(c_ref, rows, B_ATTN + THREE)).astype(BF16)
     stats = norm_stats(mid_ref)
@@ -692,7 +677,7 @@
     parts = [slice(DIM * k, DIM * k + DIM) for k in range(FOUR)]
 
     def open_part(k):
-        pre[k % TWO][...] = nn(up[parts[k], :], h_ref[...])
+        pre[k % TWO][...] = tn(up[:, parts[k]], h_ref[...])
 
     open_part(ZERO)
     for k, part in enumerate(parts):
@@ -711,7 +696,7 @@
 
     @pl.when(layer == ZERO)
     def _():
-        s_a[...] = nn(down[...], act_ref[...])
+        s_a[...] = tn(down[...], act_ref[...])
         for rows in row_chunks():
             xt[rows, :] = (mid_ref[rows, :].astype(F32) + s_a[rows, :] + column(c_ref, rows, B_DOWN)).astype(BF16)
 
@@ -731,16 +716,16 @@
         return jnp.where(s < FOUR, ZERO, ONE), jnp.where(s < EIGHT, s % FOUR, THREE), ZERO, ZERO
 
     outs = [saved(xs_at, DIM, BF16)] + [saved(attn_at, DIM, BF16)] * THREE
-    outs += [(jax.ShapeDtypeStruct((TWO, SEQS, HEADS, TOK, TOK), BF16), HBM), saved(attn_at, DIM, F32)]
+    outs += [(jax.ShapeDtypeStruct((TWO, SEQS, HEADS, TOK, TOK), BF16), pl.BlockSpec((ONE, ONE, HEADS, TOK, TOK), lambda s: (*attn_at(s), ZERO))), saved(attn_at, DIM, F32)]
     outs += [saved(mlp_at, DIM, BF16), saved(mlp_at, FFN, BF16), saved(mlp_at, FFN, F32), saved(attn_at, EIGHT, F32), saved(mlp_at, EIGHT, F32)]
     outs += [(jax.ShapeDtypeStruct((TWO, *COLS), F32), once((TWO, *COLS)))]
     weights = ((THREE, DIM, DIM), (DIM, DIM), (DIM, FFN), (FFN, DIM))
     outs += [(jax.ShapeDtypeStruct((TWO, *w), BF16), HBM) for w in weights]
-    scratch = [(SEQS, *SQUARE), (SEQS, *SQUARE), weights[ZERO], weights[ONE], weights[THREE], weights[TWO], *weights, (HEADS, TOK, TOK), SQUARE]
+    scratch = [(SEQS, *SQUARE), (SEQS, *SQUARE), *weights, SQUARE]
     scratch = [pltpu.VMEM(s, BF16) for s in scratch] + [pltpu.VMEM(SQUARE, F32)] * THREE + [pltpu.VMEM((*GRID, TWO, ONE, ONE, LANES), F32)]
     scratch += [pltpu.VMEM((TWO, *GRID, TWO, n, SIXTEEN, LANES), BF16) for n in (ONE, THREE) for _ in range(THREE)]
     scratch += [pltpu.VMEM((SEQS, EIGHT, TOK), F32)] + [pltpu.VMEM((15, n, SIXTEEN, LANES), BF16) for n in (ONE, THREE)]
-    scratch += [pltpu.VMEM((15, ONE, ONE, LANES), F32), DMA((7, TWO, 5)), DMA((7, TWO, 5)), DMA((HEADS,)), DMA((FOUR,)), DMA((SEQS,))]
+    scratch += [pltpu.VMEM((15, ONE, ONE, LANES), F32), DMA((7, TWO, 5)), DMA((7, TWO, 5)), DMA((FOUR,)), DMA((SEQS,))]
     return pl.pallas_call(
         forward_kernel, grid=(SIXTEEN,),
         out_shape=[o[ZERO] for o in outs], out_specs=[o[ONE] for o in outs],
@@ -829,6 +814,12 @@
     turn = jnp.where(live, ZERO, ONE)
     qkv_sums = Reduce(place, ((ZERO,), (ONE,), (TWO,)), grads, [(a, ra, rb, rp.at[turn], *last) for a, ra, rb, rp, *last in qkv_bufs], send.at[turn], recv.at[turn])
     mo_sums = Reduce(place, COLOURS, grads, mo_bufs, send.at[TWO], recv.at[TWO])
+
+    def third(i):
+        one = pl.ds(i, ONE)
+        bufs = [(a.at[one], ra.at[one], rb.at[:, one], rp.at[:, one], mine.at[one], other.at[one]) for a, ra, rb, rp, mine, other in mo_bufs]
+        return Reduce(place, [units[i:i + ONE] for units in COLOURS], grads, bufs, send.at[THREE + i], recv.at[THREE + i]).steps(store(ONE - turn))
+
     small_refs = small_bufs[::THREE]
     early, middle, late = [Late(place, small_refs[i], small_bufs[THREE * i + ONE], late_sem.at[i, ZERO], late_sem.at[i, ONE], small_bufs[THREE * i + TWO],
                                 plane_sem.at[i, ZERO], plane_sem.at[i, ONE]).steps() for i in range(THREE)]
@@ -884,10 +875,15 @@
     def plan(slots, steps):
         return [((slot,), run) for slot, run in zip(slots, steps)]
 
-    attn_hook = hooks(step * FOUR, plan((48, 57, 61, 63), middle) + plan((SIXTEEN, 24, 28), mo_steps) + plan((48, 53, 58), mo_steps) +
+    thirds = [], []
+    for i, slots in enumerate(((48, 50, 54, 59, 73, 74), (48, 51, 55, 62, 73, 74), (48, 53, 57, 63, 73, 74))):
+        steps = plan(slots, third(i))
+        thirds[ZERO].extend(steps[:FOUR])
+        thirds[ONE].extend(steps[FOUR:])
+    attn_hook = hooks(step * FOUR, plan((48, 57, 61, 63), middle) + plan((SIXTEEN, 24, 28), mo_steps) + thirds[ZERO] +
                       plan((53, 53), qkv_steps[FOUR:]))
     mlp_plan = plan((37, 45, 46), mo_steps[THREE:]) + plan((32, 36, 40, 47), qkv_steps) + plan((34, 41, 45, 47), early)
-    mlp_hook = hooks(step * FOUR, mlp_plan + plan((64, 66, 70, 72, 75), qkv_steps) + plan((64, 72, 74, 75), late) + plan((65, 73, 74), mo_steps[THREE:]) +
+    mlp_hook = hooks(step * FOUR, mlp_plan + plan((64, 66, 70, 72, 75), qkv_steps) + plan((64, 72, 74, 75), late) + thirds[ONE] +
                      plan((75,), qkv_steps[5:]))
 
 
@@ -1126,7 +1122,7 @@
             ring_a, ring_b, plane, *last = landing_shapes(order, n)
             plane = (TWO, *plane) if n == ONE else plane
             scratch += [pltpu.VMEM(s, F32) for s in ((n, *GRID, EIGHT, WIDTH), ring_a, ring_b, plane, *last)]
-    scratch += [DMA((THREE, THREE, 9)), DMA((THREE, THREE, 9)), DMA((THREE, TWO, 6)), DMA((THREE, TWO)), DMA((EIGHT,)), DMA((TWO,)), DMA((TWO,))]
+    scratch += [DMA((6, THREE, 9)), DMA((6, THREE, 9)), DMA((THREE, TWO, 6)), DMA((THREE, TWO)), DMA((EIGHT,)), DMA((TWO,)), DMA((TWO,))]
     outs = ((TWO, FOUR, FOUR, DIM), (TWO, FOUR, FFN), (TWO, SIXTEEN, DIM), (32, DIM))
     whole = [pl.BlockSpec(s, lambda i, n=len(s): (ZERO,) * n, pipeline_mode=pl.Buffered(ONE)) for s in outs]
     dx_at = lambda s: (jnp.clip(s - 12, ZERO, THREE), ZERO, ZERO)

time: 291 us -> 285 us (0.979)
  Pallas kernels: 289 us -> 283 us
    pallas_call x1, Pallas kernels: 121 us -> 116 us  [forward(): pl.pallas_call(forward_kernel, grid=(SIXTEEN,), out_shape=[o[ZERO] for o...]
where the time goes in v6:
time: 285 us; the launch traced here: 284 us
  Pallas kernels  283 us (99%)
    pallas_call x1, Pallas kernels, backward(): pl.pallas_call(backward_kernel, grid=(19,), out_shape=[jax.ShapeDtypeStru...  164 us
    pallas_call x1, Pallas kernels, forward(): pl.pallas_call(forward_kernel, grid=(SIXTEEN,), out_shape=[o[ZERO] for o...  116 us

profile of v6, /device:TPU:1, one launch (start us, length us, event | category | flops | bytes accessed | tf_op | source)
XLA Modules:
  0.0 284.4 jit_solution(8359316065789725366)
XLA Ops:
  0.6 1.0 fusion
  1.6 116.3 %forward.1 = (bf16[2,4,512,512]{3,2,1,0:T(8,128)(2,1)}, bf16[2,4,512,512]{3,2,1,0:T(8,128)(2,1)}, bf16[2,4,512,512]{3,2,1,0:T(8,128)(2,1)}, bf16[2,4,512,512]{3,...) custom-call(s32[4]{0:T(128)} %len_ref.1, ...), custom_call_target="tpu_custom_call" | custom-call | tf_op jit(solution)/shard_map/forward/pallas_call | solution.py:729
  117.9 163.6 %backward.1 = (bf16[4,512,512]{2,1,0:T(8,128)(2,1)}, f32[2,4,4,512]{3,2,1,0:T(4,128)}, f32[2,4,2048]{2,1,0:T(4,128)}, f32[2,16,512]{2,1,0:T(8,128)}, f32[32,512]{1,0:T(8,128)}) custom-call(bf16[4,512,512]{2,1,0:T(8,128)(2,1)} %dy_ref.1, bf16[2,4,512,512]{3,2,1,0:T(8,128)(2,1)} %get-tuple-element.29.mid_ref, f32[2,4,512,512]{3,2,1,0:T(8,128)} %get-tuple-element.30.ctx_ref, ...), custom_call_target="tpu_custom_call" | custom-call | tf_op jit(solution)/shard_map/backward/pallas_call | solution.py:1129
  281.5 2.8 results.1
  (1 shorter events, 0.0 us)

commit v7 on v6

--- a/solution.py
+++ b/solution.py
@@ -399,11 +399,11 @@
 
 
 def spread(buf, u, out_ref, column_base):
-    @pl.loop(ZERO, EIGHT)
-    def _(block):
-        for part in range(FOUR):
-            g = block * FOUR + part
-            tiles = [buf[block // TWO, lax.rem(block, TWO) * TWO + part // TWO, part % TWO * TWO + k // TWO, k % TWO, u].astype(F32) for k in range(FOUR)]
+    @pl.loop(ZERO, FOUR)
+    def _(z):
+        for part in range(EIGHT):
+            g = z * EIGHT + part
+            tiles = [buf[z, part // TWO, part % TWO * TWO + k // TWO, k % TWO, u].astype(F32) for k in range(FOUR)]
             rows = pl.ds(pl.multiple_of(g * SIXTEEN, SIXTEEN), SIXTEEN)
             for j, cols in enumerate(lane_tiles()):
                 value = jnp.concatenate([t[FOUR * j:FOUR * j + FOUR] for t in tiles], axis=ZERO).astype(BF16)
@@ -539,7 +539,8 @@
                 else:
                     mo_bufs[(unit - THREE) // THREE][l, z, y, x, place.core, (unit - THREE) % THREE] = tile
         sbuf[z, y, x, place.core, ZERO] = small_row(b_attn, ln_par, b_up, b_down)
-        first, second = gather_steps(group(qkv_bufs, ZERO, ZERO) + [little]), gather_steps(group(mo_bufs, THREE, ZERO))
+        parts = group(qkv_bufs, ZERO, ZERO)
+        first, second = gather_steps([little] + parts), gather_steps(group(mo_bufs, THREE, ZERO))
 
         def ready(s):
             x_copies[s].wait()
@@ -556,8 +557,10 @@
         ready(THREE)
         first[TWO]()
         second[ONE]()
-        first[THREE]()
+        little.end()
         small_columns(sbuf, c_ref)
+        for part in parts:
+            part.end()
 
     attn_hook = hooks(step * FOUR, [((when, when + 32), run) for when, run in zip((9, 13), gather_steps(group(mo_bufs, THREE, layer))[TWO:])])
     mlp_steps = gather_steps(group(qkv_bufs, ZERO, ONE)) + gather_steps(group(mo_bufs, THREE, ONE))[:TWO]
@@ -883,7 +886,7 @@
     attn_hook = hooks(step * FOUR, plan((48, 57, 61, 63), middle) + plan((SIXTEEN, 24, 28), mo_steps) + thirds[ZERO] +
                       plan((53, 53), qkv_steps[FOUR:]))
     mlp_plan = plan((37, 45, 46), mo_steps[THREE:]) + plan((32, 36, 40, 47), qkv_steps) + plan((34, 41, 45, 47), early)
-    mlp_hook = hooks(step * FOUR, mlp_plan + plan((64, 66, 70, 72, 75), qkv_steps) + plan((64, 72, 74, 75), late) + thirds[ONE] +
+    mlp_hook = hooks(step * FOUR, mlp_plan + plan((64, 66, 70, 72, 75), qkv_steps) + plan((65, 72, 74, 75), late) + thirds[ONE] +
                      plan((75,), qkv_steps[5:]))
 
 
@@ -903,6 +906,10 @@
             wait(mlp_weights(layer)[ZERO])
 
         mlp_hook(ZERO)
+
+        @pl.when(step == SIXTEEN)
+        def _():
+            small_refs[TWO][...] = columns_of([sums[i] for i in range(5)])
 
         def after_first():
             pl.when(seq < THREE)(lambda: start(saved_mlp(layer, seq + ONE)))
@@ -955,17 +962,9 @@
                       g_qkv, dpre, h_ref, s_a, s_b, d_a, d_b, sums, attn_hook,
                       after_heads)
 
-        @pl.when(seq == THREE)
-        def _():
-            value = columns_of([sums[i] for i in range(5)])
-
-            @pl.when(layer == ONE)
-            def _():
-                small_refs[ZERO][EIGHT:, :] = value
-
-            @pl.when(layer == ZERO)
-            def _():
-                small_refs[TWO][...] = value
+        @pl.when(step == 7)
+        def _():
+            small_refs[ZERO][EIGHT:, :] = columns_of([sums[i] for i in range(5)])
 
         @pl.when(step == 7)
         def _():

time: 285 us -> 282 us (0.989)
  Pallas kernels: 283 us -> 280 us
where the time goes in v7:
time: 282 us; the launch traced here: 281 us
  Pallas kernels  280 us (99%)
    pallas_call x1, Pallas kernels, backward(): pl.pallas_call(backward_kernel, grid=(19,), out_shape=[jax.ShapeDtypeStru...  163 us
    pallas_call x1, Pallas kernels, forward(): pl.pallas_call(forward_kernel, grid=(SIXTEEN,), out_shape=[o[ZERO] for o...  114 us

profile of v7, /device:TPU:1, one launch (start us, length us, event | category | flops | bytes accessed | tf_op | source)
XLA Modules:
  0.0 281.4 jit_solution(16516829502465008812)
XLA Ops:
  0.6 1.0 fusion
  1.6 113.9 %forward.1 = (bf16[2,4,512,512]{3,2,1,0:T(8,128)(2,1)}, bf16[2,4,512,512]{3,2,1,0:T(8,128)(2,1)}, bf16[2,4,512,512]{3,2,1,0:T(8,128)(2,1)}, bf16[2,4,512,512]{3,...) custom-call(s32[4]{0:T(128)} %len_ref.1, ...), custom_call_target="tpu_custom_call" | custom-call | tf_op jit(solution)/shard_map/forward/pallas_call | solution.py:732
  115.5 163.0 %backward.1 = (bf16[4,512,512]{2,1,0:T(8,128)(2,1)}, f32[2,4,4,512]{3,2,1,0:T(4,128)}, f32[2,4,2048]{2,1,0:T(4,128)}, f32[2,16,512]{2,1,0:T(8,128)}, f32[32,512]{1,0:T(8,128)}) custom-call(bf16[4,512,512]{2,1,0:T(8,128)(2,1)} %dy_ref.1, bf16[2,4,512,512]{3,2,1,0:T(8,128)(2,1)} %get-tuple-element.29.mid_ref, f32[2,4,512,512]{3,2,1,0:T(8,128)} %get-tuple-element.30.ctx_ref, ...), custom_call_target="tpu_custom_call" | custom-call | tf_op jit(solution)/shard_map/backward/pallas_call | solution.py:1128
  278.5 2.8 results.1
  (1 shorter events, 0.0 us)

commit v8 on v7

--- a/solution.py
+++ b/solution.py
@@ -1,6 +1,7 @@
 import math
 import functools
 import jax
+import numpy as np
 import jax.numpy as jnp
 from jax import lax
 from jax.experimental import pallas as pl
@@ -35,7 +36,7 @@
     return [slice(i, i + size) for i in range(ZERO, width, size)]
 
 
-def row_chunks(rows=DIM, size=64):
+def row_chunks(rows=DIM, size=128):
     return [slice(i, i + size) for i in range(ZERO, rows, size)]
 
 
@@ -104,9 +105,9 @@
 
 
 def rotary_tables():
-    inv_freq = 1.0 / (THETA ** (jnp.arange(HALF, dtype=F32) * (2.0 / HEAD)))
-    angles = inv_freq[:, None] * jnp.arange(TOK, dtype=F32)[None, :]
-    return jnp.cos(angles), jnp.sin(angles)
+    inv_freq = np.float32(1.0) / np.float32(THETA) ** (np.arange(HALF, dtype=np.float32) * np.float32(2.0 / HEAD))
+    angles = inv_freq[:, None] * np.arange(TOK, dtype=np.float32)[None, :]
+    return np.cos(angles).astype(np.float32), np.sin(angles).astype(np.float32)
 
 
 MESH = pl.DeviceIdType.MESH
@@ -399,11 +400,11 @@
 
 
 def spread(buf, u, out_ref, column_base):
-    @pl.loop(ZERO, FOUR)
-    def _(z):
-        for part in range(EIGHT):
-            g = z * EIGHT + part
-            tiles = [buf[z, part // TWO, part % TWO * TWO + k // TWO, k % TWO, u].astype(F32) for k in range(FOUR)]
+    @pl.loop(ZERO, TWO)
+    def _(half):
+        for part in range(SIXTEEN):
+            g = half * SIXTEEN + part
+            tiles = [buf[half * TWO + part // EIGHT, part // TWO % FOUR, part % TWO * TWO + k // TWO, k % TWO, u].astype(F32) for k in range(FOUR)]
             rows = pl.ds(pl.multiple_of(g * SIXTEEN, SIXTEEN), SIXTEEN)
             for j, cols in enumerate(lane_tiles()):
                 value = jnp.concatenate([t[FOUR * j:FOUR * j + FOUR] for t in tiles], axis=ZERO).astype(BF16)

time: 282 us -> 279 us (0.989)
  no operation moved by 1% of the time
where the time goes in v8:
time: 279 us; the launch traced here: 278 us
  Pallas kernels  278 us (100%)
    pallas_call x1, Pallas kernels, backward(): pl.pallas_call(backward_kernel, grid=(19,), out_shape=[jax.ShapeDtypeStru...  162 us
    pallas_call x1, Pallas kernels, forward(): pl.pallas_call(forward_kernel, grid=(SIXTEEN,), out_shape=[o[ZERO] for o...  113 us

profile of v8, /device:TPU:1, one launch (start us, length us, event | category | flops | bytes accessed | tf_op | source)
XLA Modules:
  0.0 278.5 jit_solution(6992623573851350726)
XLA Ops:
  0.6 113.1 %forward.1 = (bf16[2,4,512,512]{3,2,1,0:T(8,128)(2,1)}, bf16[2,4,512,512]{3,2,1,0:T(8,128)(2,1)}, bf16[2,4,512,512]{3,2,1,0:T(8,128)(2,1)}, bf16[2,4,512,512]{3,...) custom-call(s32[4]{0:T(128)} %len_ref.1, ...), custom_call_target="tpu_custom_call" | custom-call | tf_op jit(solution)/shard_map/forward/pallas_call | solution.py:733
  113.8 161.7 %backward.1 = (bf16[4,512,512]{2,1,0:T(8,128)(2,1)}, f32[2,4,4,512]{3,2,1,0:T(4,128)}, f32[2,4,2048]{2,1,0:T(4,128)}, f32[2,16,512]{2,1,0:T(8,128)}, f32[32,512]{1,0:T(8,128)}) custom-call(bf16[4,512,512]{2,1,0:T(8,128)(2,1)} %dy_ref.1, bf16[2,4,512,512]{3,2,1,0:T(8,128)(2,1)} %get-tuple-element.29.mid_ref, f32[2,4,512,512]{3,2,1,0:T(8,128)} %get-tuple-element.30.ctx_ref, ...), custom_call_target="tpu_custom_call" | custom-call | tf_op jit(solution)/shard_map/backward/pallas_call | solution.py:1129
  275.5 2.8 %results.1 = (bf16[4,512,512]{2,1,0:T(8,128)(2,1)}, f32[2,4,4,512]{3,2,1,0:T(4,128)}, f32[2,4,4]{2,1,0:T(4,128)}, f32[2,4,4]{2,1,0:T(4,128)}, f32[2,4,2048]{2,1,...) custom-call(bf16[4,512,512]{2,1,0:T(8,128)(2,1)} %get-tuple-element.45.dx_ref, ...), custom_call_target="tpu_custom_call" | custom-call | tf_op jit(solution)/shard_map/results/pallas_call | solution.py:1162
